TPU v7x, 32 devices: a whole 2x2x4 slice. The times are simulated.
32 devices in a mesh: dp: 8 (over z, x), seq: 4 (over y, core).
Axes of the slice: x: 2, y: 2, z: 4, core: 2. Of those that a mesh axis runs over, the one named last changes fastest.
Arguments:
- tokens: bfloat16 [16, 1024, 1024], P('dp', 'seq'), may hold values from -6 to 6
- cotangent: bfloat16 [16, 1024, 1024], P('dp', 'seq'), may hold values from -6 to 6
- doc_ids: int32 [16, 1024], P('dp', 'seq'), may hold values from 0 to 7, never falling along the last dimension, each value on 1 to 512 neighbouring positions
- master_blocks: float32 [768, 128, 128], P('dp'), may hold values from -1.5 to 1.5
- block_of_slot: int32 [768], replicated, may hold values from 0 to 767, as said below
- left_stats: float32 [768, 128, 128], P('dp'), may hold values from -0.3 to 4, as said below
- right_stats: float32 [768, 128, 128], P('dp'), may hold values from -0.3 to 4, as said below
- left_roots: float32 [768, 128, 128], P('dp'), may hold values from -0.25 to 4, as said below
- right_roots: float32 [768, 128, 128], P('dp'), may hold values from -0.25 to 4, as said below
- vector_params: float32 [37192], replicated, may hold values from -7.7 to 2.1
- first_moment: float32 [37192], replicated, may hold values from -0.6 to 0.6
- second_moment: float32 [37192], replicated, may hold values from 0.0005 to 0.002
- adam_step: int32 [1], replicated, may hold values from 1 to 4
Outputs:
- layer_out: bfloat16 [16, 1024, 1024], P('dp', 'seq')
- grad_tokens: float32 [16, 1024, 1024], P('dp', 'seq')
- grad_blocks: float32 [768, 128, 128], P('dp')
- new_left: float32 [768, 128, 128], P('dp')
- new_right: float32 [768, 128, 128], P('dp')
- new_master: float32 [768, 128, 128], P('dp')
- master_copy: bfloat16 [768, 128, 128], P('dp')
- grad_vectors: float32 [37192], replicated
- new_vectors: float32 [37192], replicated
- new_first: float32 [37192], replicated
- new_second: float32 [37192], replicated
Inputs may be any that keep to these rules, and one draw needn't show every extreme that they name: `doc_ids`: within each sequence the ids never fall; every document holds 1 to 512 tokens, and one document of each sequence holds exactly 512. `block_of_slot`: each of the 768 blocks stands in exactly one slot. `left_stats`: each block is symmetric. `right_stats`: each block is symmetric. `left_roots`: each block is symmetric. `right_roots`: each block is symmetric.
All inputs are finite; a program needn't handle non-finite values.
Results may differ from a plain program's by a relative error of at most 0.019.
Values may be sent and summed in bfloat16 or wider, within the bound.
A program may use at most 384 MiB of HBM per device.

v0:
```python
import functools
import math

import jax
import jax.numpy as jnp
from jax import lax
from jax.experimental import pallas as pl
from jax.experimental.pallas import tpu as pltpu
from jax.sharding import PartitionSpec as P

D = 1024
HEADS_SSM = 24
HEAD = 64
NSTATE = 128
HEADS = 8
KV_HEADS = 2
FF = 2048
KERNEL = 4
BS = 128
DOC_MOST = 512
INNER = HEADS_SSM * HEAD
CHANNELS = INNER + 2 * NSTATE
REACH = KERNEL - 1
QDIM = HEADS * HEAD
KDIM = KV_HEADS * HEAD
LANES = 128
PAIRS = INNER // LANES

EPS = 1e-05
THETA = 100000000000.0
LR_MATRIX = 0.02
LR_VECTOR = 0.08
BETA_ONE = 0.9
BETA_TWO = 0.999
ADAM_EPS = 1e-08
NEG_BIG = -1e30
F32 = jnp.float32
BF16 = jnp.bfloat16
HIGHEST = lax.Precision.HIGHEST
VMEM_MOST = 60 << 20

SHAPES = (
    (D, INNER), (D, INNER), (D, 2 * NSTATE), (D, QDIM), (D, KDIM), (D, KDIM),
    (INNER, D), (QDIM, D), (D, FF), (D, FF), (FF, D),
)
WIDE_IN, TALL_OUT, WIDE_FF, TALL_FF = (0, 1, 2, 3, 4, 5), (6, 7), (8, 9), (10,)
SIZES = (D, D, INNER, KERNEL * CHANNELS, CHANNELS, HEADS_SSM, HEADS_SSM, HEADS_SSM, D * HEADS_SSM)


def block_offsets():
    starts, total = [], 0
    for rows, cols in SHAPES:
        starts.append(total)
        total += rows // BS * (cols // BS)
    return starts


def wide_order(members):
    starts = block_offsets()
    rows = SHAPES[members[0]][0] // BS
    return [starts[m] + r * (SHAPES[m][1] // BS) + q for r in range(rows) for m in members for q in range(SHAPES[m][1] // BS)]


def tall_order(members):
    starts = block_offsets()
    return [starts[m] + i for m in members for i in range(SHAPES[m][0] // BS * (SHAPES[m][1] // BS))]


def all_orders():
    return [wide_order(WIDE_IN), tall_order(TALL_OUT), wide_order(WIDE_FF), tall_order(TALL_FF)]


def unpack_vectors(flat):
    result, offset = [], 0
    for count in SIZES:
        result.append(flat[offset : offset + count])
        offset += count
    return result


def dot(left, right, precision=None):
    return jnp.dot(left, right, preferred_element_type=F32, precision=precision)


def dot_nt(left, right):
    return lax.dot_general(left, right, (((1,), (1,)), ((), ())), preferred_element_type=F32)


def dot_tn(left, right):
    return lax.dot_general(left, right, (((0,), (0,)), ((), ())), preferred_element_type=F32)


def sigmoid(v):
    return 1.0 / (1.0 + jnp.exp(-v))


def rms_scale(values):
    return lax.rsqrt(jnp.mean(values * values, axis=-1, keepdims=True) + EPS)


def kernel_params(**more):
    return pltpu.CompilerParams(vmem_limit_bytes=VMEM_MOST, **more)


def whole(shape):
    return pl.BlockSpec(shape, lambda *_: (0,) * len(shape))


MESH = pl.DeviceIdType.MESH
CORES = 2


def grid_of(mesh):
    try:
        wide = len({device.coords[0] for device in mesh.devices.flat})
    except AttributeError:
        wide = mesh.shape["seq"] // CORES
    return wide, mesh.shape["seq"] // CORES, mesh.shape["dp"] // wide


def parts_of(slots, tall):
    half = slots // CORES
    lone = half * 17 // 48 if tall == 2 and half >= 16 else 0
    return half, lone, half - lone


def place(grid):
    wide, tall, deep = grid
    dp, seq = lax.axis_index("dp"), lax.axis_index("seq")
    return dp % wide, seq // CORES, dp // wide, seq % CORES


def gather_kernel(grid, slots, src, out, kept, sem_own, sz, rz, sx, rx, sy, ry, sc, rc):
    wide, tall, deep = grid
    x, y, z, c = place(grid)
    half, lone, bulk = parts_of(slots, tall)
    me = z * wide + x
    seq = y * CORES + c
    base = c * half
    bulk_at = base + y * (half - bulk)
    lone_at = base + y * bulk
    other_at = base + (1 - y) * bulk if lone else base
    mate = y * CORES + (1 - c)
    over = (tall - 1 - y) * CORES + c

    barrier = pltpu.get_barrier_semaphore()
    count = jnp.int32(0)
    for axis, at, size in (("z", z, deep), ("x", x, wide)):
        for step in (1, -1):
            ok = (at + step >= 0) & (at + step < size)
            there = me + step * (wide if axis == "z" else 1)

            @pl.when(ok)
            def _(there=there):
                pl.semaphore_signal(barrier, inc=1, device_id=(there, seq), device_id_type=MESH)

            count = count + ok.astype(jnp.int32)
    pl.semaphore_signal(barrier, inc=1, device_id=(me, mate), device_id_type=MESH)
    count = count + 1
    if lone:
        pl.semaphore_signal(barrier, inc=1, device_id=(me, over), device_id_type=MESH)
        count = count + 1
    pl.semaphore_wait(barrier, count)

    take = pltpu.make_async_copy(src, kept, sem_own.at[0])
    take.start()
    sent = []

    def send(ok, source, target, send_sem, recv_sem, device):
        copy = pltpu.make_async_remote_copy(
            src_ref=source, dst_ref=target, send_sem=send_sem, recv_sem=recv_sem,
            device_id=device, device_id_type=MESH,
        )

        @pl.when(ok)
        def _():
            copy.start()

        sent.append((ok, copy))

    def arrived(ok, target, recv_sem):
        copy = pltpu.make_async_remote_copy(
            src_ref=target, dst_ref=target, send_sem=sem_own.at[0], recv_sem=recv_sem,
            device_id=(me, seq), device_id_type=MESH,
        )

        @pl.when(ok)
        def _():
            copy.wait_recv()

    yes = jnp.bool_(True)

    def piece(shard, at, size):
        return out.at[shard, pl.ds(at, size)]

    def pass_on(ok, shard):
        send(ok, piece(shard, bulk_at, bulk), piece(shard, bulk_at, bulk), sc.at[0, shard], rc.at[0, shard], (me, mate))
        if lone:
            send(ok, piece(shard, lone_at, lone), piece(shard, lone_at, lone), sy.at[shard], ry.at[shard], (me, over))

    def along_x(ok, zs, dirs, hop, own):
        for d, step in dirs:
            shard = zs * wide + x - step * hop
            go = ok & (x + step >= 0) & (x + step < wide)
            source = src.at[pl.ds(bulk_at, bulk)] if own else piece(shard, bulk_at, bulk)
            send(go, source, piece(shard, bulk_at, bulk), sx.at[d, hop, zs], rx.at[d, hop + 1, zs], (me + step, seq))

    both = ((0, 1), (1, -1))

    def columns(s):
        return [(yes, z)] if s == 0 else [((z - step * s >= 0) & (z - step * s < deep), z - step * s) for _, step in both]

    def x_in(s, hop):
        for ok, zs in columns(s):
            for d, step in both:
                from_x = x - step * hop
                come = ok & (from_x >= 0) & (from_x < wide)
                shard = zs * wide + from_x
                arrived(come, piece(shard, bulk_at, bulk), rx.at[d, hop, zs])
                along_x(come, zs, ((d, step),), hop, False)
                pass_on(come, shard)

    def y_in(ok, shard):
        if lone:
            arrived(ok, piece(shard, other_at, lone), ry.at[shard])
            send(ok, piece(shard, other_at, lone), piece(shard, other_at, lone), sc.at[1, shard], rc.at[1, shard], (me, mate))

    def y_all(s):
        for ok, zs in columns(s):
            if s > 0:
                y_in(ok, zs * wide + x)
            for hop in range(1, wide):
                for _, step in both:
                    from_x = x - step * hop
                    y_in(ok & (from_x >= 0) & (from_x < wide), zs * wide + from_x)

    for s in range(deep):
        for d, step in both:
            zs = z - step * s
            ok = (zs >= 0) & (zs < deep)
            shard = zs * wide + x
            if s:
                arrived(ok, piece(shard, bulk_at, bulk), rz.at[d, s])
            go = ok & (z + step >= 0) & (z + step < deep)
            source = piece(shard, bulk_at, bulk) if s else src.at[pl.ds(bulk_at, bulk)]
            if s + 1 < deep:
                send(go, source, piece(shard, bulk_at, bulk), sz.at[d, s], rz.at[d, s + 1], (me + step * wide, seq))
            if s:
                along_x(ok, zs, both, 0, False)
                pass_on(ok, shard)
        if s == 0:
            along_x(yes, z, both, 0, True)
            take.wait()
            put = pltpu.make_async_copy(kept, out.at[me], sem_own.at[1])
            put.start()
        else:
            for hop in range(1, wide):
                x_in(s - 1, hop)
        if s >= 2:
            y_all(s - 2)
    for hop in range(1, wide):
        x_in(deep - 1, hop)
    for s in range(max(deep - 2, 0), deep):
        y_all(s)
    put.wait()

    mate_base = (1 - c) * half
    mate_bulk = mate_base + y * (half - bulk)
    mate_other = mate_base + (1 - y) * bulk if lone else mate_base

    def last(shard, _):
        ok = shard != me
        arrived(ok, piece(shard, mate_bulk, bulk), rc.at[0, shard])
        if lone:
            arrived(ok, piece(shard, mate_other, lone), rc.at[1, shard])
        return 0

    lax.fori_loop(0, wide * deep, last, 0)
    for ok, copy in sent:
        @pl.when(ok)
        def _(copy=copy):
            copy.wait_send()


def gather_blocks(grid, own):
    wide, tall, deep = grid
    slots = own.shape[0]
    n = wide * deep
    sem = pltpu.SemaphoreType.DMA
    return pl.pallas_call(
        functools.partial(gather_kernel, grid, slots),
        out_shape=jax.ShapeDtypeStruct((n,) + own.shape, own.dtype),
        in_specs=[pl.BlockSpec(memory_space=pl.ANY)],
        out_specs=pl.BlockSpec(memory_space=pl.ANY),
        scratch_shapes=[
            pltpu.VMEM(own.shape, own.dtype),
            sem((2,)),
            sem((2, deep)), sem((2, deep + 1)),
            sem((2, wide, deep)), sem((2, wide + 1, deep)),
            sem((n,)), sem((n,)),
            sem((2, n)), sem((2, n)),
        ],
        compiler_params=pltpu.CompilerParams(collective_id=0, has_side_effects=True),
        name="gather_blocks",
    )(own)

def far_first(at, size, i):
    above, below = size - 1 - at, at
    less, more = jnp.minimum(above, below), jnp.maximum(above, below)
    long_side = jnp.where(above >= below, 1, -1)
    j = i - (more - less)
    near = at + jnp.where(j % 2 == 0, 1, -1) * (less - j // 2)
    return jnp.where(j < 0, at + long_side * (more - i), near)


def entry(at, size, source_below, target):
    lower = jnp.where(at > 0, size - at, 0) if size > 2 else 0
    return target - at if source_below else lower + at - target


def entries(size):
    return size + 1 if size > 2 else 1

SUBS = 2
LAG = 2
LONE = 1 / 3


def split_of(slots, tall):
    half = slots // CORES
    piece = half // SUBS
    lone = round(piece * LONE) if tall == 2 and piece >= 8 else 0
    return half, piece, lone, piece - lone


def reduce_kernel(grid, slots, part, vec, out, vec_out, acc, land_c, land_y, land_x, land_z, fin, vbuf, vland,
                  s_load, s_c, r_c, s_y, r_y, s_x, r_x, s_z, r_z, s_f, r_f, s_m, r_m, s_v, r_v):
    wide, tall, deep = grid
    n = wide * deep
    x, y, z, c = place(grid)
    half, size, lone, bulk = split_of(slots, tall)
    me = z * wide + x
    seq = y * CORES + c
    mate = y * CORES + (1 - c)
    bulk_at = y * lone
    lone_at = y * bulk
    other_at = (1 - y) * bulk
    bits = lambda size: [1 << b for b in range(size.bit_length() - 1)]
    partners = [(me, mate)]
    partners += [(me, (y ^ b) * CORES + c) for b in bits(tall)]
    partners += [(z * wide + (x ^ b), seq) for b in bits(wide)]
    partners += [((z ^ b) * wide + x, seq) for b in bits(deep)]

    barrier = pltpu.get_barrier_semaphore()
    count = jnp.int32(0)
    for step_by, at, length in ((wide, z, deep), (1, x, wide)):
        for step in (1, -1):
            ok = (at + step >= 0) & (at + step < length)

            @pl.when(ok)
            def _(there=me + step * step_by):
                pl.semaphore_signal(barrier, inc=1, device_id=(there, seq), device_id_type=MESH)

            count = count + ok.astype(jnp.int32)
    for device in partners:
        pl.semaphore_signal(barrier, inc=1, device_id=device, device_id_type=MESH)
    pl.semaphore_wait(barrier, count + len(partners))

    def remote(source, target, send_sem, recv_sem, device):
        return pltpu.make_async_remote_copy(
            src_ref=source, dst_ref=target, send_sem=send_sem, recv_sem=recv_sem,
            device_id=device, device_id_type=MESH,
        )

    def landed(target, recv_sem):
        remote(target, target, s_load.at[0], recv_sem, (me, seq)).wait_recv()

    group = wide * SUBS
    total = n * SUBS

    def item_of(k):
        xs, zs = far_first(x, wide, k % wide), far_first(z, deep, k // group)
        sub = (k // wide) % SUBS
        return xs, zs, sub, (zs * wide + xs) * SUBS + sub

    def own(k):
        xs, zs, sub, item = item_of(k)
        return pltpu.make_async_copy(part.at[zs * wide + xs, pl.ds(c * half + sub * size, size)], acc.at[item], s_load.at[item])

    def swap(k):
        xs, zs, sub, item = item_of(k)
        source = part.at[zs * wide + xs, pl.ds((1 - c) * half + sub * size, size)]
        return remote(source, land_c.at[item], s_c.at[item], r_c.at[item], (me, mate))

    def cross(item):
        return remote(acc.at[item, pl.ds(other_at, lone)], land_y.at[item], s_y.at[item], r_y.at[item], (me, (tall - 1 - y) * CORES + c))

    def begin(k, _):
        own(k).start()
        swap(k).start()
        return 0

    rounds = len(partners)

    def vec_copy(t):
        return remote(vbuf.at[t], vland.at[t], s_v.at[t], r_v.at[t], partners[t])

    vbuf[0] = vec[...]
    vec_copy(0).start()
    lax.fori_loop(0, total, begin, 0)
    for t in range(rounds):
        landed(vland.at[t], r_v.at[t])
        vbuf[t + 1] = vbuf[t] + vland[t]
        if t + 1 < rounds:
            vec_copy(t + 1).start()
    vec_out[...] = vbuf[rounds]

    def add(item, at, count, ref, first):
        def one(i, _):
            acc[item, at + i] = acc[item, at + i] + ref[first + (i,)]
            return 0

        lax.fori_loop(0, count, one, 0, unroll=4)

    def step_x(k, begin_it):
        xs, zs, sub, item = item_of(k)
        for below, step in ((True, 1), (False, -1)):
            to = entry(x + step, wide, below, xs)
            sent = remote(acc.at[item, pl.ds(bulk_at, bulk)], land_x.at[to, zs * SUBS + sub], s_x.at[item],
                          r_x.at[to, zs * SUBS + sub], (me + step, seq))

            @pl.when((xs - x) * step > 0)
            def _():
                if begin_it:
                    sent.start()
                else:
                    sent.wait_send()

    def take_x(k):
        xs, zs, sub, item = item_of(k)
        for below, step in ((True, 1), (False, -1)):
            comes = ((xs - x) * step >= 0) & (x - step >= 0) & (x - step < wide)
            at = entry(x, wide, below, xs)

            @pl.when(comes)
            def _():
                landed(land_x.at[at, zs * SUBS + sub], r_x.at[at, zs * SUBS + sub])
                add(item, bulk_at, bulk, land_x, (at, zs * SUBS + sub))

    def step_z(k, begin_it):
        xs, zs, sub, item = item_of(k)
        for below, step in ((True, 1), (False, -1)):
            to = entry(z + step, deep, below, zs)
            sent = remote(acc.at[item, pl.ds(bulk_at, bulk)], land_z.at[to, sub], s_z.at[zs * SUBS + sub], r_z.at[to, sub],
                          (me + step * wide, seq))

            @pl.when((zs - z) * step > 0)
            def _():
                if begin_it:
                    sent.start()
                else:
                    sent.wait_send()

    def take_z(k):
        xs, zs, sub, item = item_of(k)
        for below, step in ((True, 1), (False, -1)):
            comes = ((zs - z) * step >= 0) & (z - step >= 0) & (z - step < deep)
            at = entry(z, deep, below, zs)

            @pl.when(comes)
            def _():
                landed(land_z.at[at, sub], r_z.at[at, sub])
                add(item, bulk_at, bulk, land_z, (at, sub))

    planes = bits(tall)

    def swap_plane(t, sub):
        mine = pl.ds(bulk_at, bulk)
        return remote(acc.at[me * SUBS + sub, mine], fin.at[t, sub, mine], s_f.at[t, sub], r_f.at[t, sub], (me, (y ^ planes[t]) * CORES + c))

    def take_plane(t, sub):
        item = me * SUBS + sub
        theirs = pl.ds((1 - y) * lone if lone else 0, bulk)
        landed(fin.at[t, sub, theirs], r_f.at[t, sub])
        swap_plane(t, sub).wait_send()
        add(item, lone, size - 2 * lone, fin.at[t, sub, pl.ds(lone, size - 2 * lone)], ())
        if lone:
            cross(item).wait_send()
            acc[item, pl.ds(other_at, lone)] = fin[t, sub, pl.ds(other_at, lone)]

    def swap_core(sub):
        return remote(acc.at[me * SUBS + sub], out.at[pl.ds(c * half + sub * size, size)], s_m.at[sub], r_m.at[sub], (me, mate))

    def first(k, _):
        item = item_of(k)[3]
        own(k).wait()
        landed(land_c.at[item], r_c.at[item])
        add(item, 0, size, land_c, (item,))
        if lone:
            cross(item).start()
        return 0

    def second(k, _):
        @pl.when(k < total)
        def _():
            item = item_of(k)[3]
            if lone:
                landed(land_y.at[item], r_y.at[item])
                add(item, lone_at, lone, land_y, (item,))
            if wide > 2:
                @pl.when(item_of(k)[0] != x)
                def _():
                    take_x(k)
            step_x(k, True)

        late = k - LAG * wide

        @pl.when((late >= 0) & (late % wide == wide - 1))
        def _():
            take_x(late)
            take_z(late)
            step_z(late, True)

        return 0

    lax.fori_loop(0, total, first, 0)
    lax.fori_loop(0, total + (LAG - 1) * wide, second, 0)
    def finish(k, _):
        swap(k).wait_send()
        if lone:
            item = item_of(k)[3]

            @pl.when(item // SUBS != me)
            def _():
                cross(item).wait_send()

        step_x(k, False)

        @pl.when(k % wide == wide - 1)
        def _():
            step_z(k, False)

        return 0

    tail = [total + (LAG - 1) * wide + i for i in range(wide)]
    for k in tail:
        second(jnp.int32(k), 0)
    for t in range(len(planes)):
        for sub in range(SUBS):
            swap_plane(t, sub).start()
        for sub in range(SUBS):
            take_plane(t, sub)
            if t == len(planes) - 1:
                swap_core(sub).start()
    for sub in range(SUBS):
        out[pl.ds(c * half + sub * size, size)] = acc[me * SUBS + sub]
    lax.fori_loop(0, total, finish, 0)
    for t in range(rounds):
        vec_copy(t).wait_send()
    for sub in range(SUBS):
        swap_core(sub).wait_send()
        landed(out.at[pl.ds((1 - c) * half + sub * size, size)], r_m.at[sub])


def reduce_blocks(grid, part, vec):
    wide, tall, deep = grid
    n, slots = part.shape[:2]
    half, size, lone, bulk = split_of(slots, tall)
    tile = part.shape[2:]
    sem = pltpu.SemaphoreType.DMA
    rounds = sum(length.bit_length() - 1 for length in (CORES, wide, tall, deep))
    planes = max(tall.bit_length() - 1, 1)
    items = n * SUBS
    buf = lambda *lead: pltpu.VMEM(lead + tile, part.dtype)
    return pl.pallas_call(
        functools.partial(reduce_kernel, grid, slots),
        out_shape=(jax.ShapeDtypeStruct((slots,) + tile, part.dtype), jax.ShapeDtypeStruct(vec.shape, vec.dtype)),
        in_specs=[pl.BlockSpec(memory_space=pl.ANY), pl.BlockSpec(memory_space=pltpu.VMEM)],
        out_specs=(pl.BlockSpec(memory_space=pltpu.VMEM), pl.BlockSpec(memory_space=pltpu.VMEM)),
        scratch_shapes=[
            buf(items, size), buf(items, size), buf(items, max(lone, 1)), buf(entries(wide), deep * SUBS, bulk),
            buf(entries(deep), SUBS, bulk), buf(planes, SUBS, size),
            pltpu.VMEM((rounds + 1,) + vec.shape, vec.dtype), pltpu.VMEM((rounds,) + vec.shape, vec.dtype),
            sem((items,)), sem((items,)), sem((items,)), sem((items,)), sem((items,)), sem((items,)),
            sem((entries(wide), deep * SUBS)), sem((deep * SUBS,)), sem((entries(deep), SUBS)),
            sem((planes, SUBS)), sem((planes, SUBS)), sem((SUBS,)), sem((SUBS,)), sem((rounds,)), sem((rounds,)),
        ],
        compiler_params=pltpu.CompilerParams(collective_id=1, has_side_effects=True, vmem_limit_bytes=63 << 20),
        name="reduce_blocks",
    )(part, vec)


STEP_BLOCKS = 32
DEPTH = 4


def assemble_kernel(table, blocks, w_in, w_out, w_ff, w_down, wide, tall, s_in, s_out):
    outs = []
    for ref in (w_in, w_out, w_ff, w_down):
        rows, cols = ref.shape
        per_row = cols // BS
        deep = STEP_BLOCKS // per_row
        for r in range(rows // (BS * deep)):
            outs.append((ref, r * BS * deep, deep, per_row))

    def target(step):
        ref, at, deep, per_row = outs[step]
        slot = step % DEPTH
        return (wide.at[slot] if deep == 1 else tall.at[slot]), ref.at[pl.ds(at, BS * deep)], deep, per_row

    def fetch(step):
        buffer, _, deep, per_row = target(step)

        def one(i, _):
            rows = pl.ds(pl.multiple_of(i // per_row * BS, BS), BS)
            cols = pl.ds(pl.multiple_of(i % per_row * BS, BS), BS)
            pltpu.make_async_copy(blocks.at[table[step * STEP_BLOCKS + i]], buffer.at[rows, cols], s_in.at[step % DEPTH]).start()
            return 0

        lax.fori_loop(0, STEP_BLOCKS, one, 0)

    def put(step):
        buffer, place_to, _, _ = target(step)
        return pltpu.make_async_copy(buffer, place_to, s_out.at[step % DEPTH])

    steps = len(outs)
    for step in range(min(DEPTH - 1, steps)):
        fetch(step)
    for step in range(steps):
        buffer, place_to, _, _ = target(step)
        pltpu.make_async_copy(place_to, buffer, s_in.at[step % DEPTH]).wait()
        put(step).start()
        ahead = step + DEPTH - 1
        if ahead < steps:
            if step >= 1:
                put(step - 1).wait()
            fetch(ahead)
    for step in range(max(steps - DEPTH, 0), steps):
        put(step).wait()


def assemble(blocks, inverse):
    table = jnp.take(inverse, jnp.array(sum(all_orders(), []), jnp.int32))
    shapes = [(D, sum(SHAPES[m][1] for m in WIDE_IN)), (sum(SHAPES[m][0] for m in TALL_OUT), D), (D, 2 * FF), (FF, D)]
    hbm = pl.BlockSpec(memory_space=pl.ANY)
    return pl.pallas_call(
        assemble_kernel,
        out_shape=tuple(jax.ShapeDtypeStruct(shape, BF16) for shape in shapes),
        grid_spec=pltpu.PrefetchScalarGridSpec(
            num_scalar_prefetch=1, grid=(1,), in_specs=[hbm], out_specs=(hbm,) * 4,
            scratch_shapes=[
                pltpu.VMEM((DEPTH, BS, STEP_BLOCKS * BS), BF16),
                pltpu.VMEM((DEPTH, STEP_BLOCKS // (D // BS) * BS, D), BF16),
                pltpu.SemaphoreType.DMA((DEPTH,)), pltpu.SemaphoreType.DMA((DEPTH,)),
            ],
        ),
        compiler_params=kernel_params(),
        name="assemble",
    )(table, blocks)


GROUP = 32


def slot_grads_kernel(left_at, right_at, ins, mids, downs, outs, g_in, g_hidden, g_ff, cot, out, left, right):
    at = 0

    @pl.when(pl.program_id(0) == 0)
    def _():
        at = 0
        for ref in (ins, outs, mids, downs):
            for q in range(ref.shape[1] // BS):
                left[at : at + BS, :] = ref[:, q * BS : (q + 1) * BS].T
                at += BS
        at = 0
        for ref in (g_in, g_hidden, g_ff, cot):
            cols = ref.shape[1]
            right[:, at : at + cols] = ref[...]
            at += cols

    base = pl.program_id(0) * GROUP

    def one(i, _):
        rows = pl.ds(pl.multiple_of(left_at[base + i] * BS, BS), BS)
        cols = pl.ds(pl.multiple_of(right_at[base + i] * BS, BS), BS)
        out[i] = dot(left[rows, :], right[:, cols]).astype(BF16)
        return 0

    lax.fori_loop(0, GROUP, one, 0, unroll=4)


def grad_tables():
    lefts, rights = [], []
    left_base = {0: 0, 1: D, 2: D + INNER + QDIM, 3: 2 * D + INNER + QDIM}
    right_base = {0: 0, 1: 2 * INNER + 2 * NSTATE + QDIM + 2 * KDIM}
    right_base[2] = right_base[1] + D
    right_base[3] = right_base[2] + 2 * FF
    for kind, members in enumerate((WIDE_IN, TALL_OUT, WIDE_FF, TALL_FF)):
        row_at, col_at = left_base[kind] // BS, right_base[kind] // BS
        for m in members:
            rows, cols = SHAPES[m][0] // BS, SHAPES[m][1] // BS
            for r in range(rows):
                for q in range(cols):
                    lefts.append(row_at + r)
                    rights.append(col_at + q)
            if kind in (0, 2):
                col_at += cols
            else:
                row_at += rows
    return lefts, rights


def slot_grads(block_of_slot, ins, mids, downs, outs, g_in, g_hidden, g_ff, cot):
    lefts, rights = grad_tables()
    left_at = jnp.take(jnp.array(lefts, jnp.int32), block_of_slot)
    right_at = jnp.take(jnp.array(rights, jnp.int32), block_of_slot)
    count = block_of_slot.shape[0]
    arrays = (ins, mids, downs, outs, g_in, g_hidden, g_ff, cot)
    tokens = ins.shape[0]
    return pl.pallas_call(
        slot_grads_kernel,
        out_shape=jax.ShapeDtypeStruct((count, BS, BS), BF16),
        grid_spec=pltpu.PrefetchScalarGridSpec(
            num_scalar_prefetch=2, grid=(count // GROUP,),
            in_specs=[pl.BlockSpec(a.shape, lambda *_: (0, 0), pipeline_mode=pl.Buffered(1)) for a in arrays],
            out_specs=pl.BlockSpec((GROUP, BS, BS), lambda i, *_: (i, 0, 0)),
            scratch_shapes=[
                pltpu.VMEM((sum(a.shape[1] for a in arrays[:4]), tokens), BF16),
                pltpu.VMEM((tokens, sum(a.shape[1] for a in arrays[4:])), BF16),
            ],
        ),
        compiler_params=kernel_params(),
        name="slot_grads",
    )(left_at, right_at, *arrays)


SHAMPOO = 8


def shampoo_kernel(norm, total, master, left, right, left_root, right_root, grad, new_left, new_right, new_master, low):
    for i in range(SHAMPOO):
        g = total[i]
        value = g.astype(F32) * norm
        grad[i] = value
        new_left[i] = 0.5 * left[i] + dot_nt(g, g) * (0.5 * norm * norm / BS)
        new_right[i] = 0.5 * right[i] + dot_tn(g, g) * (0.5 * norm * norm / BS)
        inner = dot(g, right_root[i].astype(BF16))
        moved = dot(left_root[i].astype(BF16), inner.astype(BF16)) * (LR_MATRIX * norm)
        fresh = master[i] - moved
        new_master[i] = fresh
        low[i] = fresh.astype(BF16)


def shampoo(norm, total, master, left, right, left_root, right_root):
    slots = total.shape[0]
    spec = pl.BlockSpec((SHAMPOO, BS, BS), lambda i: (i, 0, 0))
    full = jax.ShapeDtypeStruct(master.shape, F32)
    return pl.pallas_call(
        functools.partial(shampoo_kernel, norm),
        out_shape=(full, full, full, full, jax.ShapeDtypeStruct(master.shape, BF16)),
        grid=(slots // SHAMPOO,),
        in_specs=[spec] * 6,
        out_specs=(spec,) * 5,
        compiler_params=kernel_params(),
        name="shampoo",
    )(total, master, left, right, left_root, right_root)


BLOCK = 256
HALO = 8


def lane_index(shape):
    return lax.broadcasted_iota(jnp.int32, shape, len(shape) - 1)


def conv_tile(extended, taps, marks, count):
    total = jnp.broadcast_to(taps[KERNEL : KERNEL + 1, :], (count, extended.shape[1]))
    for tap in range(KERNEL):
        total = total + taps[tap : tap + 1, :] * near_rows(extended, tap, count) * marks[:, tap : tap + 1]
    return total


def near_rows(extended, tap, count):
    back = REACH - tap
    moved = pltpu.roll(extended, back, 0) if back else extended
    return moved[HALO : HALO + count, :]


def softplus(v):
    return jnp.maximum(v, 0.0) + jnp.log(1.0 + jnp.exp(-jnp.abs(v)))


def chunk_decays(raw, params):
    delta = softplus(raw + params[0:1, :])
    decay = -delta * jnp.exp(params[1:2, :])
    block = raw.shape[0] if raw.shape[0] < BLOCK else BLOCK
    rows = lax.broadcasted_iota(jnp.int32, (block, block), 0)
    lower = (rows >= lane_index((block, block))).astype(F32)
    sums = [dot(lower, decay[i : i + block, :], HIGHEST) for i in range(0, raw.shape[0], block)]
    return delta, decay, jnp.concatenate(sums, axis=0)


def end_weights(delta, sums, marks):
    last = sums[-1:, :]
    return jnp.exp(last - sums) * delta * marks[:, 5:6], jnp.exp(last) * marks[-1:, 4:5]


def spread_matrix():
    rows = lax.broadcasted_iota(jnp.int32, (LANES, INNER), 0)
    return (rows == lane_index((LANES, INNER)) // HEAD).astype(F32)


def mix_first_kernel(proj_x, proj_bc, halo, taps, params, raw, marks, xbc, decays, decays_t, state, factor):
    tokens = raw.shape[0]
    mark = marks[...]
    for ref, at in ((proj_x, 0), (proj_bc, INNER)):
        step = 256
        for q in range(0, ref.shape[1], step):
            cols = slice(at + q, at + q + step)
            own = ref[:, q : q + step].astype(BF16).astype(F32)
            extended = jnp.concatenate([halo[:, cols].astype(F32), own], axis=0)
            value = conv_tile(extended, taps[:, cols], mark, tokens)
            xbc[:, cols] = (value * sigmoid(value)).astype(BF16)
    delta, decay, sums = chunk_decays(raw[...], params[...])
    decays[0] = delta
    decays[1] = sums
    decays_t[...] = sums.T
    spread = spread_matrix()
    total = jnp.zeros((NSTATE, INNER), F32)
    product = jnp.ones((1, LANES), F32)
    for i in range(0, tokens, BLOCK):
        rows = slice(i, i + BLOCK)
        weight, own = end_weights(delta[rows], sums[rows], mark[rows])
        weighted = (xbc[rows, :INNER].astype(F32) * dot(weight.astype(BF16), spread.astype(BF16))).astype(BF16)
        keep = dot(jnp.broadcast_to(own, (8, LANES)), spread, HIGHEST)[0:1]
        total = keep * total + dot_tn(xbc[rows, INNER : INNER + NSTATE], weighted)
        product = product * own
    state[...] = total.astype(BF16)
    factor[...] = jnp.broadcast_to(product, factor.shape)


def mix_first(proj, halo, taps, params, raw, marks):
    tokens = raw.shape[0]
    vmem = pl.BlockSpec(memory_space=pltpu.VMEM)
    return pl.pallas_call(
        mix_first_kernel,
        out_shape=(
            jax.ShapeDtypeStruct((tokens, CHANNELS), BF16),
            jax.ShapeDtypeStruct((2, tokens, LANES), F32),
            jax.ShapeDtypeStruct((LANES, tokens), F32),
            jax.ShapeDtypeStruct((NSTATE, INNER), BF16),
            jax.ShapeDtypeStruct((8, LANES), F32),
        ),
        grid=(1,),
        in_specs=[
            pl.BlockSpec((tokens, INNER), lambda i: (0, 1)),
            pl.BlockSpec((tokens, 2 * NSTATE), lambda i: (0, 2 * INNER // (2 * NSTATE))),
            vmem, vmem, vmem, vmem, vmem,
        ],
        out_specs=(vmem,) * 5,
        compiler_params=kernel_params(),
        name="mix_first",
    )(proj, proj, halo, taps, params, raw, marks)


def attend(left, right, mark_rows, mark_cols):
    return jnp.where(mark_rows & mark_cols, dot_nt(left, right), 0.0)


def halves(tile):
    low = lane_index(tile.shape) < HEAD
    zero = jnp.zeros_like(tile)
    return jnp.where(low, tile, zero), jnp.where(low, zero, tile)


def pair_column(values, a):
    return values[:, a * HEAD : a * HEAD + 1]


def mix_second_kernel(x, b, c, z, decays, decays_t, marks, labels, incoming, skip, gain, y, normed, states,
                      wide_sums, wide_delta, wide_end, keep, near, b_t, state, gated, squares):
    j = pl.program_id(0)
    tokens = x.shape[0]
    blocks = tokens // BLOCK
    cols = pl.ds(pl.multiple_of(j * LANES, LANES), LANES)

    @pl.when(j == 0)
    def _():
        spread = spread_matrix()
        rows = lax.broadcasted_iota(jnp.int32, (BLOCK, BLOCK), 0)
        ordered = rows >= lane_index((BLOCK, BLOCK))
        for i in range(blocks):
            at = slice(i * BLOCK, (i + 1) * BLOCK)
            mark = marks[at]
            same = mark[:, 6:7] == labels[0:1, at]
            near[i] = jnp.where(ordered & same, dot_nt(c[at], b[at]), 0.0)
            b_t[i] = b[at].T
            weight, own = end_weights(decays[0, at], decays[1, at], mark)
            wide_end[at] = dot(weight.astype(BF16), spread.astype(BF16)).astype(BF16)
            wide_sums[at] = dot(decays[1, at], spread, HIGHEST)
            wide_delta[at] = dot(decays[0, at].astype(BF16), spread.astype(BF16)).astype(BF16)
            keep[i] = dot(jnp.broadcast_to(own, (8, LANES)), spread, HIGHEST)
        squares[...] = jnp.zeros_like(squares)

    state[...] = incoming[...].astype(F32)
    for i in range(blocks):
        at = slice(i * BLOCK, (i + 1) * BLOCK)
        states[i] = state[...]
        tile = x[at].astype(F32)
        scaled = (tile * wide_delta[at, cols].astype(F32)).astype(BF16)
        sums = wide_sums[at, cols]
        total = jnp.zeros((BLOCK, LANES), F32)
        for a, part in enumerate(halves(scaled)):
            row = decays_t[pl.ds(2 * j + a, 1), at]
            weight = near[i] * jnp.exp(jnp.minimum(pair_column(sums, a) - row, 0.0))
            total = total + dot(weight.astype(BF16), part)
        carried = dot(c[at], state[...].astype(BF16))
        total = total + carried * jnp.exp(sums) * marks[at, 4:5] + skip[0:1, cols] * tile
        y[at] = total
        gate = z[at]
        gate = total * gate * sigmoid(gate)
        gated[at, cols] = gate
        squares[at] += gate * gate
        weighted = (tile * wide_end[at, cols].astype(F32)).astype(BF16)
        state[...] = keep[i, 0:1, cols] * state[...] + dot(b_t[i], weighted)
    states[blocks] = state[...]

    @pl.when(j == PAIRS - 1)
    def _():
        for i in range(blocks):
            at = slice(i * BLOCK, (i + 1) * BLOCK)
            scale = lax.rsqrt(jnp.sum(squares[at], axis=1, keepdims=True) / INNER + EPS)
            normed[at] = (gated[at] * scale * gain[0:1, :]).astype(BF16)


def mix_second(xbc, proj, decays, decays_t, marks, labels, incoming, skip, gain):
    tokens = xbc.shape[0]
    blocks = tokens // BLOCK
    tile = pl.BlockSpec((tokens, LANES), lambda j: (0, j))
    return pl.pallas_call(
        mix_second_kernel,
        out_shape=(
            jax.ShapeDtypeStruct((tokens, INNER), F32),
            jax.ShapeDtypeStruct((tokens, INNER), BF16),
            jax.ShapeDtypeStruct((blocks + 1, NSTATE, INNER), F32),
        ),
        grid=(PAIRS,),
        in_specs=[
            tile,
            pl.BlockSpec((tokens, NSTATE), lambda j: (0, INNER // NSTATE)),
            pl.BlockSpec((tokens, NSTATE), lambda j: (0, INNER // NSTATE + 1)),
            tile,
            whole(decays.shape), whole(decays_t.shape), whole(marks.shape), whole(labels.shape),
            pl.BlockSpec((NSTATE, LANES), lambda j: (0, j)),
            whole(skip.shape), whole(gain.shape),
        ],
        out_specs=(tile, whole((tokens, INNER)), pl.BlockSpec((blocks + 1, NSTATE, LANES), lambda j: (0, 0, j))),
        scratch_shapes=[
            pltpu.VMEM((tokens, INNER), F32), pltpu.VMEM((tokens, INNER), BF16), pltpu.VMEM((tokens, INNER), BF16),
            pltpu.VMEM((blocks, 8, INNER), F32), pltpu.VMEM((blocks, BLOCK, BLOCK), F32),
            pltpu.VMEM((blocks, NSTATE, BLOCK), BF16), pltpu.VMEM((NSTATE, LANES), F32),
            pltpu.VMEM((tokens, INNER), F32), pltpu.VMEM((tokens, LANES), F32),
        ],
        compiler_params=kernel_params(),
        name="mix_second",
    )(xbc, xbc, xbc, proj, decays, decays_t, marks, labels, incoming, skip, gain)


def gate_back_kernel(grad, y, z, gain, c, decays, marks, g_y, g_z, g_gain, g_state):
    step = pl.program_id(0)
    value, gate = y[...], z[...]
    opened = sigmoid(gate)
    swish = gate * opened
    gated = value * swish
    scale = lax.rsqrt(jnp.mean(gated * gated, axis=1, keepdims=True) + EPS)
    unit = gated * scale
    given = grad[...]
    scaled = given * gain[0:1, :]
    g_gated = scale * (scaled - unit * jnp.mean(scaled * unit, axis=1, keepdims=True))
    fresh = g_gated * swish
    g_y[...] = fresh.astype(BF16)
    g_z[...] = (g_gated * value * (opened + swish * (1.0 - opened))).astype(BF16)
    spread = spread_matrix()
    sums = decays[1]
    mark = marks[...]
    entry_weight = jnp.exp(sums) * mark[:, 4:5]
    own = jnp.exp(sums[-1:, :]) * mark[-1:, 4:5]
    keep = dot(jnp.broadcast_to(own, (8, LANES)), spread, HIGHEST)[0:1]
    weighted = (fresh * dot(entry_weight.astype(BF16), spread.astype(BF16))).astype(BF16)
    local = dot_tn(c[...], weighted)
    gains = jnp.broadcast_to(jnp.sum(given * unit, axis=0, keepdims=True), g_gain.shape)

    @pl.when(step == 0)
    def _():
        g_state[...] = local
        g_gain[...] = gains

    @pl.when(step > 0)
    def _():
        g_state[...] = keep * g_state[...] + local
        g_gain[...] += gains


def gate_back(grad, y, proj, gain, xbc, decays, marks):
    tokens = y.shape[0]
    blocks = tokens // BLOCK
    rows = lambda width, col: pl.BlockSpec((BLOCK, width), lambda i: (blocks - 1 - i, col))
    return pl.pallas_call(
        gate_back_kernel,
        out_shape=(
            jax.ShapeDtypeStruct((tokens, INNER), BF16),
            jax.ShapeDtypeStruct((tokens, INNER), BF16),
            jax.ShapeDtypeStruct((8, INNER), F32),
            jax.ShapeDtypeStruct((NSTATE, INNER), F32),
        ),
        grid=(blocks,),
        in_specs=[
            rows(INNER, 0), rows(INNER, 0), rows(INNER, 0), whole(gain.shape), rows(NSTATE, INNER // NSTATE + 1),
            pl.BlockSpec((2, BLOCK, LANES), lambda i: (0, blocks - 1 - i, 0)), rows(LANES, 0),
        ],
        out_specs=(rows(INNER, 0), rows(INNER, 0), whole((8, INNER)), whole((NSTATE, INNER))),
        compiler_params=kernel_params(),
        name="gate_back",
    )(grad, y, proj, gain, xbc, decays, marks)


def conv_back(grad, extended, taps, marks, count):
    acc = conv_tile(extended, taps, marks, count)
    opened = sigmoid(acc)
    g_acc = grad * (opened + acc * opened * (1.0 - opened))
    width = g_acc.shape[1]
    weights, result = [], jnp.zeros((HALO + count, width), F32)
    for tap in range(KERNEL):
        marked = g_acc * marks[:, tap : tap + 1]
        weights.append(jnp.sum(marked * near_rows(extended, tap, count), axis=0, keepdims=True))
        spread = jnp.concatenate([jnp.zeros((HALO, width), F32), marked * taps[tap : tap + 1, :]], axis=0)
        back = REACH - tap
        result = result + (pltpu.roll(spread, HALO + count - back, 0) if back else spread)
    weights.append(jnp.sum(g_acc, axis=0, keepdims=True))
    weights.append(jnp.zeros((8 - KERNEL - 1, width), F32))
    return result, jnp.concatenate(weights, axis=0)


def mix_back_kernel(x, b, c, proj_x, proj_bc, halo, taps, y, g_y, decays, decays_t, raw, params, marks, labels, states, leaving, skip,
                    g_conv, g_rim, g_taps, g_raw, g_params,
                    wide_sums, wide_delta, wide_end, wide_skip, keep, near, c_t, state, g_near, g_b, g_c, g_cum, g_delta, g_skip, ends):
    j = pl.program_id(0)
    tokens = x.shape[0]
    blocks = tokens // BLOCK
    cols = pl.ds(pl.multiple_of(j * LANES, LANES), LANES)
    lane = lane_index((LANES, LANES))
    gather = ((lax.broadcasted_iota(jnp.int32, (LANES, LANES), 0) // HEAD + 2 * j) == lane).astype(BF16)

    def collect(values):
        high = values.astype(BF16)
        return dot(high, gather) + dot((values - high.astype(F32)).astype(BF16), gather)

    @pl.when(j == 0)
    def _():
        spread = spread_matrix()
        rows = lax.broadcasted_iota(jnp.int32, (BLOCK, BLOCK), 0)
        ordered = rows <= lane_index((BLOCK, BLOCK))
        for i in range(blocks):
            at = slice(i * BLOCK, (i + 1) * BLOCK)
            mark = marks[at]
            same = mark[:, 6:7] == labels[0:1, at]
            near[i] = jnp.where(ordered & same, dot_nt(b[at], c[at]), 0.0)
            c_t[i] = c[at].T
            weight, own = end_weights(decays[0, at], decays[1, at], mark)
            end_only = jnp.exp(decays[1, at][-1:, :] - decays[1, at]) * mark[:, 5:6]
            wide_end[at] = dot(end_only.astype(BF16), spread.astype(BF16)).astype(BF16)
            wide_sums[at] = dot(decays[1, at], spread, HIGHEST)
            wide_delta[at] = dot(decays[0, at].astype(BF16), spread.astype(BF16)).astype(BF16)
            keep[i] = dot(jnp.broadcast_to(own, (8, LANES)), spread, HIGHEST)
        for ref in (g_near, g_b, g_c, g_cum, g_delta, g_skip, ends):
            ref[...] = jnp.zeros_like(ref)

    state[...] = leaving[...].astype(F32)
    g_x = []
    for i in range(blocks - 1, -1, -1):
        at = slice(i * BLOCK, (i + 1) * BLOCK)
        tile = x[at].astype(F32)
        step = wide_delta[at, cols].astype(F32)
        scaled = tile * step
        low_scaled = scaled.astype(BF16)
        sums = wide_sums[at, cols]
        end = wide_end[at, cols].astype(F32)
        given = g_y[at]
        low_state = state[...].astype(BF16)
        ends[i] += collect(jnp.broadcast_to(jnp.sum(states[i + 1] * state[...], axis=0, keepdims=True), (8, LANES)))
        total = end * dot(b[at], low_state)
        for a, (part, grad) in enumerate(zip(halves(low_scaled), halves(given))):
            row = decays_t[pl.ds(2 * j + a, 1), at]
            decay = jnp.exp(jnp.minimum(row - pair_column(sums, a), 0.0))
            total = total + dot((near[i] * decay).astype(BF16), grad)
            g_near[i] += decay * dot_nt(part, given)
        given = given.astype(F32)
        entry = jnp.exp(sums) * marks[at, 4:5]
        reached = (given * entry).astype(BF16)
        g_b[at] += dot_nt((scaled * end).astype(BF16), low_state)
        g_c[at] += dot_nt(reached, states[i].astype(BF16))
        own_skip = skip[0:1, cols]
        g_cum[at] += collect(given * (y[at] - own_skip * tile) - scaled * total)
        g_delta[at] += collect(total * tile)
        g_skip[...] += collect(jnp.broadcast_to(jnp.sum(given * tile, axis=0, keepdims=True), (8, LANES)))
        g_x.append(step * total + own_skip * given)
        state[...] = keep[i, 0:1, cols] * state[...] + dot(c_t[i], reached)

    mark = marks[...]
    own = proj_x[...].astype(BF16).astype(F32)
    extended = jnp.concatenate([halo[:, cols].astype(F32), own], axis=0)
    result, weights = conv_back(jnp.concatenate(g_x[::-1], axis=0), extended, taps[:, cols], mark, tokens)
    g_rim[:HALO, cols] = result[:HALO]
    g_rim[HALO:, cols] = result[tokens:]
    g_conv[:, cols] = result[HALO:].astype(BF16)
    g_taps[:, cols] = weights

    @pl.when(j == PAIRS - 1)
    def _():
        for i in range(blocks):
            at = slice(i * BLOCK, (i + 1) * BLOCK)
            rows = lax.broadcasted_iota(jnp.int32, (BLOCK, BLOCK), 0)
            seen = (rows <= lane_index((BLOCK, BLOCK))) & (marks[at, 6:7] == labels[0:1, at])
            grad = jnp.where(seen, g_near[i], 0.0)
            g_b[at] += dot(grad.astype(BF16), c[at])
            g_c[at] += dot(grad.T.astype(BF16), b[at])
        for k, ref in enumerate((g_b, g_c)):
            at = slice(INNER + k * NSTATE, INNER + (k + 1) * NSTATE)
            own = proj_bc[:, k * NSTATE : (k + 1) * NSTATE].astype(BF16).astype(F32)
            extended = jnp.concatenate([halo[:, at].astype(F32), own], axis=0)
            result, weights = conv_back(ref[...], extended, taps[:, at], mark, tokens)
            g_rim[:HALO, at] = result[:HALO]
            g_rim[HALO:, at] = result[tokens:]
            g_conv[:, at] = result[HALO:].astype(BF16)
            g_taps[:, at] = weights
        rate = -jnp.exp(params[1:2, :])
        bias_sum = jnp.zeros((1, LANES), F32)
        rate_sum = jnp.zeros((1, LANES), F32)
        rows = lax.broadcasted_iota(jnp.int32, (BLOCK, BLOCK), 0)
        upper = (rows <= lane_index((BLOCK, BLOCK))).astype(F32)
        for i in range(blocks):
            at = slice(i * BLOCK, (i + 1) * BLOCK)
            g_decay = dot(upper, g_cum[at], HIGHEST) + ends[i, 0:1, :]
            delta = decays[0, at]
            full = g_delta[at] + g_decay * rate
            full = full * sigmoid(raw[at] + params[0:1, :])
            g_raw[at] = full.astype(BF16)
            bias_sum = bias_sum + jnp.sum(full, axis=0, keepdims=True)
            rate_sum = rate_sum + jnp.sum(g_decay * delta * rate, axis=0, keepdims=True)
        g_params[...] = jnp.concatenate([bias_sum, rate_sum, g_skip[0:1, :], jnp.zeros((5, LANES), F32)], axis=0)


def mix_back(xbc, proj, halo, taps, y, g_y, decays, decays_t, raw, params, marks, labels, states, leaving, skip):
    tokens = xbc.shape[0]
    blocks = tokens // BLOCK
    tile = pl.BlockSpec((tokens, LANES), lambda j: (0, j))
    acc = lambda *shape: pltpu.VMEM(shape, F32)
    return pl.pallas_call(
        mix_back_kernel,
        out_shape=(
            jax.ShapeDtypeStruct((tokens, CHANNELS), BF16),
            jax.ShapeDtypeStruct((2 * HALO, CHANNELS), F32),
            jax.ShapeDtypeStruct((8, CHANNELS), F32),
            jax.ShapeDtypeStruct((tokens, LANES), BF16),
            jax.ShapeDtypeStruct((8, LANES), F32),
        ),
        grid=(PAIRS,),
        in_specs=[
            tile,
            pl.BlockSpec((tokens, NSTATE), lambda j: (0, INNER // NSTATE)),
            pl.BlockSpec((tokens, NSTATE), lambda j: (0, INNER // NSTATE + 1)),
            pl.BlockSpec((tokens, LANES), lambda j: (0, PAIRS + j)),
            pl.BlockSpec((tokens, 2 * NSTATE), lambda j: (0, 2 * INNER // (2 * NSTATE))),
            whole(halo.shape), whole(taps.shape), tile, tile,
            whole(decays.shape), whole(decays_t.shape), whole(raw.shape), whole(params.shape), whole(marks.shape), whole(labels.shape),
            pl.BlockSpec((blocks + 1, NSTATE, LANES), lambda j: (0, 0, j)),
            pl.BlockSpec((NSTATE, LANES), lambda j: (0, j)),
            whole(skip.shape),
        ],
        out_specs=(
            whole((tokens, CHANNELS)), whole((2 * HALO, CHANNELS)), whole((8, CHANNELS)), whole((tokens, LANES)), whole((8, LANES)),
        ),
        scratch_shapes=[
            acc(tokens, INNER), pltpu.VMEM((tokens, INNER), BF16), pltpu.VMEM((tokens, INNER), BF16), acc(8, LANES),
            acc(blocks, 8, INNER), acc(blocks, BLOCK, BLOCK), pltpu.VMEM((blocks, NSTATE, BLOCK), BF16), acc(NSTATE, LANES),
            acc(blocks, BLOCK, BLOCK), acc(tokens, NSTATE), acc(tokens, NSTATE), acc(tokens, LANES), acc(tokens, LANES),
            acc(8, LANES), acc(blocks, 8, LANES),
        ],
        compiler_params=kernel_params(),
        name="mix_back",
    )(xbc, xbc, xbc, proj, proj, halo, taps, y, g_y, decays, decays_t, raw, params, marks, labels, states, leaving, skip)


QBLOCK = 256
GROUPS = HEADS // KV_HEADS
QPAIRS = QDIM // LANES
SCALE = 1.0 / math.sqrt(HEAD)


def swap_halves(values):
    half = HEAD // 2
    front = lane_index(values.shape) % HEAD < half
    width = values.shape[-1]
    return jnp.where(front, pltpu.roll(values, width - half, 1), pltpu.roll(values, half, 1))


def turn(values, cosine, sine):
    return values * cosine + swap_halves(values) * sine


def rope_kernel(*refs):
    queries, (k, v, cosine, sine, q_out, kv_out) = refs[:QPAIRS], refs[QPAIRS:]
    cos, sin = cosine[...], sine[...]
    for p, q in enumerate(queries):
        q_out[:, p * LANES : (p + 1) * LANES] = turn(q[...], cos, sin).astype(BF16)
    kv_out[:, :KDIM] = turn(k[...], cos, sin).astype(BF16)
    kv_out[:, KDIM:] = v[...].astype(BF16)


def rope_all(proj, cosine, sine):
    tokens = proj.shape[0]
    start = 2 * INNER + 2 * NSTATE
    return pl.pallas_call(
        rope_kernel,
        out_shape=(jax.ShapeDtypeStruct((tokens, QDIM), BF16), jax.ShapeDtypeStruct((tokens, 2 * KDIM), BF16)),
        grid=(1,),
        in_specs=[
            pl.BlockSpec((tokens, LANES), lambda i, p=p: (0, start // LANES + p)) for p in range(QPAIRS + 2)
        ] + [whole(cosine.shape), whole(sine.shape)],
        out_specs=(whole((tokens, QDIM)), whole((tokens, 2 * KDIM))),
        compiler_params=kernel_params(),
        name="rope",
    )(*[proj] * (QPAIRS + 2), cosine, sine)


def both_sides(tile, both):
    low = lane_index(tile.shape) < HEAD
    zero = jnp.zeros_like(tile)
    moved = pltpu.roll(tile.astype(F32), HEAD, 1).astype(tile.dtype)
    both[0, 0] = jnp.where(low, tile, zero)
    both[0, 1] = jnp.where(low, zero, moved)
    both[1, 0] = jnp.where(low, moved, zero)
    both[1, 1] = jnp.where(low, zero, tile)


def attend_kernel(q, kv, key_labels, marks, context, stats, keys, values):
    block, pair = pl.program_id(0), pl.program_id(1)
    window = DOC_MOST + QBLOCK
    start = pl.multiple_of(block * QBLOCK, QBLOCK)

    @pl.when((block == 0) & (pair == 0))
    def _():
        both_sides(kv[:, :KDIM], keys)
        both_sides(kv[:, KDIM:], values)

    group = pair // (GROUPS // 2)
    rows = lax.broadcasted_iota(jnp.int32, (QBLOCK, window), 0)
    cols = lane_index((QBLOCK, window))
    seen = (cols <= rows + DOC_MOST) & (marks[:, 6:7] == key_labels[0, 0:1, :])
    total = jnp.zeros((QBLOCK, LANES), F32)
    found = jnp.zeros((QBLOCK, LANES), F32)
    for a in range(2):
        scores = dot_nt(q[...], keys[group, a, pl.ds(start, window), :]) * SCALE
        scores = jnp.where(seen, scores, NEG_BIG)
        most = jnp.max(scores, axis=1, keepdims=True)
        probs = jnp.exp(scores - most)
        mass = jnp.sum(probs, axis=1, keepdims=True)
        probs = probs * (1.0 / mass)
        total = total + dot(probs.astype(BF16), values[group, a, pl.ds(start, window), :])
        found = jnp.where(lane_index(found.shape) == a, most + jnp.log(mass), found)
    context[...] = total.astype(BF16)
    stats[0] = found.T[0:8, :]


def attend(q, kv, key_labels, marks):
    tokens = q.shape[0]
    blocks = tokens // QBLOCK
    tile = pl.BlockSpec((QBLOCK, LANES), lambda i, p: (i, p))
    return pl.pallas_call(
        attend_kernel,
        out_shape=(jax.ShapeDtypeStruct((tokens, QDIM), BF16), jax.ShapeDtypeStruct((QPAIRS, 8, tokens), F32)),
        grid=(blocks, QPAIRS),
        in_specs=[
            tile, whole(kv.shape), pl.BlockSpec((1,) + key_labels.shape[1:], lambda i, p: (i, 0, 0)),
            pl.BlockSpec((QBLOCK, LANES), lambda i, p: (i, 0)),
        ],
        out_specs=(tile, pl.BlockSpec((1, 8, QBLOCK), lambda i, p: (p, 0, i))),
        scratch_shapes=[pltpu.VMEM((2, 2) + (kv.shape[0], LANES), BF16)] * 2,
        compiler_params=kernel_params(),
        name="attend",
    )(q, kv, key_labels, marks)


def attend_back_kernel(q, kv, given, key_marks, query_labels, stats, cosine, sine, g_q, g_kv, keys, values, g_key, g_value):
    block, pair = pl.program_id(0), pl.program_id(1)
    window = DOC_MOST + QBLOCK
    start = pl.multiple_of(block * QBLOCK, QBLOCK)

    @pl.when((block == 0) & (pair == 0))
    def _():
        both_sides(kv[:, :KDIM], keys)
        both_sides(kv[:, KDIM:], values)
        g_key[...] = jnp.zeros_like(g_key)
        g_value[...] = jnp.zeros_like(g_value)

    group = pair // (GROUPS // 2)
    rows = lax.broadcasted_iota(jnp.int32, (window, QBLOCK), 0)
    cols = lane_index((window, QBLOCK))
    seen = (rows <= cols + DOC_MOST) & (key_marks[0, :, 0:1] == query_labels[0:1, :])
    at = pl.ds(start, window)
    query, grad = q[...], given[...].astype(BF16)
    total = jnp.zeros((QBLOCK, LANES), F32)
    for a, (query_part, grad_part) in enumerate(zip(halves(query), halves(grad))):
        key = keys[group, a, at, :]
        scores = jnp.where(seen, dot_nt(key, query) * SCALE, NEG_BIG)
        probs = jnp.exp(scores - stats[0, a : a + 1, :])
        g_probs = dot_nt(values[group, a, at, :], grad)
        mean = jnp.sum(probs * g_probs, axis=0, keepdims=True)
        g_scores = (probs * (g_probs - mean)).astype(BF16)
        g_key[group, at] += dot(g_scores, query_part) * SCALE
        g_value[group, at] += dot(probs.astype(BF16), grad_part)
        total = total + dot_tn(g_scores, key)
    g_q[...] = turn(total * SCALE, cosine[...], -sine[...]).astype(BF16)

    @pl.when((block == pl.num_programs(0) - 1) & (pair == QPAIRS - 1))
    def _():
        for k, ref in enumerate((g_key, g_value)):
            first = ref[0] + pltpu.roll(ref[0], HEAD, 1)
            second = ref[1] + pltpu.roll(ref[1], HEAD, 1)
            g_kv[:, k * KDIM : (k + 1) * KDIM] = jnp.where(lane_index(first.shape) < HEAD, first, second).astype(BF16)


def attend_back(q, kv, given, key_marks, query_labels, stats, cosine, sine):
    tokens = q.shape[0]
    blocks = tokens // QBLOCK
    tile = pl.BlockSpec((QBLOCK, LANES), lambda i, p: (i, p))
    row = pl.BlockSpec((QBLOCK, LANES), lambda i, p: (i, 0))
    return pl.pallas_call(
        attend_back_kernel,
        out_shape=(jax.ShapeDtypeStruct((tokens, QDIM), BF16), jax.ShapeDtypeStruct(kv.shape, BF16)),
        grid=(blocks, QPAIRS),
        in_specs=[
            tile, whole(kv.shape), pl.BlockSpec((QBLOCK, LANES), lambda i, p: (i, PAIRS + p)),
            pl.BlockSpec((1,) + key_marks.shape[1:], lambda i, p: (i, 0, 0)),
            pl.BlockSpec((8, QBLOCK), lambda i, p: (0, i)),
            pl.BlockSpec((1, 8, QBLOCK), lambda i, p: (p, 0, i)), row, row,
        ],
        out_specs=(tile, whole(kv.shape)),
        scratch_shapes=[pltpu.VMEM((2, 2) + (kv.shape[0], LANES), BF16)] * 2 + [pltpu.VMEM((2, kv.shape[0], LANES), F32)] * 2,
        compiler_params=kernel_params(),
        name="attend_back",
    )(q, kv, given, key_marks, query_labels, stats, cosine, sine)


def turn_back_kernel(g_kv, cosine, sine, out):
    out[:, :KDIM] = turn(g_kv[:, :KDIM], cosine[...], -sine[...]).astype(BF16)
    out[:, KDIM:] = g_kv[:, KDIM:].astype(BF16)


def turn_back(g_kv, cosine, sine):
    return pl.pallas_call(
        turn_back_kernel, out_shape=jax.ShapeDtypeStruct(g_kv.shape, BF16), compiler_params=kernel_params(), name="turn_back",
    )(g_kv, cosine, sine)


def spans(seq, micro):
    return seq // micro, micro


def regroup(rows, micro):
    seq = lax.axis_size("seq")
    each = seq // micro
    here = lax.axis_index("seq")
    pieces = []
    for t in range(micro):
        pairs = [(j, ((j + t) % micro) * each + j // micro) for j in range(seq)]
        pieces.append(lax.ppermute(lax.dynamic_index_in_dim(rows, (here + t) % micro, 0, False), "seq", pairs))
    order = here // each
    stacked = jnp.stack(pieces)
    return jnp.concatenate([lax.dynamic_index_in_dim(stacked, (order - q) % micro, 0, False) for q in range(micro)], axis=0)


def ungroup(rows, micro):
    seq = lax.axis_size("seq")
    each = seq // micro
    here = lax.axis_index("seq")
    order = here // each
    cut = rows.reshape((micro, rows.shape[0] // micro) + rows.shape[1:])
    pieces = []
    for t in range(micro):
        pairs = [(((j + t) % micro) * each + j // micro, j) for j in range(seq)]
        pieces.append(lax.ppermute(lax.dynamic_index_in_dim(cut, (order - t) % micro, 0, False), "seq", pairs))
    stacked = jnp.stack(pieces)
    return jnp.stack([lax.dynamic_index_in_dim(stacked, (m - here) % micro, 0, False) for m in range(micro)])


def along(value, steps, micro):
    seq = lax.axis_size("seq")
    each = seq // micro
    pairs = [(s, s + steps) for s in range(seq) if 0 <= s % each + steps < each]
    return lax.ppermute(value, "seq", pairs)


def pad_rows(*rows):
    width = rows[0].shape[-1]
    return jnp.concatenate([r.reshape(-1, width) for r in rows] + [jnp.zeros((8 - sum(r.size // width for r in rows), width), F32)], axis=0)


def shards(grid, tokens, cotangent, doc_ids, master_blocks, block_of_slot, left_stats, right_stats, left_roots, right_roots,
           vector_params, first_moment, second_moment, adam_step):
    micro, piece = tokens.shape[:2]
    seq = lax.axis_size("seq")
    each = seq // micro
    count = micro * piece
    here = lax.axis_index("seq")
    rank = here % each
    start = rank * count
    slots = master_blocks.shape[0]

    inverse = jnp.zeros_like(block_of_slot).at[block_of_slot].set(jnp.arange(block_of_slot.shape[0], dtype=jnp.int32), unique_indices=True)
    gathered = gather_blocks(grid, master_blocks.astype(BF16)).reshape(-1, BS, BS)
    w_in, w_out, w_ff, w_down = assemble(gathered, inverse)
    gain_in, gain_mid, gain_mix, conv_weight, conv_bias, dt_bias, a_log, skip, w_dt = unpack_vectors(vector_params)
    w_dt = jnp.pad(w_dt.reshape(D, HEADS_SSM), ((0, 0), (0, LANES - HEADS_SSM))).astype(BF16)
    taps = pad_rows(conv_weight.reshape(KERNEL, CHANNELS), conv_bias)
    lane_pad = lambda v: jnp.pad(v, (0, LANES - HEADS_SSM))
    params = pad_rows(lane_pad(dt_bias), lane_pad(a_log))
    wide_skip = pad_rows(jnp.repeat(skip, HEAD))
    wide_gain = pad_rows(gain_mix)

    labels_all = lax.all_gather(doc_ids, "seq", axis=1, tiled=True)
    row = lax.dynamic_index_in_dim(labels_all, here // each, 0, False)
    before = jnp.concatenate([jnp.full((DOC_MOST,), -1, jnp.int32), row])
    window = lax.dynamic_slice_in_dim(before, start, DOC_MOST + count)
    labels = window[DOC_MOST:]
    blocks = count // BLOCK
    columns = [(window[DOC_MOST - REACH + tap : DOC_MOST - REACH + tap + count] == labels).astype(F32) for tap in range(KERNEL)]
    by_block = labels.reshape(blocks, BLOCK)
    entries_at = window[DOC_MOST - 1 : DOC_MOST - 1 + count].reshape(blocks, BLOCK)[:, :1]
    columns.append((by_block == entries_at).astype(F32).reshape(-1))
    columns.append((by_block == by_block[:, -1:]).astype(F32).reshape(-1))
    columns.append(labels.astype(F32))
    marks = jnp.pad(jnp.stack(columns, axis=1), ((0, 0), (0, LANES - len(columns))))
    label_rows = jnp.broadcast_to(labels.astype(F32)[None], (8, count))
    far = jnp.stack([window[i : i + DOC_MOST + QBLOCK] for i in range(0, count, QBLOCK)]).astype(F32)
    key_labels = jnp.broadcast_to(far[:, None, :], (far.shape[0], 8, far.shape[1]))
    key_marks = jnp.broadcast_to(far[:, :, None], far.shape + (8,))
    first = jnp.sum((row[None, :] < labels[:, None]).astype(jnp.int32), axis=1)
    positions = (start + jnp.arange(count) - first).astype(F32)
    half = HEAD // 2
    frequency = jnp.exp(jnp.arange(half, dtype=F32) * (-2.0 * math.log(THETA) / HEAD))
    angles = positions[:, None] * frequency[None, :]
    cos, sin = jnp.cos(angles), jnp.sin(angles)
    cosine = jnp.concatenate([cos] * 4, axis=1)
    sine = jnp.concatenate([-sin, sin] * 2, axis=1)

    rows = regroup(tokens, micro)
    given = regroup(cotangent, micro)
    inputs = rows.astype(F32)
    normed_in = (inputs * rms_scale(inputs) * gain_in).astype(BF16)
    proj = dot(normed_in, w_in)
    raw = dot(normed_in, w_dt)
    halo = along(proj[count - HALO :, INNER : INNER + CHANNELS].astype(BF16), 1, micro)
    q, kv = rope_all(proj, cosine, sine)
    xbc, decays, decays_t, state, factor = mix_first(proj, halo, taps, params, raw, marks)
    past = min(each - 1, -(-DOC_MOST // count))
    earlier = [along(kv, back, micro) for back in range(past, 0, -1)]
    if past * count < DOC_MOST:
        earlier.insert(0, jnp.zeros((DOC_MOST - past * count, kv.shape[1]), BF16))
    reach = jnp.concatenate(earlier + [kv], axis=0)[-(DOC_MOST + count) :]
    wide = lambda f: jnp.repeat(f[0, :HEADS_SSM], HEAD)[None]
    incoming = along(state, each - 1, micro).astype(F32) if each > 1 else jnp.zeros(state.shape, F32)
    for back in range(each - 2, 0, -1):
        incoming = along(state, back, micro).astype(F32) + wide(along(factor, back, micro)) * incoming
    y, normed_ssm, states = mix_second(xbc, proj, decays, decays_t, marks, label_rows, incoming, wide_skip, wide_gain)
    context, stats = attend(q, reach, key_labels, marks)
    hidden = inputs + (dot(normed_ssm, w_out[:INNER]) + dot(context, w_out[INNER:]))
    normed_mid = (hidden * rms_scale(hidden) * gain_mid).astype(BF16)
    both = dot(normed_mid, w_ff)
    gate, upper = both[:, :FF], both[:, FF:]
    opened = sigmoid(gate)
    mixed = (gate * opened * upper).astype(BF16)
    layer_out = ungroup((hidden + dot(mixed, w_down)).astype(BF16), micro)

    g_mixed = dot_nt(given, w_down)
    g_gate = g_mixed * upper * (opened + gate * opened * (1.0 - opened))
    g_ff = jnp.concatenate([g_gate.astype(BF16), (g_mixed * gate * opened).astype(BF16)], axis=1)

    def norm_back(grad, values, gain):
        scale = rms_scale(values)
        unit = values * scale
        scaled = grad * gain
        return scale * (scaled - unit * jnp.mean(scaled * unit, axis=1, keepdims=True)), jnp.sum(grad * unit, axis=0)

    g_values, g_gain_mid = norm_back(dot_nt(g_ff, w_ff), hidden, gain_mid)
    g_hidden = given.astype(F32) + g_values
    hidden_low = g_hidden.astype(BF16)
    g_out = dot_nt(hidden_low, w_out)
    g_y, g_z, g_gain_mix, g_state = gate_back(g_out, y, proj, wide_gain, xbc, decays, marks)
    low_state = g_state.astype(BF16)
    leaving = along(low_state, 1 - each, micro).astype(F32) if each > 1 else jnp.zeros(state.shape, F32)
    for ahead in range(each - 2, 0, -1):
        leaving = along(low_state, -ahead, micro).astype(F32) + wide(along(factor, -ahead, micro)) * leaving
    g_q, g_reach = attend_back(q, reach, g_out, key_marks, label_rows, stats, cosine, sine)
    g_conv, g_rim, g_taps, g_raw, g_params = mix_back(
        xbc, proj, halo, taps, y, g_y, decays, decays_t, raw, params, marks, label_rows, states, leaving, wide_skip
    )
    g_kv = g_reach[-count:].astype(F32)
    for back in range(1, past + 1):
        low = max(0, DOC_MOST - back * count)
        part = g_reach[low : DOC_MOST - (back - 1) * count]
        moved = along(part, -back, micro).astype(F32)
        g_kv = g_kv + jnp.pad(moved, ((count - part.shape[0], 0), (0, 0)))
    g_kv = turn_back(g_kv, cosine, sine)
    rim = along(g_rim[:HALO], -1, micro)
    g_conv = lax.dynamic_update_slice(g_conv, (g_rim[HALO:] + rim).astype(BF16), (count - HALO, 0))
    g_in = jnp.concatenate([g_z, g_conv, g_q, g_kv], axis=1)
    g_values, g_gain_in = norm_back(dot_nt(g_in, w_in) + dot_nt(g_raw, w_dt), inputs, gain_in)
    grad_tokens = ungroup((g_values + g_hidden).astype(BF16), micro).astype(F32)
    g_w_dt = dot_tn(normed_in, g_raw)

    flat = slot_grads(block_of_slot, normed_in, normed_mid, mixed, jnp.concatenate([normed_ssm, context], axis=1),
                      g_in, hidden_low, g_ff, given)
    parts = [g_gain_in, g_gain_mid, g_gain_mix[0], g_taps[:KERNEL].reshape(-1), g_taps[KERNEL]]
    parts += [g_params[i, :HEADS_SSM] for i in range(3)] + [g_w_dt[:, :HEADS_SSM].reshape(-1)]
    width = vector_params.shape[0]
    height = -(-width // (8 * LANES)) * 8
    vector = jnp.concatenate(parts + [jnp.zeros((height * LANES - width,), F32)]).reshape(height, LANES)
    total, vector = reduce_blocks(grid, flat.reshape(-1, slots, BS, BS), vector)
    norm = 1.0 / math.sqrt(count * seq * lax.axis_size("dp"))
    updates = shampoo(norm, total, master_blocks, left_stats, right_stats, left_roots, right_roots)
    g_vector = vector.reshape(-1)[:width] * norm
    step = adam_step[0].astype(F32)
    new_first = BETA_ONE * first_moment + (1.0 - BETA_ONE) * g_vector
    new_second = BETA_TWO * second_moment + (1.0 - BETA_TWO) * g_vector * g_vector
    first_hat = new_first / (1.0 - jnp.power(BETA_ONE, step))
    second_hat = new_second / (1.0 - jnp.power(BETA_TWO, step))
    new_vector = vector_params - LR_VECTOR * first_hat / (jnp.sqrt(second_hat) + ADAM_EPS)
    return (layer_out, grad_tokens) + tuple(updates) + (g_vector, new_vector, new_first, new_second)


def solution(mesh):
    line, block, copied = P("dp", "seq", None), P("dp", None, None), P()
    return jax.shard_map(
        functools.partial(shards, grid_of(mesh)),
        mesh=mesh,
        in_specs=(line, line, P("dp", "seq"), block, copied, block, block, block, block, copied, copied, copied, copied),
        out_specs=(line, line) + (block,) * 5 + (copied,) * 4,
        check_vma=False,
    )
```

profile of v0, /device:TPU:11, one launch (start us, length us, event | category | flops | bytes accessed | tf_op | source)
XLA Modules:
  0.0 679.4 jit_solution(14346509298953427461)
XLA Ops:
  10.0 21.6 %all_gather.3 = s32[2,1024]{1,0:T(2,128)S(1)} all-gather(s32[2,256]{1,0:T(2,128)S(1)} %copy-done.35), channel_id=1, replica_groups=mesh['dp'=8,'seq'=4] {'seq'}, dimensions={1}, use_global_device_ids=true | all-gather | bytes 10240 | tf_op jit(solution)/shard_map/all_gather | solution.py:1432
  35.9 5.1 convert_element_type.102.src
  41.0 114.4 %gather_blocks.1 = bf16[8,96,128,128]{3,2,1,0:T(8,128)(2,1)} custom-call(bf16[96,128,128]{2,1,0:T(8,128)(2,1)} %convert_element_type.102.src), custom_call_target="tpu_custom_call" | custom-call | tf_op jit(solution)/shard_map/gather_blocks/pallas_call | solution.py:290
  166.4 4.9 gather_fusion
  171.3 18.3 %assemble.1 = (bf16[1024,4096]{1,0:T(8,128)(2,1)}, bf16[2048,1024]{1,0:T(8,128)(2,1)}, bf16[1024,4096]{1,0:T(8,128)(2,1)}, bf16[2048,1024]{1,0:T(8,128)(2,1)}) custom-call(s32[768]{0:T(1024)} %gather_fusion, bf16[768,128,128]{2,1,0:T(8,128)(2,1)} %bitcast.81), custom_call_target="tpu_custom_call" | custom-call | tf_op jit(solution)/shard_map/assemble/pallas_call | solution.py:646
  197.8 4.6 fusion.53.proj_x.proj_bc.z.refs_0_.refs_1_.refs_2_.refs_3_.refs_4_.refs_5_
  214.5 8.2 %mix_first.1 = (bf16[512,1792]{1,0:T(8,128)(2,1)}, f32[2,512,128]{2,1,0:T(8,128)}, f32[128,512]{1,0:T(8,128)}, bf16[128,1536]{1,0:T(8,128)(2,1)}, f32[8,128]{1,0:T(8,128)}) custom-call(f32[512,4096]{1,0:T(8,128)} %copy-done.2, f32[512,4096]{1,0:T(8,128)} %copy-done.2, bf16[8,1792]{1,0:T(8,128)(2,1)} %copy-done.31, f32[8,1792]{1,0:T(8,128)} %maximum_maximum_fusion.taps, ...), custom_call_target="tpu_custom_call" | custom-call | tf_op jit(solution)/shard_map/mix_first/pallas_call | solution.py:846
  226.8 10.9 %attend.1 = (bf16[512,512]{1,0:T(8,128)(2,1)}, f32[4,8,512]{2,1,0:T(8,128)}) custom-call(bf16[512,512]{1,0:T(8,128)(2,1)} %get-tuple-element.52.q, bf16[1024,256]{1,0:T(8,128)(2,1)} %copy-done.14, f32[2,8,768]{2,1,0:T(8,128)} %broadcast_in_dim.35.key_labels, f32[512,128]{1,0:T(8,128)} %pad.22.marks), custom_call_target="tpu_custom_call" | custom-call | tf_op jit(solution)/shard_map/attend/pallas_call | solution.py:1280
  243.8 16.8 %mix_second.1 = (f32[512,1536]{1,0:T(8,128)}, bf16[512,1536]{1,0:T(8,128)(2,1)}, f32[3,128,1536]{2,1,0:T(8,128)}) custom-call(bf16[512,1792]{1,0:T(8,128)(2,1)} %get-tuple-element.46.x.b.c, bf16[512,1792]{1,0:T(8,128)(2,1)} %get-tuple-element.46.x.b.c, bf16[512,1792]{1,0:T(8,128)(2,1)} %get-tuple-element.46.x.b.c, f32[512,4096]{1,0:T(8,128)} %copy-done.2, ...), custom_call_target="tpu_custom_call" | custom-call | tf_op jit(solution)/shard_map/mix_second/pallas_call | solution.py:941
  260.6 5.1 multiply_reduce_fusion.2
  266.1 6.7 fusion.54
  272.8 8.0 %multiply_convert_fusion.1 = (bf16[512,2048]{1,0:T(8,128)(2,1)S(1)}, bf16[512,2048]{1,0:T(8,128)(2,1)S(1)}, bf16[512,2048]{1,0:T(8,128)(2,1)}) fusion(f32[512,4096]{1,0:T(8,128)} %fusion.54, bf16[2048,1024]{1,0:T(8,128)(2,1)S(1)} %copy-done.37, bf16[256,1024]{1,0:T(8,128)(2,1)S(1)} %get-tuple-element.98, bf16[256,1024]{1,0:T(8,128)(2,1)S(1)} %get-tuple-element.97), kind=kOutput, calls=%fused_computation.7 | convolution fusion | flops 2165309440 | bytes 19922944 | tf_op jit(solution)/shard_map/dot_general | solution.py:86
  280.8 7.4 %multiply_reduce_fusion = (f32[1024]{0:T(1024)S(1)}, f32[512]{0:T(512)S(1)}, f32[512,1024]{1,0:T(8,128)S(1)}) fusion(f32[512,1024]{1,0:T(8,128)S(1)} %get-tuple-element.131, f32[512]{0:T(512)S(1)} %add_rsqrt_fusion, f32[1024]{0:T(1024)S(1)} %get-tuple-element.109, bf16[1024,4096]{1,0:T(8,128)(2,1)} %get-tuple-element.55, ...), kind=kOutput, calls=%fused_computation.29 | convolution fusion | flops 4306500096 | bytes 16789504 | tf_op jit(solution)/shard_map/dot_general | solution.py:86
  294.9 4.4 fusion.55.grad.given
  299.3 7.6 %gate_back.1 = (bf16[512,1536]{1,0:T(8,128)(2,1)}, bf16[512,1536]{1,0:T(8,128)(2,1)}, f32[8,1536]{1,0:T(8,128)}, f32[128,1536]{1,0:T(8,128)}) custom-call(f32[512,2048]{1,0:T(8,128)} %fusion.55.grad.given, f32[512,1536]{1,0:T(8,128)} %get-tuple-element.57.y, f32[512,4096]{1,0:T(8,128)} %copy-done.2, f32[8,1536]{1,0:T(8,128)} %concatenate.55.gain, ...), custom_call_target="tpu_custom_call" | custom-call | tf_op jit(solution)/shard_map/gate_back/pallas_call | solution.py:1009
  308.1 5.3 collective-permute-start.9
  314.5 17.4 %attend_back.1 = (bf16[512,512]{1,0:T(8,128)(2,1)}, bf16[1024,256]{1,0:T(8,128)(2,1)}) custom-call(bf16[512,512]{1,0:T(8,128)(2,1)} %get-tuple-element.52.q, bf16[1024,256]{1,0:T(8,128)(2,1)} %copy-done.14, f32[512,2048]{1,0:T(8,128)} %fusion.55.grad.given, f32[2,768,8]{2,1,0:T(8,128)} %broadcast_in_dim.36.key_marks, ...), custom_call_target="tpu_custom_call" | custom-call | tf_op jit(solution)/shard_map/attend_back/pallas_call | solution.py:1339
  334.2 5.8 add_convert_fusion
  352.8 29.9 %mix_back.1 = (bf16[512,1792]{1,0:T(8,128)(2,1)}, f32[16,1792]{1,0:T(8,128)}, f32[8,1792]{1,0:T(8,128)}, bf16[512,128]{1,0:T(8,128)(2,1)}, f32[8,128]{1,0:T(8,128)}) custom-call(bf16[512,1792]{1,0:T(8,128)(2,1)} %get-tuple-element.46.x.b.c, bf16[512,1792]{1,0:T(8,128)(2,1)} %get-tuple-element.46.x.b.c, bf16[512,1792]{1,0:T(8,128)(2,1)} %get-tuple-element.46.x.b.c, ...), custom_call_target="tpu_custom_call" | custom-call | tf_op jit(solution)/shard_map/mix_back/pallas_call | solution.py:1159
  391.1 4.1 pad_maximum_fusion.1.g_in
  396.4 9.0 %fusion.12 = (f32[1024]{0:T(1024)S(1)}, f32[512]{0:T(512)S(1)}, f32[512,1024]{1,0:T(8,128)S(1)}) fusion(f32[512]{0:T(512)S(1)} %add_rsqrt_fusion.1, f32[512,1024]{1,0:T(8,128)S(1)} %copy-done.9, bf16[256,1024]{1,0:T(8,128)(2,1)S(1)} %copy-done.5, bf16[256,1024]{1,0:T(8,128)(2,1)S(1)} %copy-done.7, f32[1024]{0:T(1024)S(1)} %get-tuple-element.110, ...), kind=kOutput, calls=%fused_computation.26 | convolution fusion | flops 4317510144 | bytes 17838080 | tf_op jit(solution)/shard_map/dot_general | solution.py:86
  409.4 75.2 %slot_grads.1 = bf16[768,128,128]{2,1,0:T(8,128)(2,1)} custom-call(s32[768]{0:T(1024)} %broadcast_select_fusion.1.left_at, s32[768]{0:T(1024)} %get-tuple-element.86.right_at, bf16[512,1024]{1,0:T(8,128)(2,1)} %copy-done.3, bf16[512,1024]{1,0:T(8,128)(2,1)} %copy-done.13, bf16[512,2048]{1,0:T(8,128)(2,1)} %get-tuple-element.92.downs, ...), custom_call_target="tpu_custom_call" | custom-call | tf_op jit(solution)/shard_map/slot_grads/pallas_call | solution.py:720
  485.3 159.0 %reduce_blocks.1 = (bf16[96,128,128]{2,1,0:T(8,128)(2,1)}, f32[296,128]{1,0:T(8,128)}) custom-call(bf16[8,96,128,128]{3,2,1,0:T(8,128)(2,1)} %bitcast.82, f32[296,128]{1,0:T(8,128)} %bitcast.85), custom_call_target="tpu_custom_call" | custom-call | tf_op jit(solution)/shard_map/reduce_blocks/pallas_call | solution.py:575
  646.1 27.5 %shampoo.1 = (f32[96,128,128]{2,1,0:T(8,128)}, f32[96,128,128]{2,1,0:T(8,128)}, f32[96,128,128]{2,1,0:T(8,128)}, f32[96,128,128]{2,1,0:T(8,128)}, bf16[96,128,128]{2,1,0:T(8,128)(2,1)}) custom-call(bf16[96,128,128]{2,1,0:T(8,128)(2,1)} %get-tuple-element.71.total, f32[96,128,128]{2,1,0:T(8,128)} %master.1, f32[96,128,128]{2,1,0:T(8,128)} %left.1, ...), custom_call_target="tpu_custom_call" | custom-call | tf_op jit(solution)/shard_map/shampoo/pallas_call | solution.py:758
  (210 shorter events, 99.6 us)
Async XLA Ops:
  0.7 31.7 %copy-start.33 = (s32[768]{0:T(1024)S(1)}, s32[768]{0:T(1024)}, u32[]{:S(2)}) copy-start(s32[768]{0:T(1024)} %param.22) | copy-start | bytes 9220
  0.7 31.7 %copy-start.34 = (s32[768]{0:T(1024)S(1)}, s32[768]{0:T(1024)}, u32[]{:S(2)}) copy-start(s32[768]{0:T(1024)} %constant.236) | copy-start | bytes 9220
  3.0 190.9 %collective-permute-start = (bf16[256,1024]{1,0:T(8,128)(2,1)}, bf16[256,1024]{1,0:T(8,128)(2,1)S(1)}, u32[]{:S(2)}, u32[]{:S(2)}) collective-permute-start(bf16[256,1024]{1,0:T(8,128)(2,1)} %get-tuple-element.108), channel_id=1, source_target_pairs={{0,0},{1,2},{2,1},{3,3},{4,4},{5,6},{6,5},{7,7},{8,8},{9,10},{10,9... | collective-permute-start | bytes 1572872 | tf_op jit(solution)/shard_map/ppermute | solution.py:1378
  6.8 187.2 %collective-permute-start.1 = (bf16[256,1024]{1,0:T(8,128)(2,1)}, bf16[256,1024]{1,0:T(8,128)(2,1)S(1)}, u32[]{:S(2)}, u32[]{:S(2)}) collective-permute-start(bf16[256,1024]{1,0:T(8,128)(2,1)} %get-tuple-element.107), channel_id=1, source_target_pairs={{0,2},{1,0},{2,3},{3,1},{4,6},{5,4},{6,7},{7,5},{8,10},{9,8},{10,1... | collective-permute-start | bytes 1572872 | tf_op jit(solution)/shard_map/ppermute | solution.py:1378
  7.8 186.1 %collective-permute-start.7 = (bf16[256,1024]{1,0:T(8,128)(2,1)}, bf16[256,1024]{1,0:T(8,128)(2,1)S(1)}, u32[]{:S(2)}, u32[]{:S(2)}) collective-permute-start(bf16[256,1024]{1,0:T(8,128)(2,1)} %get-tuple-element.100), channel_id=1, source_target_pairs={{0,0},{1,2},{2,1},{3,3},{4,4},{5,6},{6,5},{7,7},{8,8},{9,10},{10,9... | collective-permute-start | bytes 1572872 | tf_op jit(solution)/shard_map/ppermute | solution.py:1378
  9.8 184.2 %collective-permute-start.8 = (bf16[256,1024]{1,0:T(8,128)(2,1)}, bf16[256,1024]{1,0:T(8,128)(2,1)S(1)}, u32[]{:S(2)}, u32[]{:S(2)}) collective-permute-start(bf16[256,1024]{1,0:T(8,128)(2,1)} %get-tuple-element.99), channel_id=1, source_target_pairs={{0,2},{1,0},{2,3},{3,1},{4,6},{5,4},{6,7},{7,5},{8,10},{9,8},{10,1... | collective-permute-start | bytes 1572872 | tf_op jit(solution)/shard_map/ppermute | solution.py:1378
  41.0 117.0 %slice-start = ((f32[37192]{0:T(1024)}), f32[1536]{0:T(1024)S(1)}, s32[]{:S(2)}) async-start(f32[37192]{0:T(1024)} %param.27), calls=%async_computation | async-start | bytes 16384 | tf_op jit(solution)/shard_map/slice | solution.py:76
  197.2 63.4 %copy-start.4 = (bf16[256,1024]{1,0:T(8,128)(2,1)}, bf16[256,1024]{1,0:T(8,128)(2,1)S(1)}, u32[]{:S(2)}) copy-start(bf16[256,1024]{1,0:T(8,128)(2,1)S(1)} %get-tuple-element.136) | copy-start | bytes 1572868
  197.2 63.4 %copy-start.6 = (bf16[256,1024]{1,0:T(8,128)(2,1)}, bf16[256,1024]{1,0:T(8,128)(2,1)S(1)}, u32[]{:S(2)}) copy-start(bf16[256,1024]{1,0:T(8,128)(2,1)S(1)} %get-tuple-element.137) | copy-start | bytes 1572868
  197.2 75.6 %copy-start.10 = (bf16[256,1024]{1,0:T(8,128)(2,1)}, bf16[256,1024]{1,0:T(8,128)(2,1)S(1)}, u32[]{:S(2)}) copy-start(bf16[256,1024]{1,0:T(8,128)(2,1)S(1)} %get-tuple-element.98) | copy-start | bytes 1572868
  197.8 187.6 %copy-start.3 = (bf16[512,1024]{1,0:T(8,128)(2,1)}, bf16[512,1024]{1,0:T(8,128)(2,1)S(1)}, u32[]{:S(2)}) copy-start(bf16[512,1024]{1,0:T(8,128)(2,1)S(1)} %fusion.6.ins) | copy-start | bytes 3145732
  205.7 8.2 %collective-permute-start.2 = (bf16[8,1792]{1,0:T(8,128)(2,1)S(1)}, bf16[8,1792]{1,0:T(8,128)(2,1)S(1)}, u32[]{:S(2)}, u32[]{:S(2)}) collective-permute-start(bf16[8,1792]{1,0:T(8,128)(2,1)S(1)} %slice.216), channel_id=1, source_target_pairs={{0,1},{2,3},{4,5},{6,7},{8,9},{10,11},{12,13},{14,15},{16,17},{18,... | collective-permute-start | bytes 86024 | tf_op jit(solution)/shard_map/ppermute | solution.py:1402
  210.0 14.1 %collective-permute-start.4 = (bf16[512,256]{1,0:T(8,128)(2,1)}, bf16[512,256]{1,0:T(8,128)(2,1)}, u32[]{:S(2)}, u32[]{:S(2)}) collective-permute-start(bf16[512,256]{1,0:T(8,128)(2,1)} %get-tuple-element.53), channel_id=1, source_target_pairs={{0,1},{2,3},{4,5},{6,7},{8,9},{10,11},{12,13},{14,15},{16,17},{18,... | collective-permute-start | bytes 786440 | tf_op jit(solution)/shard_map/ppermute | solution.py:1402
  222.8 18.4 %collective-permute-start.3 = (bf16[128,1536]{1,0:T(8,128)(2,1)}, bf16[128,1536]{1,0:T(8,128)(2,1)}, u32[]{:S(2)}, u32[]{:S(2)}) collective-permute-start(bf16[128,1536]{1,0:T(8,128)(2,1)} %get-tuple-element.49), channel_id=1, source_target_pairs={{0,1},{2,3},{4,5},{6,7},{8,9},{10,11},{12,13},{14,15},{16,17},{18,... | collective-permute-start | bytes 1179656 | tf_op jit(solution)/shard_map/ppermute | solution.py:1402
  308.1 42.7 %collective-permute-start.9 = (bf16[128,1536]{1,0:T(8,128)(2,1)S(1)}, bf16[128,1536]{1,0:T(8,128)(2,1)}, u32[]{:S(2)}, u32[]{:S(2)}) collective-permute-start(bf16[128,1536]{1,0:T(8,128)(2,1)S(1)} %convert_element_type.115), channel_id=1, source_target_pairs={{1,0},{3,2},{5,4},{7,6},{9,8},{11,10},{13,12},{15,14},{17,16},{19,... | collective-permute-start | bytes 1179656 | tf_op jit(solution)/shard_map/ppermute | solution.py:1402
  332.9 14.9 %collective-permute-start.11 = (bf16[512,256]{1,0:T(8,128)(2,1)S(1)}, bf16[512,256]{1,0:T(8,128)(2,1)S(1)}, u32[]{:S(2)}, u32[]{:S(2)}) collective-permute-start(bf16[512,256]{1,0:T(8,128)(2,1)S(1)} %slice.142), channel_id=1, source_target_pairs={{1,0},{3,2},{5,4},{7,6},{9,8},{11,10},{13,12},{15,14},{17,16},{19,... | collective-permute-start | bytes 786440 | tf_op jit(solution)/shard_map/ppermute | solution.py:1402
  341.1 332.5 %collective-permute-start.5 = (bf16[256,1024]{1,0:T(8,128)(2,1)}, bf16[256,1024]{1,0:T(8,128)(2,1)}, u32[]{:S(2)}, u32[]{:S(2)}) collective-permute-start(bf16[256,1024]{1,0:T(8,128)(2,1)} %get-tuple-element.104), channel_id=1, source_target_pairs={{0,0},{2,1},{1,2},{3,3},{4,4},{6,5},{5,6},{7,7},{8,8},{10,9},{9,10... | collective-permute-start | bytes 1572872 | tf_op jit(solution)/shard_map/ppermute | solution.py:1393
  343.2 330.4 %collective-permute-start.6 = (bf16[256,1024]{1,0:T(8,128)(2,1)}, bf16[256,1024]{1,0:T(8,128)(2,1)}, u32[]{:S(2)}, u32[]{:S(2)}) collective-permute-start(bf16[256,1024]{1,0:T(8,128)(2,1)} %get-tuple-element.103), channel_id=1, source_target_pairs={{2,0},{0,1},{3,2},{1,3},{6,4},{4,5},{7,6},{5,7},{10,8},{8,9},{11,1... | collective-permute-start | bytes 1572872 | tf_op jit(solution)/shard_map/ppermute | solution.py:1393
  386.7 3.8 collective-permute-start.10
  407.1 269.2 %collective-permute-start.12 = (bf16[256,1024]{1,0:T(8,128)(2,1)}, bf16[256,1024]{1,0:T(8,128)(2,1)S(1)}, u32[]{:S(2)}, u32[]{:S(2)}) collective-permute-start(bf16[256,1024]{1,0:T(8,128)(2,1)} %get-tuple-element.96), channel_id=1, source_target_pairs={{0,0},{2,1},{1,2},{3,3},{4,4},{6,5},{5,6},{7,7},{8,8},{10,9},{9,10... | collective-permute-start | bytes 1572872 | tf_op jit(solution)/shard_map/ppermute | solution.py:1393
  409.0 267.3 %collective-permute-start.13 = (bf16[256,1024]{1,0:T(8,128)(2,1)}, bf16[256,1024]{1,0:T(8,128)(2,1)}, u32[]{:S(2)}, u32[]{:S(2)}) collective-permute-start(bf16[256,1024]{1,0:T(8,128)(2,1)} %get-tuple-element.95), channel_id=1, source_target_pairs={{2,0},{0,1},{3,2},{1,3},{6,4},{4,5},{7,6},{5,7},{10,8},{8,9},{11,1... | collective-permute-start | bytes 1572872 | tf_op jit(solution)/shard_map/ppermute | solution.py:1393
  485.3 159.0 %copy-start.26 = (f32[37192]{0:T(1024)S(1)}, f32[37192]{0:T(1024)}, u32[]{:S(2)}) copy-start(f32[37192]{0:T(1024)} %param.27) | copy-start | bytes 446308
  485.3 159.0 %copy-start.28 = (f32[37192]{0:T(1024)S(1)}, f32[37192]{0:T(1024)}, u32[]{:S(2)}) copy-start(f32[37192]{0:T(1024)} %param.28) | copy-start | bytes 446308
  485.3 159.0 %copy-start.29 = (f32[37192]{0:T(1024)S(1)}, f32[37192]{0:T(1024)}, u32[]{:S(2)}) copy-start(f32[37192]{0:T(1024)} %param.29) | copy-start | bytes 446308
  (31 other events, 155.6 us)
where the time goes:
time: 686 us; the launch traced here: 679 us
  Pallas kernels  490 us (71%)
  matrix products  59.5 us (9%)
  local copies, waits for them, and re-layouts  40.9 us (6%)
  other arithmetic  38 us (6%)
  starting transfers between devices  26.3 us (4%)
  blocking collectives  21.6 us (3%)
    pallas_call x1, Pallas kernels, reduce_blocks(): pl.pallas_call(functools.partial(reduce_kernel, grid, slots), out_shape=(...  159 us
    pallas_call x1, Pallas kernels, gather_blocks(): pl.pallas_call(functools.partial(gather_kernel, grid, slots), out_shape=j...  114 us
    pallas_call x1, Pallas kernels, slot_grads(): pl.pallas_call(slot_grads_kernel, out_shape=jax.ShapeDtypeStruct((count,...  75.2 us
    dot_general x5, matrix products, dot_nt(): lax.dot_general(left, right, (((1,), (1,)), ((), ())), preferred_element_...  31.4 us
    pallas_call x1, Pallas kernels, mix_back(): pl.pallas_call(mix_back_kernel, out_shape=(jax.ShapeDtypeStruct((tokens,...  29.9 us
    pallas_call x1, Pallas kernels, shampoo(): pl.pallas_call(functools.partial(shampoo_kernel, norm), out_shape=(full,...  27.5 us
    dot_general x6, matrix products, dot(): return jnp.dot(left, right, preferred_element_type=F32, precision=precision)  26.8 us
    all_gather x1, blocking collectives, shards(): labels_all = lax.all_gather(doc_ids, 'seq', axis=1, tiled=True)  21.6 us
  transfers between devices with their start and end apart: 14, of which 0 were waited for; matrix products, arithmetic and copies ran while one was open for 11% of the time, Pallas kernels for 69%

commit v1 on v0

--- a/solution.py
+++ b/solution.py
@@ -130,7 +130,8 @@
     return dp % wide, seq // CORES, dp // wide, seq % CORES
 
 
-def gather_kernel(grid, slots, src, out, kept, sem_own, sz, rz, sx, rx, sy, ry, sc, rc):
+def gather_kernel(grid, slots, master, tokens, cotangent, docs, out, rows, given, labels, wide_own, src, bounce,
+                  sem_own, sem_load, sz, rz, sx, rx, sy, ry, sc, rc, s_rows, r_rows, s_docs, r_docs):
     wide, tall, deep = grid
     x, y, z, c = place(grid)
     half, lone, bulk = parts_of(slots, tall)
@@ -142,6 +143,15 @@
     other_at = base + (1 - y) * bulk if lone else base
     mate = y * CORES + (1 - c)
     over = (tall - 1 - y) * CORES + c
+    peers = tall * CORES
+    micro = tokens.shape[0]
+    each = peers // micro
+
+    loads = []
+    for k in range(CORES):
+        part = pl.ds(((c + k) % CORES) * half, half)
+        loads.append((part, pltpu.make_async_copy(master.at[part], wide_own.at[part], sem_load.at[k])))
+        loads[-1][1].start()
 
     barrier = pltpu.get_barrier_semaphore()
     count = jnp.int32(0)
@@ -155,15 +165,9 @@
                 pl.semaphore_signal(barrier, inc=1, device_id=(there, seq), device_id_type=MESH)
 
             count = count + ok.astype(jnp.int32)
-    pl.semaphore_signal(barrier, inc=1, device_id=(me, mate), device_id_type=MESH)
-    count = count + 1
-    if lone:
-        pl.semaphore_signal(barrier, inc=1, device_id=(me, over), device_id_type=MESH)
-        count = count + 1
-    pl.semaphore_wait(barrier, count)
-
-    take = pltpu.make_async_copy(src, kept, sem_own.at[0])
-    take.start()
+    for k in range(1, peers):
+        pl.semaphore_signal(barrier, inc=1, device_id=(me, (seq + k) % peers), device_id_type=MESH)
+    pl.semaphore_wait(barrier, count + (peers - 1))
     sent = []
 
     def send(ok, source, target, send_sem, recv_sem, device):
@@ -189,6 +193,39 @@
             copy.wait_recv()
 
     yes = jnp.bool_(True)
+
+    at_home = []
+    for t in range(micro):
+        m = (seq + t) % micro
+        there = m * each + seq // micro
+        for k, (source, target) in enumerate(((tokens, rows), (cotangent, given))):
+            place_to = target.at[seq % micro]
+            send(there != seq, source.at[m], place_to, s_rows.at[k, t], r_rows.at[k, seq % micro], (me, there))
+            take = pltpu.make_async_copy(source.at[m], bounce.at[k], sem_own.at[k])
+            put = pltpu.make_async_copy(bounce.at[k], place_to, sem_own.at[k])
+            at_home.append((there == seq, take, put))
+
+            @pl.when(there == seq)
+            def _(take=take):
+                take.start()
+
+    labels[seq] = docs[...]
+    for k in range(1, peers):
+        there = (seq + k) % peers
+        send(yes, docs, labels.at[seq], s_docs.at[k], r_docs.at[seq], (me, there))
+
+    def convert(k):
+        part, copy = loads[k]
+        copy.wait()
+        base_at = ((c + k) % CORES) * half
+
+        def one(i, _):
+            src[base_at + i] = wide_own[base_at + i].astype(src.dtype)
+            return 0
+
+        lax.fori_loop(0, half, one, 0, unroll=2)
+
+    convert(0)
 
     def piece(shard, at, size):
         return out.at[shard, pl.ds(at, size)]
@@ -250,9 +287,14 @@
                 pass_on(ok, shard)
         if s == 0:
             along_x(yes, z, both, 0, True)
-            take.wait()
-            put = pltpu.make_async_copy(kept, out.at[me], sem_own.at[1])
-            put.start()
+            convert(1)
+            keep = pltpu.make_async_copy(src, out.at[me], sem_load.at[0])
+            keep.start()
+            for ok, take, put in at_home:
+                @pl.when(ok)
+                def _(take=take, put=put):
+                    take.wait()
+                    put.start()
         else:
             for hop in range(1, wide):
                 x_in(s - 1, hop)
@@ -262,7 +304,18 @@
         x_in(deep - 1, hop)
     for s in range(max(deep - 2, 0), deep):
         y_all(s)
-    put.wait()
+    keep.wait()
+    for ok, take, put in at_home:
+        @pl.when(ok)
+        def _(put=put):
+            put.wait()
+    for q in range(micro):
+        source = seq % each * micro + q
+        for k, target in enumerate((rows, given)):
+            arrived(source != seq, target.at[q], r_rows.at[k, q])
+    for k in range(1, peers):
+        source = (seq + k) % peers
+        arrived(yes, labels.at[source], r_docs.at[source])
 
     mate_base = (1 - c) * half
     mate_bulk = mate_base + y * (half - bulk)
@@ -282,27 +335,37 @@
             copy.wait_send()
 
 
-def gather_blocks(grid, own):
+def gather_blocks(grid, master, tokens, cotangent, docs):
     wide, tall, deep = grid
-    slots = own.shape[0]
+    slots = master.shape[0]
     n = wide * deep
+    peers = tall * CORES
+    micro = tokens.shape[0]
+    low = tokens.dtype
     sem = pltpu.SemaphoreType.DMA
+    hbm = pl.BlockSpec(memory_space=pl.ANY)
+    vmem = pl.BlockSpec(memory_space=pltpu.VMEM)
     return pl.pallas_call(
         functools.partial(gather_kernel, grid, slots),
-        out_shape=jax.ShapeDtypeStruct((n,) + own.shape, own.dtype),
-        in_specs=[pl.BlockSpec(memory_space=pl.ANY)],
-        out_specs=pl.BlockSpec(memory_space=pl.ANY),
+        out_shape=(
+            jax.ShapeDtypeStruct((n,) + master.shape, low),
+            jax.ShapeDtypeStruct(tokens.shape, low), jax.ShapeDtypeStruct(tokens.shape, low),
+            jax.ShapeDtypeStruct((peers,) + docs.shape, docs.dtype),
+        ),
+        in_specs=[hbm, hbm, hbm, vmem],
+        out_specs=(hbm, hbm, hbm, vmem),
         scratch_shapes=[
-            pltpu.VMEM(own.shape, own.dtype),
-            sem((2,)),
+            pltpu.VMEM(master.shape, master.dtype), pltpu.VMEM(master.shape, low), pltpu.VMEM((2,) + tokens.shape[1:], low),
+            sem((2,)), sem((CORES,)),
             sem((2, deep)), sem((2, deep + 1)),
             sem((2, wide, deep)), sem((2, wide + 1, deep)),
             sem((n,)), sem((n,)),
             sem((2, n)), sem((2, n)),
+            sem((2, micro)), sem((2, micro)), sem((peers,)), sem((peers,)),
         ],
-        compiler_params=pltpu.CompilerParams(collective_id=0, has_side_effects=True),
+        compiler_params=pltpu.CompilerParams(collective_id=0, has_side_effects=True, vmem_limit_bytes=32 << 20),
         name="gather_blocks",
-    )(own)
+    )(master, tokens, cotangent, docs)
 
 def far_first(at, size, i):
     above, below = size - 1 - at, at
@@ -639,8 +702,12 @@
         put(step).wait()
 
 
-def assemble(blocks, inverse):
-    table = jnp.take(inverse, jnp.array(sum(all_orders(), []), jnp.int32))
+def slots_in_order(block_of_slot, order):
+    match = jnp.array(order, jnp.int32)[:, None] == block_of_slot[None, :]
+    return jnp.sum(jnp.where(match, jnp.arange(block_of_slot.shape[0], dtype=jnp.int32)[None, :], 0), axis=1)
+
+
+def assemble(blocks, table):
     shapes = [(D, sum(SHAPES[m][1] for m in WIDE_IN)), (sum(SHAPES[m][0] for m in TALL_OUT), D), (D, 2 * FF), (FF, D)]
     hbm = pl.BlockSpec(memory_space=pl.ANY)
     return pl.pallas_call(
@@ -659,79 +726,91 @@
     )(table, blocks)
 
 
-GROUP = 32
-
-
-def slot_grads_kernel(left_at, right_at, ins, mids, downs, outs, g_in, g_hidden, g_ff, cot, out, left, right):
-    at = 0
-
-    @pl.when(pl.program_id(0) == 0)
-    def _():
-        at = 0
-        for ref in (ins, outs, mids, downs):
-            for q in range(ref.shape[1] // BS):
-                left[at : at + BS, :] = ref[:, q * BS : (q + 1) * BS].T
-                at += BS
-        at = 0
-        for ref in (g_in, g_hidden, g_ff, cot):
-            cols = ref.shape[1]
-            right[:, at : at + cols] = ref[...]
-            at += cols
-
-    base = pl.program_id(0) * GROUP
-
-    def one(i, _):
-        rows = pl.ds(pl.multiple_of(left_at[base + i] * BS, BS), BS)
-        cols = pl.ds(pl.multiple_of(right_at[base + i] * BS, BS), BS)
-        out[i] = dot(left[rows, :], right[:, cols]).astype(BF16)
-        return 0
-
-    lax.fori_loop(0, GROUP, one, 0, unroll=4)
-
-
-def grad_tables():
-    lefts, rights = [], []
-    left_base = {0: 0, 1: D, 2: D + INNER + QDIM, 3: 2 * D + INNER + QDIM}
-    right_base = {0: 0, 1: 2 * INNER + 2 * NSTATE + QDIM + 2 * KDIM}
-    right_base[2] = right_base[1] + D
-    right_base[3] = right_base[2] + 2 * FF
-    for kind, members in enumerate((WIDE_IN, TALL_OUT, WIDE_FF, TALL_FF)):
-        row_at, col_at = left_base[kind] // BS, right_base[kind] // BS
-        for m in members:
-            rows, cols = SHAPES[m][0] // BS, SHAPES[m][1] // BS
-            for r in range(rows):
-                for q in range(cols):
-                    lefts.append(row_at + r)
-                    rights.append(col_at + q)
-            if kind in (0, 2):
-                col_at += cols
-            else:
-                row_at += rows
-    return lefts, rights
-
-
-def slot_grads(block_of_slot, ins, mids, downs, outs, g_in, g_hidden, g_ff, cot):
-    lefts, rights = grad_tables()
-    left_at = jnp.take(jnp.array(lefts, jnp.int32), block_of_slot)
-    right_at = jnp.take(jnp.array(rights, jnp.int32), block_of_slot)
-    count = block_of_slot.shape[0]
-    arrays = (ins, mids, downs, outs, g_in, g_hidden, g_ff, cot)
-    tokens = ins.shape[0]
+UNIT_ROWS = 256
+UNIT_COLS = 1024
+STAGES = 3
+
+
+def slot_grads_kernel(sizes, slot_of, *refs):
+    count = sum(len(left) + len(right) for left, right in sizes)
+    arrays, (out, left, right, turned, stage, s_in, s_out) = refs[:count], refs[count:]
+    units = []
+    groups, k, left_at, right_at, first = [], 0, 0, 0, 0
+    for lefts, rights in sizes:
+        copies, at = [], left_at
+        for width in lefts:
+            copies.append(pltpu.make_async_copy(arrays[k], left.at[:, pl.ds(at, width)], s_in.at[k]))
+            at, k = at + width, k + 1
+        rows, at = at - left_at, right_at
+        for width in rights:
+            copies.append(pltpu.make_async_copy(arrays[k], right.at[:, pl.ds(at, width)], s_in.at[k]))
+            at, k = at + width, k + 1
+        cols = at - right_at
+        groups.append((copies, left_at, rows, right_at, cols, first))
+        left_at, right_at = left_at + rows, right_at + cols
+        first += rows // BS * (cols // BS)
+    for copies, *_ in groups:
+        for copy in copies:
+            copy.start()
+
+    def drain(slot):
+        pltpu.make_async_copy(out.at[pl.ds(0, UNIT_ROWS // BS * (UNIT_COLS // BS))], out.at[pl.ds(0, UNIT_ROWS // BS * (UNIT_COLS // BS))],
+                              s_out.at[slot]).wait()
+
+    done = 0
+    for copies, left_at, rows, right_at, cols, first in groups:
+        for copy in copies:
+            copy.wait()
+        across = cols // UNIT_COLS
+
+        def one(u, _, left_at=left_at, right_at=right_at, cols=cols, first=first, across=across, done=done):
+            r, q = u // across, u % across
+            slot = (done + u) % STAGES
+
+            @pl.when(q == 0)
+            def _():
+                turned[...] = left[:, pl.ds(pl.multiple_of(left_at + r * UNIT_ROWS, BS), UNIT_ROWS)].T
+
+            @pl.when(done + u >= STAGES)
+            def _():
+                drain(slot)
+
+            column = pl.multiple_of(right_at + q * UNIT_COLS, BS)
+            stage[slot] = dot(turned[...], right[:, pl.ds(column, UNIT_COLS)]).astype(BF16)
+            for i in range(UNIT_ROWS // BS):
+                for p in range(UNIT_COLS // BS):
+                    block = first + (r * (UNIT_ROWS // BS) + i) * (cols // BS) + q * (UNIT_COLS // BS) + p
+                    pltpu.make_async_copy(stage.at[slot, pl.ds(i * BS, BS), pl.ds(p * BS, BS)], out.at[slot_of[block]], s_out.at[slot]).start()
+            return 0
+
+        total = rows // UNIT_ROWS * across
+        lax.fori_loop(0, total, one, 0)
+        done += total
+    for u in range(max(done - STAGES, 0), done):
+        drain(u % STAGES)
+
+
+def slot_grads(slot_of, groups):
+    arrays = [a for lefts, rights in groups for a in lefts + rights]
+    sizes = [([a.shape[1] for a in lefts], [a.shape[1] for a in rights]) for lefts, rights in groups]
+    tokens = arrays[0].shape[0]
+    hbm = pl.BlockSpec(memory_space=pl.ANY)
     return pl.pallas_call(
-        slot_grads_kernel,
-        out_shape=jax.ShapeDtypeStruct((count, BS, BS), BF16),
+        functools.partial(slot_grads_kernel, sizes),
+        out_shape=jax.ShapeDtypeStruct((slot_of.shape[0], BS, BS), BF16),
         grid_spec=pltpu.PrefetchScalarGridSpec(
-            num_scalar_prefetch=2, grid=(count // GROUP,),
-            in_specs=[pl.BlockSpec(a.shape, lambda *_: (0, 0), pipeline_mode=pl.Buffered(1)) for a in arrays],
-            out_specs=pl.BlockSpec((GROUP, BS, BS), lambda i, *_: (i, 0, 0)),
+            num_scalar_prefetch=1, grid=(1,), in_specs=[hbm] * len(arrays), out_specs=hbm,
             scratch_shapes=[
-                pltpu.VMEM((sum(a.shape[1] for a in arrays[:4]), tokens), BF16),
-                pltpu.VMEM((tokens, sum(a.shape[1] for a in arrays[4:])), BF16),
+                pltpu.VMEM((tokens, sum(sum(left) for left, _ in sizes)), BF16),
+                pltpu.VMEM((tokens, sum(sum(right) for _, right in sizes)), BF16),
+                pltpu.VMEM((UNIT_ROWS, tokens), BF16),
+                pltpu.VMEM((STAGES, UNIT_ROWS, UNIT_COLS), BF16),
+                pltpu.SemaphoreType.DMA((len(arrays),)), pltpu.SemaphoreType.DMA((STAGES,)),
             ],
         ),
         compiler_params=kernel_params(),
         name="slot_grads",
-    )(left_at, right_at, *arrays)
+    )(slot_of, *arrays)
 
 
 SHAMPOO = 8
@@ -1364,23 +1443,6 @@
     )(g_kv, cosine, sine)
 
 
-def spans(seq, micro):
-    return seq // micro, micro
-
-
-def regroup(rows, micro):
-    seq = lax.axis_size("seq")
-    each = seq // micro
-    here = lax.axis_index("seq")
-    pieces = []
-    for t in range(micro):
-        pairs = [(j, ((j + t) % micro) * each + j // micro) for j in range(seq)]
-        pieces.append(lax.ppermute(lax.dynamic_index_in_dim(rows, (here + t) % micro, 0, False), "seq", pairs))
-    order = here // each
-    stacked = jnp.stack(pieces)
-    return jnp.concatenate([lax.dynamic_index_in_dim(stacked, (order - q) % micro, 0, False) for q in range(micro)], axis=0)
-
-
 def ungroup(rows, micro):
     seq = lax.axis_size("seq")
     each = seq // micro
@@ -1418,9 +1480,11 @@
     start = rank * count
     slots = master_blocks.shape[0]
 
-    inverse = jnp.zeros_like(block_of_slot).at[block_of_slot].set(jnp.arange(block_of_slot.shape[0], dtype=jnp.int32), unique_indices=True)
-    gathered = gather_blocks(grid, master_blocks.astype(BF16)).reshape(-1, BS, BS)
-    w_in, w_out, w_ff, w_down = assemble(gathered, inverse)
+    orders = all_orders()
+    table = slots_in_order(block_of_slot, sum(orders, []))
+    gathered, rows, given, labels_all = gather_blocks(grid, master_blocks, tokens, cotangent, doc_ids)
+    w_in, w_out, w_ff, w_down = assemble(gathered.reshape(-1, BS, BS), table)
+    rows, given = rows.reshape(count, D), given.reshape(count, D)
     gain_in, gain_mid, gain_mix, conv_weight, conv_bias, dt_bias, a_log, skip, w_dt = unpack_vectors(vector_params)
     w_dt = jnp.pad(w_dt.reshape(D, HEADS_SSM), ((0, 0), (0, LANES - HEADS_SSM))).astype(BF16)
     taps = pad_rows(conv_weight.reshape(KERNEL, CHANNELS), conv_bias)
@@ -1429,8 +1493,7 @@
     wide_skip = pad_rows(jnp.repeat(skip, HEAD))
     wide_gain = pad_rows(gain_mix)
 
-    labels_all = lax.all_gather(doc_ids, "seq", axis=1, tiled=True)
-    row = lax.dynamic_index_in_dim(labels_all, here // each, 0, False)
+    row = lax.dynamic_index_in_dim(labels_all, here // each, 1, False).reshape(-1)
     before = jnp.concatenate([jnp.full((DOC_MOST,), -1, jnp.int32), row])
     window = lax.dynamic_slice_in_dim(before, start, DOC_MOST + count)
     labels = window[DOC_MOST:]
@@ -1455,8 +1518,6 @@
     cosine = jnp.concatenate([cos] * 4, axis=1)
     sine = jnp.concatenate([-sin, sin] * 2, axis=1)
 
-    rows = regroup(tokens, micro)
-    given = regroup(cotangent, micro)
     inputs = rows.astype(F32)
     normed_in = (inputs * rms_scale(inputs) * gain_in).astype(BF16)
     proj = dot(normed_in, w_in)
@@ -1520,8 +1581,10 @@
     grad_tokens = ungroup((g_values + g_hidden).astype(BF16), micro).astype(F32)
     g_w_dt = dot_tn(normed_in, g_raw)
 
-    flat = slot_grads(block_of_slot, normed_in, normed_mid, mixed, jnp.concatenate([normed_ssm, context], axis=1),
-                      g_in, hidden_low, g_ff, given)
+    flat = slot_grads(table, [
+        ([normed_in], [g_z, g_conv, g_q, g_kv]), ([normed_ssm, context], [hidden_low]),
+        ([normed_mid], [g_ff]), ([mixed], [given]),
+    ])
     parts = [g_gain_in, g_gain_mid, g_gain_mix[0], g_taps[:KERNEL].reshape(-1), g_taps[KERNEL]]
     parts += [g_params[i, :HEADS_SSM] for i in range(3)] + [g_w_dt[:, :HEADS_SSM].reshape(-1)]
     width = vector_params.shape[0]

time: 686 us -> 600 us (0.87)
  Pallas kernels: 490 us -> 444 us
  blocking collectives: 21.6 us -> 0 us
  other arithmetic: 38 us -> 27.6 us
  local copies, waits for them, and re-layouts: 40.9 us -> 30.9 us
    pallas_call x2, Pallas kernels: 190 us -> 144 us  [the longest x1 114 us: gather_blocks(): pl.pallas_call(functools.partial(gather_kernel, grid, slots), out_shape=(...]
    all_gather x1 -> x0, blocking collectives: 21.6 us -> none  [shards(): labels_all = lax.all_gather(doc_ids, 'seq', axis=1, tiled=True)]
    gather x3 -> x0, local copies, waits for them, and re-layouts: 11.3 us -> none  [the longest x1 4.89 us: assemble(): table = jnp.take(inverse, jnp.array(sum(all_orders(), []), jnp.int32))]
  transfers between devices with their start and end apart: 14 -> 10, of which waited for: 0 -> 0; matrix products, arithmetic and copies ran while one was open for 11% -> 10% of each run, Pallas kernels for 69% -> 49%
where the time goes in v1:
time: 600 us; the launch traced here: 588 us
  Pallas kernels  444 us (74%)
  matrix products  61.9 us (10%)
  local copies, waits for them, and re-layouts  30.9 us (5%)
  other arithmetic  27.6 us (5%)
  starting transfers between devices  20.4 us (3%)
    pallas_call x1, Pallas kernels, reduce_blocks(): pl.pallas_call(functools.partial(reduce_kernel, grid, slots), out_shape=(...  158 us
    pallas_call x1, Pallas kernels, gather_blocks(): pl.pallas_call(functools.partial(gather_kernel, grid, slots), out_shape=(...  114 us
    dot_general x5, matrix products, dot_nt(): lax.dot_general(left, right, (((1,), (1,)), ((), ())), preferred_element_...  31.2 us
    pallas_call x1, Pallas kernels, mix_back(): pl.pallas_call(mix_back_kernel, out_shape=(jax.ShapeDtypeStruct((tokens,...  30 us
    pallas_call x1, Pallas kernels, slot_grads(): pl.pallas_call(functools.partial(slot_grads_kernel, sizes), out_shape=jax...  29.5 us
    dot_general x6, matrix products, dot(): return jnp.dot(left, right, preferred_element_type=F32, precision=precision)  28.5 us
    pallas_call x1, Pallas kernels, shampoo(): pl.pallas_call(functools.partial(shampoo_kernel, norm), out_shape=(full,...  27.5 us
    pallas_call x1, Pallas kernels, assemble(): pl.pallas_call(assemble_kernel, out_shape=tuple((jax.ShapeDtypeStruct(sha...  18.3 us
  transfers between devices with their start and end apart: 10, of which 0 were waited for; matrix products, arithmetic and copies ran while one was open for 10% of the time, Pallas kernels for 49%

profile of v1, /device:TPU:11, one launch (start us, length us, event | category | flops | bytes accessed | tf_op | source)
XLA Modules:
  0.0 588.0 jit_solution(13304914874009097961)
XLA Ops:
  6.6 114.5 %gather_blocks.1 = (bf16[8,96,128,128]{3,2,1,0:T(8,128)(2,1)}, bf16[2,256,1024]{2,1,0:T(8,128)(2,1)S(1)}, bf16[2,256,1024]{2,1,0:T(8,128)(2,1)S(1)}, s32[4,2,256]{2,1,0:T(2,128)S(1)}) custom-call(f32[96,128,128]{2,1,0:T(8,128)S(1)} %copy-done, bf16[2,256,1024]{2,1,0:T(8,128)(2,1)S(1)} %copy-done.3, bf16[2,256,1024]{2,1,0:T(8,128)(2,1)S(1)} %copy-done.4, ...), custom_call_target="tpu_custom_call" | custom-call | tf_op jit(solution)/shard_map/gather_blocks/pallas_call | solution.py:348
  122.9 18.3 %assemble.1 = (bf16[1024,4096]{1,0:T(8,128)(2,1)}, bf16[2048,1024]{1,0:T(8,128)(2,1)}, bf16[1024,4096]{1,0:T(8,128)(2,1)}, bf16[2048,1024]{1,0:T(8,128)(2,1)}) custom-call(s32[768]{0:T(1024)} %select_reduce_fusion.table.slot_of, bf16[768,128,128]{2,1,0:T(8,128)(2,1)} %bitcast.99), custom_call_target="tpu_custom_call" | custom-call | tf_op jit(solution)/shard_map/assemble/pallas_call | solution.py:713
  141.2 6.9 %fusion.53.proj_x.proj_bc.z.refs_0_.refs_1_.refs_2_.refs_3_.refs_4_.refs_5_ = f32[512,4096]{1,0:T(8,128)S(1)} fusion(bf16[512,1024]{1,0:T(8,128)(2,1)S(1)} %fusion.14.refs_0_, bf16[1024,4096]{1,0:T(8,128)(2,1)} %get-tuple-element.50), kind=kOutput, calls=%fused_computation.120 | convolution fusion | flops 4294967296 | bytes 17825792 | tf_op jit(solution)/shard_map/dot_general | solution.py:82
  148.1 3.3 copy-done.6
  174.0 8.2 %mix_first.1 = (bf16[512,1792]{1,0:T(8,128)(2,1)}, f32[2,512,128]{2,1,0:T(8,128)}, f32[128,512]{1,0:T(8,128)}, bf16[128,1536]{1,0:T(8,128)(2,1)}, f32[8,128]{1,0:T(8,128)}) custom-call(f32[512,4096]{1,0:T(8,128)} %copy-done.6, f32[512,4096]{1,0:T(8,128)} %copy-done.6, bf16[8,1792]{1,0:T(8,128)(2,1)} %copy-done.23, f32[8,1792]{1,0:T(8,128)} %maximum_maximum_fusion.taps, ...), custom_call_target="tpu_custom_call" | custom-call | tf_op jit(solution)/shard_map/mix_first/pallas_call | solution.py:925
  185.8 11.0 %attend.1 = (bf16[512,512]{1,0:T(8,128)(2,1)}, f32[4,8,512]{2,1,0:T(8,128)}) custom-call(bf16[512,512]{1,0:T(8,128)(2,1)} %get-tuple-element.58.q, bf16[1024,256]{1,0:T(8,128)(2,1)} %copy-done.14, f32[2,8,768]{2,1,0:T(8,128)} %broadcast_in_dim.32.key_labels, f32[512,128]{1,0:T(8,128)} %pad.22.marks), custom_call_target="tpu_custom_call" | custom-call | tf_op jit(solution)/shard_map/attend/pallas_call | solution.py:1359
  196.8 3.4 fusion.27
  201.8 16.8 %mix_second.1 = (f32[512,1536]{1,0:T(8,128)}, bf16[512,1536]{1,0:T(8,128)(2,1)}, f32[3,128,1536]{2,1,0:T(8,128)}) custom-call(bf16[512,1792]{1,0:T(8,128)(2,1)} %get-tuple-element.52.x.b.c, bf16[512,1792]{1,0:T(8,128)(2,1)} %get-tuple-element.52.x.b.c, bf16[512,1792]{1,0:T(8,128)(2,1)} %get-tuple-element.52.x.b.c, f32[512,4096]{1,0:T(8,128)} %copy-done.6, ...), custom_call_target="tpu_custom_call" | custom-call | tf_op jit(solution)/shard_map/mix_second/pallas_call | solution.py:1020
  218.6 5.1 multiply_reduce_fusion.2
  224.1 6.8 %fusion.54 = f32[512,4096]{1,0:T(8,128)} fusion(bf16[512,1024]{1,0:T(8,128)(2,1)S(1)} %multiply_convert_fusion.3.refs_8_, bf16[1024,4096]{1,0:T(8,128)(2,1)S(1)} %bitcast.117), kind=kOutput, calls=%fused_computation.121 | convolution fusion | flops 4294967296 | bytes 17825792 | tf_op jit(solution)/shard_map/dot_general | solution.py:82
  230.9 7.3 %multiply_convert_fusion.1 = (bf16[512,2048]{1,0:T(8,128)(2,1)S(1)}, bf16[512,2048]{1,0:T(8,128)(2,1)S(1)}, bf16[512,2048]{1,0:T(8,128)(2,1)}) fusion(f32[512,4096]{1,0:T(8,128)} %fusion.54, bf16[512,1024]{1,0:T(8,128)(2,1)S(1)} %bitcast.96, bf16[2048,1024]{1,0:T(8,128)(2,1)S(1)} %copy-done.37), kind=kOutput, calls=%fused_computation.10 | convolution fusion | flops 2163212288 | bytes 19922944 | tf_op jit(solution)/shard_map/dot_general | solution.py:86
  238.2 8.0 %multiply_reduce_fusion = (f32[1024]{0:T(1024)}, f32[512]{0:T(512)S(1)}, f32[512,1024]{1,0:T(8,128)S(1)}) fusion(f32[512,1024]{1,0:T(8,128)S(1)} %get-tuple-element.126, f32[512]{0:T(512)S(1)} %add_rsqrt_fusion, f32[1024]{0:T(1024)S(1)} %get-tuple-element.104, bf16[1024,4096]{1,0:T(8,128)(2,1)} %get-tuple-element.61, ...), kind=kOutput, calls=%fused_computation.32 | convolution fusion | flops 4306500096 | bytes 16789504 | tf_op jit(solution)/shard_map/dot_general | solution.py:86
  251.1 4.4 fusion.55.grad.given
  255.4 7.6 %gate_back.1 = (bf16[512,1536]{1,0:T(8,128)(2,1)}, bf16[512,1536]{1,0:T(8,128)(2,1)}, f32[8,1536]{1,0:T(8,128)}, f32[128,1536]{1,0:T(8,128)}) custom-call(f32[512,2048]{1,0:T(8,128)} %fusion.55.grad.given, f32[512,1536]{1,0:T(8,128)} %get-tuple-element.64.y, f32[512,4096]{1,0:T(8,128)} %copy-done.6, f32[8,1536]{1,0:T(8,128)} %concatenate.45.gain, ...), custom_call_target="tpu_custom_call" | custom-call | tf_op jit(solution)/shard_map/gate_back/pallas_call | solution.py:1088
  264.2 4.5 collective-permute-start.5
  269.9 17.5 %attend_back.1 = (bf16[512,512]{1,0:T(8,128)(2,1)}, bf16[1024,256]{1,0:T(8,128)(2,1)}) custom-call(bf16[512,512]{1,0:T(8,128)(2,1)} %get-tuple-element.58.q, bf16[1024,256]{1,0:T(8,128)(2,1)} %copy-done.14, f32[512,2048]{1,0:T(8,128)} %fusion.55.grad.given, f32[2,768,8]{2,1,0:T(8,128)} %broadcast_in_dim.33.key_marks, ...), custom_call_target="tpu_custom_call" | custom-call | tf_op jit(solution)/shard_map/attend_back/pallas_call | solution.py:1418
  289.7 5.2 add_convert_fusion
  298.1 4.4 collective-permute-start.4
  308.2 30.0 %mix_back.1 = (bf16[512,1792]{1,0:T(8,128)(2,1)}, f32[16,1792]{1,0:T(8,128)}, f32[8,1792]{1,0:T(8,128)}, bf16[512,128]{1,0:T(8,128)(2,1)}, f32[8,128]{1,0:T(8,128)}) custom-call(bf16[512,1792]{1,0:T(8,128)(2,1)} %get-tuple-element.52.x.b.c, bf16[512,1792]{1,0:T(8,128)(2,1)} %get-tuple-element.52.x.b.c, bf16[512,1792]{1,0:T(8,128)(2,1)} %get-tuple-element.52.x.b.c, ...), custom_call_target="tpu_custom_call" | custom-call | tf_op jit(solution)/shard_map/mix_back/pallas_call | solution.py:1238
  346.7 10.2 %fusion.20 = (f32[1024]{0:T(1024)S(1)}, f32[512]{0:T(512)S(1)}, f32[512,1024]{1,0:T(8,128)}) fusion(bf16[2,256,1024]{2,1,0:T(8,128)(2,1)S(1)} %get-tuple-element.48, f32[512]{0:T(512)} %bitcast.108, f32[1024]{0:T(1024)S(1)} %get-tuple-element.105, f32[512,1024]{1,0:T(8,128)S(1)} %fusion.33, bf16[1024,4096]{1,0:T(8,128)(2,1)} %get-tuple-element.50, ...), kind=kOutput, calls=%fused_computation.30 | convolution fusion | flops 4315937280 | bytes 17838080 | tf_op jit(solution)/shard_map/dot_general | solution.py:86
  356.9 29.5 %slot_grads.1 = bf16[768,128,128]{2,1,0:T(8,128)(2,1)} custom-call(s32[768]{0:T(1024)} %select_reduce_fusion.table.slot_of, bf16[512,1024]{1,0:T(8,128)(2,1)} %copy-done.9, bf16[512,1536]{1,0:T(8,128)(2,1)} %get-tuple-element.65.refs_1_, bf16[512,1792]{1,0:T(8,128)(2,1)} %fusion.40.refs_2_, bf16[512,512]{1,0:T(8,128)(2,1)} %get-tuple-element.72.refs_3_, ...), custom_call_target="tpu_custom_call" | custom-call | tf_op jit(solution)/shard_map/slot_grads/pallas_call | solution.py:798
  386.5 3.9 fusion.19
  394.3 158.4 %reduce_blocks.1 = (bf16[96,128,128]{2,1,0:T(8,128)(2,1)}, f32[296,128]{1,0:T(8,128)}) custom-call(bf16[8,96,128,128]{3,2,1,0:T(8,128)(2,1)} %bitcast.98, f32[296,128]{1,0:T(8,128)} %bitcast.102), custom_call_target="tpu_custom_call" | custom-call | tf_op jit(solution)/shard_map/reduce_blocks/pallas_call | solution.py:638
  554.5 27.5 %shampoo.1 = (f32[96,128,128]{2,1,0:T(8,128)}, f32[96,128,128]{2,1,0:T(8,128)}, f32[96,128,128]{2,1,0:T(8,128)}, f32[96,128,128]{2,1,0:T(8,128)}, bf16[96,128,128]{2,1,0:T(8,128)(2,1)}) custom-call(bf16[96,128,128]{2,1,0:T(8,128)(2,1)} %get-tuple-element.78.total, f32[96,128,128]{2,1,0:T(8,128)} %master.3, f32[96,128,128]{2,1,0:T(8,128)} %left.1, ...), custom_call_target="tpu_custom_call" | custom-call | tf_op jit(solution)/shard_map/shampoo/pallas_call | solution.py:837
  (187 shorter events, 72.6 us)
Async XLA Ops:
  6.6 114.8 %copy-start.16 = (f32[37192]{0:T(1024)S(1)}, f32[37192]{0:T(1024)}, u32[]{:S(2)}) copy-start(f32[37192]{0:T(1024)} %param.23) | copy-start | bytes 446308
  121.0 127.8 %copy-start.1 = (bf16[2,256,1024]{2,1,0:T(8,128)(2,1)}, bf16[2,256,1024]{2,1,0:T(8,128)(2,1)S(1)}, u32[]{:S(2)}) copy-start(bf16[2,256,1024]{2,1,0:T(8,128)(2,1)S(1)} %get-tuple-element.63) | copy-start | bytes 3145732
  121.8 42.0 %copy-start.9 = (bf16[512,1024]{1,0:T(8,128)(2,1)}, bf16[512,1024]{1,0:T(8,128)(2,1)S(1)}, u32[]{:S(2)}) copy-start(bf16[512,1024]{1,0:T(8,128)(2,1)S(1)} %fusion.14.refs_0_) | copy-start | bytes 3145732
  152.0 21.4 %collective-permute-start = (bf16[8,1792]{1,0:T(8,128)(2,1)}, bf16[8,1792]{1,0:T(8,128)(2,1)S(1)}, u32[]{:S(2)}, u32[]{:S(2)}) collective-permute-start(bf16[8,1792]{1,0:T(8,128)(2,1)} %slice.210), channel_id=1, source_target_pairs={{0,1},{2,3},{4,5},{6,7},{8,9},{10,11},{12,13},{14,15},{16,17},{18,... | collective-permute-start | bytes 86024 | tf_op jit(solution)/shard_map/ppermute | solution.py:1464
  159.2 24.7 %collective-permute-start.2 = (bf16[512,256]{1,0:T(8,128)(2,1)}, bf16[512,256]{1,0:T(8,128)(2,1)}, u32[]{:S(2)}, u32[]{:S(2)}) collective-permute-start(bf16[512,256]{1,0:T(8,128)(2,1)} %get-tuple-element.59), channel_id=1, source_target_pairs={{0,1},{2,3},{4,5},{6,7},{8,9},{10,11},{12,13},{14,15},{16,17},{18,... | collective-permute-start | bytes 786440 | tf_op jit(solution)/shard_map/ppermute | solution.py:1464
  182.3 17.9 %collective-permute-start.1 = (bf16[128,1536]{1,0:T(8,128)(2,1)}, bf16[128,1536]{1,0:T(8,128)(2,1)S(1)}, u32[]{:S(2)}, u32[]{:S(2)}) collective-permute-start(bf16[128,1536]{1,0:T(8,128)(2,1)} %get-tuple-element.55), channel_id=1, source_target_pairs={{0,1},{2,3},{4,5},{6,7},{8,9},{10,11},{12,13},{14,15},{16,17},{18,... | collective-permute-start | bytes 1179656 | tf_op jit(solution)/shard_map/ppermute | solution.py:1464
  223.7 25.1 %copy-start.7 = (f32[512,1024]{1,0:T(8,128)}, f32[512,1024]{1,0:T(8,128)S(1)}, u32[]{:S(2)}) copy-start(f32[512,1024]{1,0:T(8,128)S(1)} %get-tuple-element.126) | copy-start | bytes 6291460
  223.7 25.1 %copy-start.24 = (f32[512]{0:T(512)}, f32[512]{0:T(512)S(1)}, u32[]{:S(2)}) copy-start(f32[512]{0:T(512)S(1)} %add_rsqrt_fusion) | copy-start | bytes 6148
  264.2 42.0 %collective-permute-start.5 = (bf16[128,1536]{1,0:T(8,128)(2,1)S(1)}, bf16[128,1536]{1,0:T(8,128)(2,1)}, u32[]{:S(2)}, u32[]{:S(2)}) collective-permute-start(bf16[128,1536]{1,0:T(8,128)(2,1)S(1)} %convert_element_type.119), channel_id=1, source_target_pairs={{1,0},{3,2},{5,4},{7,6},{9,8},{11,10},{13,12},{15,14},{17,16},{19,... | collective-permute-start | bytes 1179656 | tf_op jit(solution)/shard_map/ppermute | solution.py:1464
  269.9 19.8 %copy-start.8 = (f32[512,1024]{1,0:T(8,128)S(1)}, f32[512,1024]{1,0:T(8,128)}, u32[]{:S(2)}) copy-start(f32[512,1024]{1,0:T(8,128)} %copy-done.7) | copy-start | bytes 6291460
  288.4 14.9 %collective-permute-start.7 = (bf16[512,256]{1,0:T(8,128)(2,1)S(1)}, bf16[512,256]{1,0:T(8,128)(2,1)S(1)}, u32[]{:S(2)}, u32[]{:S(2)}) collective-permute-start(bf16[512,256]{1,0:T(8,128)(2,1)S(1)} %slice.142), channel_id=1, source_target_pairs={{1,0},{3,2},{5,4},{7,6},{9,8},{11,10},{13,12},{15,14},{17,16},{19,... | collective-permute-start | bytes 786440 | tf_op jit(solution)/shard_map/ppermute | solution.py:1464
  295.9 286.1 %collective-permute-start.3 = (bf16[256,1024]{1,0:T(8,128)(2,1)}, bf16[256,1024]{1,0:T(8,128)(2,1)}, u32[]{:S(2)}, u32[]{:S(2)}) collective-permute-start(bf16[256,1024]{1,0:T(8,128)(2,1)} %get-tuple-element.103), channel_id=1, source_target_pairs={{0,0},{2,1},{1,2},{3,3},{4,4},{6,5},{5,6},{7,7},{8,8},{10,9},{9,10... | collective-permute-start | bytes 1572872 | tf_op jit(solution)/shard_map/ppermute | solution.py:1455
  298.1 284.0 %collective-permute-start.4 = (bf16[256,1024]{1,0:T(8,128)(2,1)}, bf16[256,1024]{1,0:T(8,128)(2,1)}, u32[]{:S(2)}, u32[]{:S(2)}) collective-permute-start(bf16[256,1024]{1,0:T(8,128)(2,1)} %get-tuple-element.102), channel_id=1, source_target_pairs={{2,0},{0,1},{3,2},{1,3},{6,4},{4,5},{7,6},{5,7},{10,8},{8,9},{11,1... | collective-permute-start | bytes 1572872 | tf_op jit(solution)/shard_map/ppermute | solution.py:1455
  308.2 30.0 %copy-start.10 = (bf16[512,1024]{1,0:T(8,128)(2,1)S(1)}, bf16[512,1024]{1,0:T(8,128)(2,1)}, u32[]{:S(2)}) copy-start(bf16[512,1024]{1,0:T(8,128)(2,1)} %copy-done.9) | copy-start | bytes 3145732
  341.8 4.3 collective-permute-start.6
  356.9 29.5 %copy-start.2 = (bf16[2,256,1024]{2,1,0:T(8,128)(2,1)S(1)}, bf16[2,256,1024]{2,1,0:T(8,128)(2,1)}, u32[]{:S(2)}) copy-start(bf16[2,256,1024]{2,1,0:T(8,128)(2,1)} %copy-done.1) | copy-start | bytes 3145732
  356.9 29.5 %copy-start.25 = (f32[512]{0:T(512)S(1)}, f32[512]{0:T(512)}, u32[]{:S(2)}) copy-start(f32[512]{0:T(512)} %copy-done.24) | copy-start | bytes 6148
  356.9 29.5 %copy-start.28 = (f32[1,2,2,128]{3,1,2,0:T(2,128)S(1)}, f32[1,2,2,128]{3,1,2,0:T(2,128)}, u32[]{:S(2)}) copy-start(f32[1,2,2,128]{3,1,2,0:T(2,128)} %copy-done.27) | copy-start | bytes 6148
  356.9 29.5 %copy-start.30 = (f32[512]{0:T(512)S(1)}, f32[512]{0:T(512)}, u32[]{:S(2)}) copy-start(f32[512]{0:T(512)} %copy-done.29) | copy-start | bytes 6148
  391.5 193.2 %collective-permute-start.8 = (bf16[256,1024]{1,0:T(8,128)(2,1)}, bf16[256,1024]{1,0:T(8,128)(2,1)S(1)}, u32[]{:S(2)}, u32[]{:S(2)}) collective-permute-start(bf16[256,1024]{1,0:T(8,128)(2,1)} %get-tuple-element.99), channel_id=1, source_target_pairs={{0,0},{2,1},{1,2},{3,3},{4,4},{6,5},{5,6},{7,7},{8,8},{10,9},{9,10... | collective-permute-start | bytes 1572872 | tf_op jit(solution)/shard_map/ppermute | solution.py:1455
  393.4 191.3 %collective-permute-start.9 = (bf16[256,1024]{1,0:T(8,128)(2,1)}, bf16[256,1024]{1,0:T(8,128)(2,1)}, u32[]{:S(2)}, u32[]{:S(2)}) collective-permute-start(bf16[256,1024]{1,0:T(8,128)(2,1)} %get-tuple-element.98), channel_id=1, source_target_pairs={{2,0},{0,1},{3,2},{1,3},{6,4},{4,5},{7,6},{5,7},{10,8},{8,9},{11,1... | collective-permute-start | bytes 1572872 | tf_op jit(solution)/shard_map/ppermute | solution.py:1455
  394.2 158.5 %copy-start.17 = (f32[37192]{0:T(1024)S(1)}, f32[37192]{0:T(1024)}, u32[]{:S(2)}) copy-start(f32[37192]{0:T(1024)} %param.23) | copy-start | bytes 446308
  394.2 158.5 %copy-start.20 = (f32[37192]{0:T(1024)S(1)}, f32[37192]{0:T(1024)}, u32[]{:S(2)}) copy-start(f32[37192]{0:T(1024)} %param.24) | copy-start | bytes 446308
  394.3 158.5 %copy-start.21 = (f32[37192]{0:T(1024)S(1)}, f32[37192]{0:T(1024)}, u32[]{:S(2)}) copy-start(f32[37192]{0:T(1024)} %param.25) | copy-start | bytes 446308
  (27 other events, 122.1 us)

commit v2 on v1

--- a/solution.py
+++ b/solution.py
@@ -384,9 +384,13 @@
 def entries(size):
     return size + 1 if size > 2 else 1
 
-SUBS = 2
-LAG = 2
-LONE = 1 / 3
+SUBS = 3
+LONE = 5 / 16
+RING = 6
+STAGED = 3
+LATE_ADD, LATE_X, LATE_Z, PER_HOP = 1, 3, 6, 3
+CHUNK = 512
+HELD = 12
 
 
 def split_of(slots, tall):
@@ -396,9 +400,12 @@
     return half, piece, lone, piece - lone
 
 
-def reduce_kernel(grid, slots, part, vec, out, vec_out, acc, land_c, land_y, land_x, land_z, fin, vbuf, vland,
-                  s_load, s_c, r_c, s_y, r_y, s_x, r_x, s_z, r_z, s_f, r_f, s_m, r_m, s_v, r_v):
+def reduce_kernel(grid, slots, widths, left_at, right_at, vec, *refs):
     wide, tall, deep = grid
+    count = sum(len(w) for w in widths)
+    arrays = refs[:count]
+    (out, vec_out, turned, right, held, acc, stage, land_c, land_y, land_x, land_z, fin, vbuf, vland,
+     s_left, s_right, s_c, r_c, s_y, r_y, s_x, r_x, s_z, r_z, s_f, r_f, s_m, r_m, s_v, r_v, free) = refs[count:]
     n = wide * deep
     x, y, z, c = place(grid)
     half, size, lone, bulk = split_of(slots, tall)
@@ -408,14 +415,40 @@
     bulk_at = y * lone
     lone_at = y * bulk
     other_at = (1 - y) * bulk
-    bits = lambda size: [1 << b for b in range(size.bit_length() - 1)]
+    bits = lambda length: [1 << b for b in range(length.bit_length() - 1)]
     partners = [(me, mate)]
     partners += [(me, (y ^ b) * CORES + c) for b in bits(tall)]
     partners += [(z * wide + (x ^ b), seq) for b in bits(wide)]
     partners += [((z ^ b) * wide + x, seq) for b in bits(deep)]
+    rounds = len(partners)
+
+    chunks, k, at = [], 0, 0
+    for width in widths[0]:
+        for q in range(0, width, CHUNK):
+            chunks.append((k, q, at + q))
+        k, at = k + 1, at + width
+
+    def chunk_copy(i):
+        k, q, _ = chunks[i]
+        return pltpu.make_async_copy(arrays[k].at[:, pl.ds(q, CHUNK)], held.at[i % HELD], s_left.at[i % HELD])
+
+    ahead = min(HELD, len(chunks))
+    for i in range(ahead):
+        chunk_copy(i).start()
+    copies, at = [], 0
+    for width in widths[1]:
+        def one(q, _, k=k, at=at):
+            cols = pl.ds(pl.multiple_of(q * BS, BS), BS)
+            pltpu.make_async_copy(arrays[k].at[:, cols], right.at[at + q], s_right.at[k - len(widths[0])]).start()
+            return 0
+
+        lax.fori_loop(0, width // BS, one, 0)
+        part = right.at[pl.ds(at, width // BS)]
+        copies.append(pltpu.make_async_copy(part, part, s_right.at[k - len(widths[0])]))
+        k, at = k + 1, at + width // BS
 
     barrier = pltpu.get_barrier_semaphore()
-    count = jnp.int32(0)
+    awaited = jnp.int32(0)
     for step_by, at, length in ((wide, z, deep), (1, x, wide)):
         for step in (1, -1):
             ok = (at + step >= 0) & (at + step < length)
@@ -424,10 +457,10 @@
             def _(there=me + step * step_by):
                 pl.semaphore_signal(barrier, inc=1, device_id=(there, seq), device_id_type=MESH)
 
-            count = count + ok.astype(jnp.int32)
+            awaited = awaited + ok.astype(jnp.int32)
     for device in partners:
         pl.semaphore_signal(barrier, inc=1, device_id=device, device_id_type=MESH)
-    pl.semaphore_wait(barrier, count + len(partners))
+    pl.semaphore_wait(barrier, awaited + rounds)
 
     def remote(source, target, send_sem, recv_sem, device):
         return pltpu.make_async_remote_copy(
@@ -436,54 +469,53 @@
         )
 
     def landed(target, recv_sem):
-        remote(target, target, s_load.at[0], recv_sem, (me, seq)).wait_recv()
+        remote(target, target, s_left.at[0], recv_sem, (me, seq)).wait_recv()
+
+    def vec_copy(t):
+        return remote(vbuf.at[t], vland.at[t], s_v.at[t], r_v.at[t], partners[t])
+
+    vbuf[0] = vec[...]
+    vec_copy(0).start()
+    for i in range(len(chunks)):
+        chunk_copy(i).wait()
+        for q in range(0, CHUNK, BS):
+            turned[(chunks[i][2] + q) // BS] = held[i % HELD, :, q : q + BS].T
+        if i + HELD < len(chunks):
+            chunk_copy(i + HELD).start()
+    for copy in copies:
+        copy.wait()
 
     group = wide * SUBS
     total = n * SUBS
 
     def item_of(k):
-        xs, zs = far_first(x, wide, k % wide), far_first(z, deep, k // group)
+        xs = far_first(x, wide, k % wide)
+        zs = far_first(z, deep, k // group)
         sub = (k // wide) % SUBS
         return xs, zs, sub, (zs * wide + xs) * SUBS + sub
 
-    def own(k):
-        xs, zs, sub, item = item_of(k)
-        return pltpu.make_async_copy(part.at[zs * wide + xs, pl.ds(c * half + sub * size, size)], acc.at[item], s_load.at[item])
-
     def swap(k):
-        xs, zs, sub, item = item_of(k)
-        source = part.at[zs * wide + xs, pl.ds((1 - c) * half + sub * size, size)]
-        return remote(source, land_c.at[item], s_c.at[item], r_c.at[item], (me, mate))
+        return remote(stage.at[k % STAGED], land_c.at[k % RING], s_c.at[k % STAGED], r_c.at[k % RING], (me, mate))
 
     def cross(item):
         return remote(acc.at[item, pl.ds(other_at, lone)], land_y.at[item], s_y.at[item], r_y.at[item], (me, (tall - 1 - y) * CORES + c))
 
-    def begin(k, _):
-        own(k).start()
-        swap(k).start()
-        return 0
-
-    rounds = len(partners)
-
-    def vec_copy(t):
-        return remote(vbuf.at[t], vland.at[t], s_v.at[t], r_v.at[t], partners[t])
-
-    vbuf[0] = vec[...]
-    vec_copy(0).start()
-    lax.fori_loop(0, total, begin, 0)
-    for t in range(rounds):
-        landed(vland.at[t], r_v.at[t])
-        vbuf[t + 1] = vbuf[t] + vland[t]
-        if t + 1 < rounds:
-            vec_copy(t + 1).start()
-    vec_out[...] = vbuf[rounds]
-
-    def add(item, at, count, ref, first):
+    def grads(k, core, ref, first):
+        xs, zs, sub, item = item_of(k)
+        base = (zs * wide + xs) * slots + core * half + sub * size
+
+        def one(i, _):
+            ref[first, i] = dot(turned[left_at[base + i]], right[right_at[base + i]]).astype(ref.dtype)
+            return 0
+
+        lax.fori_loop(0, size, one, 0, unroll=min(4, size))
+
+    def add(item, at, length, ref, first):
         def one(i, _):
             acc[item, at + i] = acc[item, at + i] + ref[first + (i,)]
             return 0
 
-        lax.fori_loop(0, count, one, 0, unroll=4)
+        lax.fori_loop(0, length, one, 0, unroll=min(3, length))
 
     def step_x(k, begin_it):
         xs, zs, sub, item = item_of(k)
@@ -554,42 +586,80 @@
     def swap_core(sub):
         return remote(acc.at[me * SUBS + sub], out.at[pl.ds(c * half + sub * size, size)], s_m.at[sub], r_m.at[sub], (me, mate))
 
-    def first(k, _):
-        item = item_of(k)[3]
-        own(k).wait()
-        landed(land_c.at[item], r_c.at[item])
-        add(item, 0, size, land_c, (item,))
-        if lone:
-            cross(item).start()
-        return 0
-
-    def second(k, _):
+    late_z = LATE_Z + PER_HOP * jnp.minimum(z, deep - 1 - z)
+
+    def turn_of(k, _):
         @pl.when(k < total)
         def _():
-            item = item_of(k)[3]
+            @pl.when(k >= STAGED)
+            def _():
+                swap(k - STAGED).wait_send()
+
+            grads(k, 1 - c, stage, k % STAGED)
+
+            @pl.when(k >= RING)
+            def _():
+                pl.semaphore_wait(free, 1)
+
+            swap(k).start()
+            grads(k, c, acc, item_of(k)[3])
+
+        for t in range(1, rounds + 1):
+            @pl.when(k == t)
+            def _(t=t):
+                landed(vland.at[t - 1], r_v.at[t - 1])
+                vbuf[t] = vbuf[t - 1] + vland[t - 1]
+                if t < rounds:
+                    vec_copy(t).start()
+                else:
+                    vec_out[...] = vbuf[t]
+
+        b = k - LATE_ADD
+
+        @pl.when((b >= 0) & (b < total))
+        def _():
+            item = item_of(b)[3]
+            landed(land_c.at[b % RING], r_c.at[b % RING])
+            add(item, 0, size, land_c, (b % RING,))
+
+            @pl.when(b < total - RING)
+            def _():
+                pl.semaphore_signal(free, inc=1, device_id=(me, mate), device_id_type=MESH)
+
+            if lone:
+                cross(item).start()
+
+        b = k - LATE_X
+
+        @pl.when((b >= 0) & (b < total))
+        def _():
+            item = item_of(b)[3]
             if lone:
                 landed(land_y.at[item], r_y.at[item])
                 add(item, lone_at, lone, land_y, (item,))
             if wide > 2:
-                @pl.when(item_of(k)[0] != x)
+                @pl.when(item_of(b)[0] != x)
                 def _():
-                    take_x(k)
-            step_x(k, True)
-
-        late = k - LAG * wide
-
-        @pl.when((late >= 0) & (late % wide == wide - 1))
+                    take_x(b)
+            step_x(b, True)
+
+        b = k - late_z
+
+        @pl.when((b >= 0) & (b < total) & (b % wide == wide - 1))
         def _():
-            take_x(late)
-            take_z(late)
-            step_z(late, True)
+            take_x(b)
+            take_z(b)
+            step_z(b, True)
+            if planes:
+                @pl.when(item_of(b)[1] == z)
+                def _():
+                    swap_plane(0, item_of(b)[2]).start()
 
         return 0
 
-    lax.fori_loop(0, total, first, 0)
-    lax.fori_loop(0, total + (LAG - 1) * wide, second, 0)
+    lax.fori_loop(0, total + LATE_Z + PER_HOP * ((deep - 1) // 2), turn_of, 0)
+
     def finish(k, _):
-        swap(k).wait_send()
         if lone:
             item = item_of(k)[3]
 
@@ -605,19 +675,18 @@
 
         return 0
 
-    tail = [total + (LAG - 1) * wide + i for i in range(wide)]
-    for k in tail:
-        second(jnp.int32(k), 0)
     for t in range(len(planes)):
         for sub in range(SUBS):
-            swap_plane(t, sub).start()
+            if t:
+                swap_plane(t, sub).start()
         for sub in range(SUBS):
             take_plane(t, sub)
             if t == len(planes) - 1:
                 swap_core(sub).start()
-    for sub in range(SUBS):
-        out[pl.ds(c * half + sub * size, size)] = acc[me * SUBS + sub]
+                out[pl.ds(c * half + sub * size, size)] = acc[me * SUBS + sub]
     lax.fori_loop(0, total, finish, 0)
+    for k in range(max(total - STAGED, 0), total):
+        swap(k).wait_send()
     for t in range(rounds):
         vec_copy(t).wait_send()
     for sub in range(SUBS):
@@ -625,32 +694,38 @@
         landed(out.at[pl.ds((1 - c) * half + sub * size, size)], r_m.at[sub])
 
 
-def reduce_blocks(grid, part, vec):
+def reduce_blocks(grid, slots, left_at, right_at, lefts, rights, vec):
     wide, tall, deep = grid
-    n, slots = part.shape[:2]
+    n = wide * deep
     half, size, lone, bulk = split_of(slots, tall)
-    tile = part.shape[2:]
+    tile = (BS, BS)
+    low = lefts[0].dtype
+    tokens = lefts[0].shape[0]
+    widths = [[a.shape[1] for a in lefts], [a.shape[1] for a in rights]]
     sem = pltpu.SemaphoreType.DMA
     rounds = sum(length.bit_length() - 1 for length in (CORES, wide, tall, deep))
     planes = max(tall.bit_length() - 1, 1)
     items = n * SUBS
-    buf = lambda *lead: pltpu.VMEM(lead + tile, part.dtype)
+    buf = lambda *lead: pltpu.VMEM(lead + tile, low)
+    smem, vmem, hbm = (pl.BlockSpec(memory_space=m) for m in (pltpu.SMEM, pltpu.VMEM, pl.ANY))
     return pl.pallas_call(
-        functools.partial(reduce_kernel, grid, slots),
-        out_shape=(jax.ShapeDtypeStruct((slots,) + tile, part.dtype), jax.ShapeDtypeStruct(vec.shape, vec.dtype)),
-        in_specs=[pl.BlockSpec(memory_space=pl.ANY), pl.BlockSpec(memory_space=pltpu.VMEM)],
-        out_specs=(pl.BlockSpec(memory_space=pltpu.VMEM), pl.BlockSpec(memory_space=pltpu.VMEM)),
+        functools.partial(reduce_kernel, grid, slots, widths),
+        out_shape=(jax.ShapeDtypeStruct((slots,) + tile, low), jax.ShapeDtypeStruct(vec.shape, vec.dtype)),
+        in_specs=[smem, smem, vmem] + [hbm] * (len(lefts) + len(rights)),
+        out_specs=(vmem, vmem),
         scratch_shapes=[
-            buf(items, size), buf(items, size), buf(items, max(lone, 1)), buf(entries(wide), deep * SUBS, bulk),
+            pltpu.VMEM((sum(widths[0]) // BS, BS, tokens), low), pltpu.VMEM((sum(widths[1]) // BS, tokens, BS), low), pltpu.VMEM((HELD, tokens, CHUNK), low),
+            buf(items, size), buf(STAGED, size), buf(RING, size), buf(items, max(lone, 1)), buf(entries(wide), deep * SUBS, bulk),
             buf(entries(deep), SUBS, bulk), buf(planes, SUBS, size),
             pltpu.VMEM((rounds + 1,) + vec.shape, vec.dtype), pltpu.VMEM((rounds,) + vec.shape, vec.dtype),
-            sem((items,)), sem((items,)), sem((items,)), sem((items,)), sem((items,)), sem((items,)),
+            sem((HELD,)), sem((len(rights),)), sem((STAGED,)), sem((RING,)), sem((items,)), sem((items,)), sem((items,)),
             sem((entries(wide), deep * SUBS)), sem((deep * SUBS,)), sem((entries(deep), SUBS)),
             sem((planes, SUBS)), sem((planes, SUBS)), sem((SUBS,)), sem((SUBS,)), sem((rounds,)), sem((rounds,)),
+            pltpu.SemaphoreType.REGULAR,
         ],
         compiler_params=pltpu.CompilerParams(collective_id=1, has_side_effects=True, vmem_limit_bytes=63 << 20),
         name="reduce_blocks",
-    )(part, vec)
+    )(left_at, right_at, vec, *lefts, *rights)
 
 
 STEP_BLOCKS = 32
@@ -705,6 +780,32 @@
 def slots_in_order(block_of_slot, order):
     match = jnp.array(order, jnp.int32)[:, None] == block_of_slot[None, :]
     return jnp.sum(jnp.where(match, jnp.arange(block_of_slot.shape[0], dtype=jnp.int32)[None, :], 0), axis=1)
+
+
+def values_of(block_of_slot, values):
+    match = block_of_slot[:, None] == jnp.arange(len(values), dtype=jnp.int32)[None, :]
+    return jnp.sum(jnp.where(match, jnp.array(values, jnp.int32)[None, :], 0), axis=1)
+
+
+def grad_tables():
+    lefts, rights = [], []
+    left_base = right_base = 0
+    for members, beside in ((WIDE_IN, True), (TALL_OUT, False), (WIDE_FF, True), (TALL_FF, False)):
+        for m in members:
+            rows, cols = SHAPES[m]
+            for r in range(0, rows, BS):
+                for q in range(0, cols, BS):
+                    lefts.append((left_base + r) // BS)
+                    rights.append((right_base + q) // BS)
+            if beside:
+                right_base += cols
+            else:
+                left_base += rows
+        if beside:
+            left_base += rows
+        else:
+            right_base += cols
+    return lefts, rights
 
 
 def assemble(blocks, table):
@@ -724,93 +825,6 @@
         compiler_params=kernel_params(),
         name="assemble",
     )(table, blocks)
-
-
-UNIT_ROWS = 256
-UNIT_COLS = 1024
-STAGES = 3
-
-
-def slot_grads_kernel(sizes, slot_of, *refs):
-    count = sum(len(left) + len(right) for left, right in sizes)
-    arrays, (out, left, right, turned, stage, s_in, s_out) = refs[:count], refs[count:]
-    units = []
-    groups, k, left_at, right_at, first = [], 0, 0, 0, 0
-    for lefts, rights in sizes:
-        copies, at = [], left_at
-        for width in lefts:
-            copies.append(pltpu.make_async_copy(arrays[k], left.at[:, pl.ds(at, width)], s_in.at[k]))
-            at, k = at + width, k + 1
-        rows, at = at - left_at, right_at
-        for width in rights:
-            copies.append(pltpu.make_async_copy(arrays[k], right.at[:, pl.ds(at, width)], s_in.at[k]))
-            at, k = at + width, k + 1
-        cols = at - right_at
-        groups.append((copies, left_at, rows, right_at, cols, first))
-        left_at, right_at = left_at + rows, right_at + cols
-        first += rows // BS * (cols // BS)
-    for copies, *_ in groups:
-        for copy in copies:
-            copy.start()
-
-    def drain(slot):
-        pltpu.make_async_copy(out.at[pl.ds(0, UNIT_ROWS // BS * (UNIT_COLS // BS))], out.at[pl.ds(0, UNIT_ROWS // BS * (UNIT_COLS // BS))],
-                              s_out.at[slot]).wait()
-
-    done = 0
-    for copies, left_at, rows, right_at, cols, first in groups:
-        for copy in copies:
-            copy.wait()
-        across = cols // UNIT_COLS
-
-        def one(u, _, left_at=left_at, right_at=right_at, cols=cols, first=first, across=across, done=done):
-            r, q = u // across, u % across
-            slot = (done + u) % STAGES
-
-            @pl.when(q == 0)
-            def _():
-                turned[...] = left[:, pl.ds(pl.multiple_of(left_at + r * UNIT_ROWS, BS), UNIT_ROWS)].T
-
-            @pl.when(done + u >= STAGES)
-            def _():
-                drain(slot)
-
-            column = pl.multiple_of(right_at + q * UNIT_COLS, BS)
-            stage[slot] = dot(turned[...], right[:, pl.ds(column, UNIT_COLS)]).astype(BF16)
-            for i in range(UNIT_ROWS // BS):
-                for p in range(UNIT_COLS // BS):
-                    block = first + (r * (UNIT_ROWS // BS) + i) * (cols // BS) + q * (UNIT_COLS // BS) + p
-                    pltpu.make_async_copy(stage.at[slot, pl.ds(i * BS, BS), pl.ds(p * BS, BS)], out.at[slot_of[block]], s_out.at[slot]).start()
-            return 0
-
-        total = rows // UNIT_ROWS * across
-        lax.fori_loop(0, total, one, 0)
-        done += total
-    for u in range(max(done - STAGES, 0), done):
-        drain(u % STAGES)
-
-
-def slot_grads(slot_of, groups):
-    arrays = [a for lefts, rights in groups for a in lefts + rights]
-    sizes = [([a.shape[1] for a in lefts], [a.shape[1] for a in rights]) for lefts, rights in groups]
-    tokens = arrays[0].shape[0]
-    hbm = pl.BlockSpec(memory_space=pl.ANY)
-    return pl.pallas_call(
-        functools.partial(slot_grads_kernel, sizes),
-        out_shape=jax.ShapeDtypeStruct((slot_of.shape[0], BS, BS), BF16),
-        grid_spec=pltpu.PrefetchScalarGridSpec(
-            num_scalar_prefetch=1, grid=(1,), in_specs=[hbm] * len(arrays), out_specs=hbm,
-            scratch_shapes=[
-                pltpu.VMEM((tokens, sum(sum(left) for left, _ in sizes)), BF16),
-                pltpu.VMEM((tokens, sum(sum(right) for _, right in sizes)), BF16),
-                pltpu.VMEM((UNIT_ROWS, tokens), BF16),
-                pltpu.VMEM((STAGES, UNIT_ROWS, UNIT_COLS), BF16),
-                pltpu.SemaphoreType.DMA((len(arrays),)), pltpu.SemaphoreType.DMA((STAGES,)),
-            ],
-        ),
-        compiler_params=kernel_params(),
-        name="slot_grads",
-    )(slot_of, *arrays)
 
 
 SHAMPOO = 8
@@ -1482,6 +1496,7 @@
 
     orders = all_orders()
     table = slots_in_order(block_of_slot, sum(orders, []))
+    left_at, right_at = (values_of(block_of_slot, values) for values in grad_tables())
     gathered, rows, given, labels_all = gather_blocks(grid, master_blocks, tokens, cotangent, doc_ids)
     w_in, w_out, w_ff, w_down = assemble(gathered.reshape(-1, BS, BS), table)
     rows, given = rows.reshape(count, D), given.reshape(count, D)
@@ -1581,16 +1596,13 @@
     grad_tokens = ungroup((g_values + g_hidden).astype(BF16), micro).astype(F32)
     g_w_dt = dot_tn(normed_in, g_raw)
 
-    flat = slot_grads(table, [
-        ([normed_in], [g_z, g_conv, g_q, g_kv]), ([normed_ssm, context], [hidden_low]),
-        ([normed_mid], [g_ff]), ([mixed], [given]),
-    ])
     parts = [g_gain_in, g_gain_mid, g_gain_mix[0], g_taps[:KERNEL].reshape(-1), g_taps[KERNEL]]
     parts += [g_params[i, :HEADS_SSM] for i in range(3)] + [g_w_dt[:, :HEADS_SSM].reshape(-1)]
     width = vector_params.shape[0]
     height = -(-width // (8 * LANES)) * 8
     vector = jnp.concatenate(parts + [jnp.zeros((height * LANES - width,), F32)]).reshape(height, LANES)
-    total, vector = reduce_blocks(grid, flat.reshape(-1, slots, BS, BS), vector)
+    total, vector = reduce_blocks(grid, slots, left_at, right_at, [normed_in, normed_ssm, context, normed_mid, mixed],
+                                  [g_z, g_conv, g_q, g_kv, hidden_low, g_ff, given], vector)
     norm = 1.0 / math.sqrt(count * seq * lax.axis_size("dp"))
     updates = shampoo(norm, total, master_blocks, left_stats, right_stats, left_roots, right_roots)
     g_vector = vector.reshape(-1)[:width] * norm

time: 600 us -> 552 us (0.920)
  Pallas kernels: 444 us -> 394 us
    pallas_call x2 -> x1, Pallas kernels: 188 us -> 137 us  [reduce_blocks(): pl.pallas_call(functools.partial(reduce_kernel, grid, slots, widths), out...]
    unnamed x84 -> x76, local copies, waits for them, and re-layouts: 12.8 us -> 13.6 us
  transfers between devices with their start and end apart: 10 -> 10, of which waited for: 0 -> 0; matrix products, arithmetic and copies ran while one was open for 10% -> 11% of each run, Pallas kernels for 49% -> 44%
where the time goes in v2:
time: 552 us; the launch traced here: 542 us
  Pallas kernels  394 us (71%)
  matrix products  63.5 us (12%)
  local copies, waits for them, and re-layouts  34.4 us (6%)
  other arithmetic  26.4 us (5%)
  starting transfers between devices  20.7 us (4%)
    pallas_call x1, Pallas kernels, reduce_blocks(): pl.pallas_call(functools.partial(reduce_kernel, grid, slots, widths), out...  137 us
    pallas_call x1, Pallas kernels, gather_blocks(): pl.pallas_call(functools.partial(gather_kernel, grid, slots), out_shape=(...  114 us
    dot_general x5, matrix products, dot_nt(): lax.dot_general(left, right, (((1,), (1,)), ((), ())), preferred_element_...  32.1 us
    pallas_call x1, Pallas kernels, mix_back(): pl.pallas_call(mix_back_kernel, out_shape=(jax.ShapeDtypeStruct((tokens,...  30.1 us
    dot_general x6, matrix products, dot(): return jnp.dot(left, right, preferred_element_type=F32, precision=precision)  29.2 us
    pallas_call x1, Pallas kernels, shampoo(): pl.pallas_call(functools.partial(shampoo_kernel, norm), out_shape=(full,...  27.5 us
    pallas_call x1, Pallas kernels, assemble(): pl.pallas_call(assemble_kernel, out_shape=tuple((jax.ShapeDtypeStruct(sha...  18.4 us
    pallas_call x1, Pallas kernels, attend_back(): pl.pallas_call(attend_back_kernel, out_shape=(jax.ShapeDtypeStruct((token...  17.4 us
  transfers between devices with their start and end apart: 10, of which 0 were waited for; matrix products, arithmetic and copies ran while one was open for 11% of the time, Pallas kernels for 44%

profile of v2, /device:TPU:11, one launch (start us, length us, event | category | flops | bytes accessed | tf_op | source)
XLA Modules:
  0.0 541.6 jit_solution(1944512113254697387)
XLA Ops:
  0.7 2.8 copy-done
  6.6 114.5 %gather_blocks.1 = (bf16[8,96,128,128]{3,2,1,0:T(8,128)(2,1)}, bf16[2,256,1024]{2,1,0:T(8,128)(2,1)S(1)}, bf16[2,256,1024]{2,1,0:T(8,128)(2,1)S(1)}, s32[4,2,256]{2,1,0:T(2,128)S(1)}) custom-call(f32[96,128,128]{2,1,0:T(8,128)S(1)} %copy-done, bf16[2,256,1024]{2,1,0:T(8,128)(2,1)S(1)} %copy-done.2, bf16[2,256,1024]{2,1,0:T(8,128)(2,1)S(1)} %copy-done.3, ...), custom_call_target="tpu_custom_call" | custom-call | tf_op jit(solution)/shard_map/gather_blocks/pallas_call | solution.py:348
  123.8 18.4 %assemble.1 = (bf16[1024,4096]{1,0:T(8,128)(2,1)}, bf16[2048,1024]{1,0:T(8,128)(2,1)}, bf16[1024,4096]{1,0:T(8,128)(2,1)}, bf16[2048,1024]{1,0:T(8,128)(2,1)}) custom-call(s32[768]{0:T(1024)} %get-tuple-element.91.table, bf16[768,128,128]{2,1,0:T(8,128)(2,1)} %bitcast.97), custom_call_target="tpu_custom_call" | custom-call | tf_op jit(solution)/shard_map/assemble/pallas_call | solution.py:814
  142.1 6.9 %fusion.53.proj_x.proj_bc.z.refs_0_.refs_1_.refs_2_.refs_3_.refs_4_.refs_5_ = f32[512,4096]{1,0:T(8,128)S(1)} fusion(bf16[512,1024]{1,0:T(8,128)(2,1)S(1)} %fusion.14.refs_0_, bf16[1024,4096]{1,0:T(8,128)(2,1)} %get-tuple-element.50), kind=kOutput, calls=%fused_computation.123 | convolution fusion | flops 4294967296 | bytes 17825792 | tf_op jit(solution)/shard_map/dot_general | solution.py:82
  149.1 3.3 copy-done.5
  157.1 3.0 rope.1
  178.0 8.2 %mix_first.1 = (bf16[512,1792]{1,0:T(8,128)(2,1)}, f32[2,512,128]{2,1,0:T(8,128)}, f32[128,512]{1,0:T(8,128)}, bf16[128,1536]{1,0:T(8,128)(2,1)}, f32[8,128]{1,0:T(8,128)}) custom-call(f32[512,4096]{1,0:T(8,128)} %copy-done.5, f32[512,4096]{1,0:T(8,128)} %copy-done.5, bf16[8,1792]{1,0:T(8,128)(2,1)} %copy-done.23, f32[8,1792]{1,0:T(8,128)} %maximum_maximum_fusion.taps, ...), custom_call_target="tpu_custom_call" | custom-call | tf_op jit(solution)/shard_map/mix_first/pallas_call | solution.py:939
  190.7 10.9 %attend.1 = (bf16[512,512]{1,0:T(8,128)(2,1)}, f32[4,8,512]{2,1,0:T(8,128)}) custom-call(bf16[512,512]{1,0:T(8,128)(2,1)} %get-tuple-element.58.q, bf16[1024,256]{1,0:T(8,128)(2,1)} %copy-done.13, f32[2,8,768]{2,1,0:T(8,128)} %broadcast_in_dim.46.key_labels, f32[512,128]{1,0:T(8,128)} %pad.22.marks), custom_call_target="tpu_custom_call" | custom-call | tf_op jit(solution)/shard_map/attend/pallas_call | solution.py:1373
  201.7 3.4 fusion.27
  207.7 16.8 %mix_second.1 = (f32[512,1536]{1,0:T(8,128)}, bf16[512,1536]{1,0:T(8,128)(2,1)}, f32[3,128,1536]{2,1,0:T(8,128)}) custom-call(bf16[512,1792]{1,0:T(8,128)(2,1)} %get-tuple-element.52.x.b.c, bf16[512,1792]{1,0:T(8,128)(2,1)} %get-tuple-element.52.x.b.c, bf16[512,1792]{1,0:T(8,128)(2,1)} %get-tuple-element.52.x.b.c, f32[512,4096]{1,0:T(8,128)} %copy-done.5, ...), custom_call_target="tpu_custom_call" | custom-call | tf_op jit(solution)/shard_map/mix_second/pallas_call | solution.py:1034
  224.5 5.1 multiply_reduce_fusion.2
  230.0 6.8 %fusion.54 = f32[512,4096]{1,0:T(8,128)} fusion(bf16[512,1024]{1,0:T(8,128)(2,1)S(1)} %multiply_convert_fusion.3.refs_3_, bf16[1024,4096]{1,0:T(8,128)(2,1)S(1)} %bitcast.115), kind=kOutput, calls=%fused_computation.124 | convolution fusion | flops 4294967296 | bytes 17825792 | tf_op jit(solution)/shard_map/dot_general | solution.py:82
  236.8 7.3 %multiply_convert_fusion.1 = (bf16[512,2048]{1,0:T(8,128)(2,1)S(1)}, bf16[512,2048]{1,0:T(8,128)(2,1)S(1)}, bf16[512,2048]{1,0:T(8,128)(2,1)}) fusion(f32[512,4096]{1,0:T(8,128)} %fusion.54, bf16[512,1024]{1,0:T(8,128)(2,1)S(1)} %bitcast.95, bf16[2048,1024]{1,0:T(8,128)(2,1)S(1)} %copy-done.33), kind=kOutput, calls=%fused_computation.10 | convolution fusion | flops 2163212288 | bytes 19922944 | tf_op jit(solution)/shard_map/dot_general | solution.py:86
  246.6 8.0 %multiply_reduce_fusion = (f32[1024]{0:T(1024)}, f32[512]{0:T(512)S(1)}, f32[512,1024]{1,0:T(8,128)S(1)}) fusion(f32[512,1024]{1,0:T(8,128)S(1)} %get-tuple-element.129, f32[512]{0:T(512)S(1)} %add_rsqrt_fusion, f32[1024]{0:T(1024)S(1)} %get-tuple-element.107, bf16[1024,4096]{1,0:T(8,128)(2,1)} %get-tuple-element.61, ...), kind=kOutput, calls=%fused_computation.35 | convolution fusion | flops 4306500096 | bytes 16789504 | tf_op jit(solution)/shard_map/dot_general | solution.py:86
  257.5 4.4 fusion.55.grad.given
  261.9 7.7 %gate_back.1 = (bf16[512,1536]{1,0:T(8,128)(2,1)}, bf16[512,1536]{1,0:T(8,128)(2,1)}, f32[8,1536]{1,0:T(8,128)}, f32[128,1536]{1,0:T(8,128)}) custom-call(f32[512,2048]{1,0:T(8,128)} %fusion.55.grad.given, f32[512,1536]{1,0:T(8,128)} %get-tuple-element.64.y, f32[512,4096]{1,0:T(8,128)} %copy-done.5, f32[8,1536]{1,0:T(8,128)} %concatenate.45.gain, ...), custom_call_target="tpu_custom_call" | custom-call | tf_op jit(solution)/shard_map/gate_back/pallas_call | solution.py:1102
  270.8 5.2 collective-permute-start.5
  277.2 17.4 %attend_back.1 = (bf16[512,512]{1,0:T(8,128)(2,1)}, bf16[1024,256]{1,0:T(8,128)(2,1)}) custom-call(bf16[512,512]{1,0:T(8,128)(2,1)} %get-tuple-element.58.q, bf16[1024,256]{1,0:T(8,128)(2,1)} %copy-done.13, f32[512,2048]{1,0:T(8,128)} %fusion.55.grad.given, f32[2,768,8]{2,1,0:T(8,128)} %broadcast_in_dim.86.key_marks, ...), custom_call_target="tpu_custom_call" | custom-call | tf_op jit(solution)/shard_map/attend_back/pallas_call | solution.py:1432
  296.9 5.8 %add_convert_fusion = bf16[512,1024]{1,0:T(8,128)(2,1)S(1)} fusion(f32[512,1024]{1,0:T(8,128)} %copy-done.6, bf16[512,2048]{1,0:T(8,128)(2,1)} %get-tuple-element.98.refs_4_, bf16[2048,1024]{1,0:T(8,128)(2,1)} %get-tuple-element.62), kind=kOutput, calls=%fused_computation.38 | convolution fusion | flops 2148532224 | bytes 9437184 | tf_op jit(solution)/shard_map/dot_general | solution.py:82
  305.8 4.4 collective-permute-start.4
  316.0 30.1 %mix_back.1 = (bf16[512,1792]{1,0:T(8,128)(2,1)}, f32[16,1792]{1,0:T(8,128)}, f32[8,1792]{1,0:T(8,128)}, bf16[512,128]{1,0:T(8,128)(2,1)}, f32[8,128]{1,0:T(8,128)}) custom-call(bf16[512,1792]{1,0:T(8,128)(2,1)} %get-tuple-element.52.x.b.c, bf16[512,1792]{1,0:T(8,128)(2,1)} %get-tuple-element.52.x.b.c, bf16[512,1792]{1,0:T(8,128)(2,1)} %get-tuple-element.52.x.b.c, ...), custom_call_target="tpu_custom_call" | custom-call | tf_op jit(solution)/shard_map/mix_back/pallas_call | solution.py:1252
  354.2 9.8 %fusion.20 = (f32[1024]{0:T(1024)S(1)}, f32[512]{0:T(512)S(1)}, f32[512,1024]{1,0:T(8,128)S(1)}) fusion(bf16[2,256,1024]{2,1,0:T(8,128)(2,1)S(1)} %get-tuple-element.48, f32[512]{0:T(512)S(1)} %bitcast.106, f32[1024]{0:T(1024)S(1)} %get-tuple-element.108, f32[512,1024]{1,0:T(8,128)} %fusion.33, bf16[1024,4096]{1,0:T(8,128)(2,1)} %get-tuple-element.50, ...), kind=kOutput, calls=%fused_computation.33 | convolution fusion | flops 4315937280 | bytes 17838080 | tf_op jit(solution)/shard_map/dot_general | solution.py:86
  369.0 137.2 %reduce_blocks.1 = (bf16[96,128,128]{2,1,0:T(8,128)(2,1)}, f32[296,128]{1,0:T(8,128)}) custom-call(s32[768]{0:T(1024)} %get-tuple-element.90.left_at, s32[768]{0:T(1024)} %get-tuple-element.89.right_at, f32[296,128]{1,0:T(8,128)} %bitcast.100, bf16[512,1024]{1,0:T(8,128)(2,1)} %copy-done.8, bf16[512,1536]{1,0:T(8,128)(2,1)} %get-tuple-element.56.refs_1_, ...), custom_call_target="tpu_custom_call" | custom-call | tf_op jit(solution)/shard_map/reduce_blocks/pallas_call | solution.py:711
  508.1 27.5 %shampoo.1 = (f32[96,128,128]{2,1,0:T(8,128)}, f32[96,128,128]{2,1,0:T(8,128)}, f32[96,128,128]{2,1,0:T(8,128)}, f32[96,128,128]{2,1,0:T(8,128)}, bf16[96,128,128]{2,1,0:T(8,128)(2,1)}) custom-call(bf16[96,128,128]{2,1,0:T(8,128)(2,1)} %get-tuple-element.78.total, f32[96,128,128]{2,1,0:T(8,128)} %master.3, f32[96,128,128]{2,1,0:T(8,128)} %left.1, ...), custom_call_target="tpu_custom_call" | custom-call | tf_op jit(solution)/shard_map/shampoo/pallas_call | solution.py:851
  (178 shorter events, 74.0 us)
Async XLA Ops:
  6.6 114.8 %copy-start.17 = (f32[37192]{0:T(1024)S(1)}, f32[37192]{0:T(1024)}, u32[]{:S(2)}) copy-start(f32[37192]{0:T(1024)} %param.25) | copy-start | bytes 446308
  121.0 243.0 %copy-start.1 = (bf16[2,256,1024]{2,1,0:T(8,128)(2,1)}, bf16[2,256,1024]{2,1,0:T(8,128)(2,1)S(1)}, u32[]{:S(2)}) copy-start(bf16[2,256,1024]{2,1,0:T(8,128)(2,1)S(1)} %get-tuple-element.63) | copy-start | bytes 3145732
  121.9 224.2 %copy-start.8 = (bf16[512,1024]{1,0:T(8,128)(2,1)}, bf16[512,1024]{1,0:T(8,128)(2,1)S(1)}, u32[]{:S(2)}) copy-start(bf16[512,1024]{1,0:T(8,128)(2,1)S(1)} %fusion.14.refs_0_) | copy-start | bytes 3145732
  152.9 24.5 %collective-permute-start = (bf16[8,1792]{1,0:T(8,128)(2,1)}, bf16[8,1792]{1,0:T(8,128)(2,1)S(1)}, u32[]{:S(2)}, u32[]{:S(2)}) collective-permute-start(bf16[8,1792]{1,0:T(8,128)(2,1)} %slice.210), channel_id=1, source_target_pairs={{0,1},{2,3},{4,5},{6,7},{8,9},{10,11},{12,13},{14,15},{16,17},{18,... | collective-permute-start | bytes 86024 | tf_op jit(solution)/shard_map/ppermute | solution.py:1478
  160.2 15.9 %slice-start = ((f32[37192]{0:T(1024)}), f32[1536]{0:T(1024)S(1)}, s32[]{:S(2)}) async-start(f32[37192]{0:T(1024)} %param.25), calls=%async_computation | async-start | bytes 16384 | tf_op jit(solution)/shard_map/slice | solution.py:76
  160.2 27.8 %collective-permute-start.2 = (bf16[512,256]{1,0:T(8,128)(2,1)}, bf16[512,256]{1,0:T(8,128)(2,1)}, u32[]{:S(2)}, u32[]{:S(2)}) collective-permute-start(bf16[512,256]{1,0:T(8,128)(2,1)} %get-tuple-element.59), channel_id=1, source_target_pairs={{0,1},{2,3},{4,5},{6,7},{8,9},{10,11},{12,13},{14,15},{16,17},{18,... | collective-permute-start | bytes 786440 | tf_op jit(solution)/shard_map/ppermute | solution.py:1478
  165.4 9.8 %copy-start.32 = (f32[24]{0:T(128)S(1)}, f32[24]{0:T(128)}, u32[]{:S(2)}) copy-start(f32[24]{0:T(128)} %get-tuple-element.109) | copy-start | bytes 292
  186.2 18.9 %collective-permute-start.1 = (bf16[128,1536]{1,0:T(8,128)(2,1)}, bf16[128,1536]{1,0:T(8,128)(2,1)}, u32[]{:S(2)}, u32[]{:S(2)}) collective-permute-start(bf16[128,1536]{1,0:T(8,128)(2,1)} %get-tuple-element.55), channel_id=1, source_target_pairs={{0,1},{2,3},{4,5},{6,7},{8,9},{10,11},{12,13},{14,15},{16,17},{18,... | collective-permute-start | bytes 1179656 | tf_op jit(solution)/shard_map/ppermute | solution.py:1478
  229.6 24.9 %copy-start.6 = (f32[512,1024]{1,0:T(8,128)}, f32[512,1024]{1,0:T(8,128)S(1)}, u32[]{:S(2)}) copy-start(f32[512,1024]{1,0:T(8,128)S(1)} %get-tuple-element.129) | copy-start | bytes 6291460
  270.8 43.2 %collective-permute-start.5 = (bf16[128,1536]{1,0:T(8,128)(2,1)S(1)}, bf16[128,1536]{1,0:T(8,128)(2,1)}, u32[]{:S(2)}, u32[]{:S(2)}) collective-permute-start(bf16[128,1536]{1,0:T(8,128)(2,1)S(1)} %convert_element_type.119), channel_id=1, source_target_pairs={{1,0},{3,2},{5,4},{7,6},{9,8},{11,10},{13,12},{15,14},{17,16},{19,... | collective-permute-start | bytes 1179656 | tf_op jit(solution)/shard_map/ppermute | solution.py:1478
  295.6 15.4 %collective-permute-start.7 = (bf16[512,256]{1,0:T(8,128)(2,1)S(1)}, bf16[512,256]{1,0:T(8,128)(2,1)S(1)}, u32[]{:S(2)}, u32[]{:S(2)}) collective-permute-start(bf16[512,256]{1,0:T(8,128)(2,1)S(1)} %slice.142), channel_id=1, source_target_pairs={{1,0},{3,2},{5,4},{7,6},{9,8},{11,10},{13,12},{15,14},{17,16},{19,... | collective-permute-start | bytes 786440 | tf_op jit(solution)/shard_map/ppermute | solution.py:1478
  302.7 8.3 %copy-start.16 = (bf16[1024,256]{1,0:T(8,128)(2,1)S(1)}, bf16[1024,256]{1,0:T(8,128)(2,1)}, u32[]{:S(2)}) copy-start(bf16[1024,256]{1,0:T(8,128)(2,1)} %get-tuple-element.73) | copy-start | bytes 1572868
  303.9 231.7 %collective-permute-start.3 = (bf16[256,1024]{1,0:T(8,128)(2,1)}, bf16[256,1024]{1,0:T(8,128)(2,1)}, u32[]{:S(2)}, u32[]{:S(2)}) collective-permute-start(bf16[256,1024]{1,0:T(8,128)(2,1)} %get-tuple-element.106), channel_id=1, source_target_pairs={{0,0},{2,1},{1,2},{3,3},{4,4},{6,5},{5,6},{7,7},{8,8},{10,9},{9,10... | collective-permute-start | bytes 1572872 | tf_op jit(solution)/shard_map/ppermute | solution.py:1469
  305.8 229.8 %collective-permute-start.4 = (bf16[256,1024]{1,0:T(8,128)(2,1)}, bf16[256,1024]{1,0:T(8,128)(2,1)}, u32[]{:S(2)}, u32[]{:S(2)}) collective-permute-start(bf16[256,1024]{1,0:T(8,128)(2,1)} %get-tuple-element.105), channel_id=1, source_target_pairs={{2,0},{0,1},{3,2},{1,3},{6,4},{4,5},{7,6},{5,7},{10,8},{8,9},{11,1... | collective-permute-start | bytes 1572872 | tf_op jit(solution)/shard_map/ppermute | solution.py:1469
  346.1 7.1 %copy-start.24 = (f32[8,1792]{1,0:T(8,128)S(1)}, f32[8,1792]{1,0:T(8,128)}, u32[]{:S(2)}) copy-start(f32[8,1792]{1,0:T(8,128)} %get-tuple-element.76) | copy-start | bytes 172036
  351.1 2.5 collective-permute-start.6
  354.2 9.8 %copy-start.7 = (f32[512,1024]{1,0:T(8,128)S(1)}, f32[512,1024]{1,0:T(8,128)}, u32[]{:S(2)}) copy-start(f32[512,1024]{1,0:T(8,128)} %copy-done.6) | copy-start | bytes 6291460
  354.2 9.8 %copy-start.10 = (f32[512,1024]{1,0:T(8,128)S(1)}, f32[512,1024]{1,0:T(8,128)}, u32[]{:S(2)}) copy-start(f32[512,1024]{1,0:T(8,128)} %copy-done.9) | copy-start | bytes 6291460
  354.2 9.8 %copy-start.26 = (f32[512]{0:T(512)S(1)}, f32[512]{0:T(512)}, u32[]{:S(2)}) copy-start(f32[512]{0:T(512)} %copy-done.25) | copy-start | bytes 6148
  366.3 172.0 %collective-permute-start.8 = (bf16[256,1024]{1,0:T(8,128)(2,1)}, bf16[256,1024]{1,0:T(8,128)(2,1)S(1)}, u32[]{:S(2)}, u32[]{:S(2)}) collective-permute-start(bf16[256,1024]{1,0:T(8,128)(2,1)} %get-tuple-element.102), channel_id=1, source_target_pairs={{0,0},{2,1},{1,2},{3,3},{4,4},{6,5},{5,6},{7,7},{8,8},{10,9},{9,10... | collective-permute-start | bytes 1572872 | tf_op jit(solution)/shard_map/ppermute | solution.py:1469
  368.2 170.1 %collective-permute-start.9 = (bf16[256,1024]{1,0:T(8,128)(2,1)}, bf16[256,1024]{1,0:T(8,128)(2,1)}, u32[]{:S(2)}, u32[]{:S(2)}) collective-permute-start(bf16[256,1024]{1,0:T(8,128)(2,1)} %get-tuple-element.101), channel_id=1, source_target_pairs={{2,0},{0,1},{3,2},{1,3},{6,4},{4,5},{7,6},{5,7},{10,8},{8,9},{11,1... | collective-permute-start | bytes 1572872 | tf_op jit(solution)/shard_map/ppermute | solution.py:1469
  369.0 137.3 %copy-start.18 = (f32[37192]{0:T(1024)S(1)}, f32[37192]{0:T(1024)}, u32[]{:S(2)}) copy-start(f32[37192]{0:T(1024)} %param.25) | copy-start | bytes 446308
  369.0 137.3 %copy-start.20 = (f32[37192]{0:T(1024)S(1)}, f32[37192]{0:T(1024)}, u32[]{:S(2)}) copy-start(f32[37192]{0:T(1024)} %param.26) | copy-start | bytes 446308
  369.0 137.3 %copy-start.21 = (f32[37192]{0:T(1024)S(1)}, f32[37192]{0:T(1024)}, u32[]{:S(2)}) copy-start(f32[37192]{0:T(1024)} %param.27) | copy-start | bytes 446308
  (23 other events, 67.1 us)

commit v3 on v2

--- a/solution.py
+++ b/solution.py
@@ -108,6 +108,8 @@
 
 MESH = pl.DeviceIdType.MESH
 CORES = 2
+PIECES = 3
+APART = 5 / 16
 
 
 def grid_of(mesh):
@@ -120,8 +122,9 @@
 
 def parts_of(slots, tall):
     half = slots // CORES
-    lone = half * 17 // 48 if tall == 2 and half >= 16 else 0
-    return half, lone, half - lone
+    size = half // PIECES
+    lone = round(size * APART) if tall == 2 and size >= 8 else 0
+    return half, size, lone, size - lone
 
 
 def place(grid):
@@ -134,13 +137,13 @@
                   sem_own, sem_load, sz, rz, sx, rx, sy, ry, sc, rc, s_rows, r_rows, s_docs, r_docs):
     wide, tall, deep = grid
     x, y, z, c = place(grid)
-    half, lone, bulk = parts_of(slots, tall)
+    half, size, lone, bulk = parts_of(slots, tall)
     me = z * wide + x
     seq = y * CORES + c
     base = c * half
-    bulk_at = base + y * (half - bulk)
-    lone_at = base + y * bulk
-    other_at = base + (1 - y) * bulk if lone else base
+    bulk_at = y * (size - bulk)
+    lone_at = y * bulk
+    other_at = (1 - y) * bulk if lone else 0
     mate = y * CORES + (1 - c)
     over = (tall - 1 - y) * CORES + c
     peers = tall * CORES
@@ -155,10 +158,10 @@
 
     barrier = pltpu.get_barrier_semaphore()
     count = jnp.int32(0)
-    for axis, at, size in (("z", z, deep), ("x", x, wide)):
+    for step_by, at, length in ((wide, z, deep), (1, x, wide)):
         for step in (1, -1):
-            ok = (at + step >= 0) & (at + step < size)
-            there = me + step * (wide if axis == "z" else 1)
+            ok = (at + step >= 0) & (at + step < length)
+            there = me + step * step_by
 
             @pl.when(ok)
             def _(there=there):
@@ -168,171 +171,207 @@
     for k in range(1, peers):
         pl.semaphore_signal(barrier, inc=1, device_id=(me, (seq + k) % peers), device_id_type=MESH)
     pl.semaphore_wait(barrier, count + (peers - 1))
-    sent = []
-
-    def send(ok, source, target, send_sem, recv_sem, device):
-        copy = pltpu.make_async_remote_copy(
-            src_ref=source, dst_ref=target, send_sem=send_sem, recv_sem=recv_sem,
-            device_id=device, device_id_type=MESH,
-        )
-
-        @pl.when(ok)
-        def _():
-            copy.start()
-
-        sent.append((ok, copy))
-
-    def arrived(ok, target, recv_sem):
-        copy = pltpu.make_async_remote_copy(
-            src_ref=target, dst_ref=target, send_sem=sem_own.at[0], recv_sem=recv_sem,
-            device_id=(me, seq), device_id_type=MESH,
-        )
-
-        @pl.when(ok)
-        def _():
-            copy.wait_recv()
-
+    both = ((0, 1), (1, -1))
     yes = jnp.bool_(True)
 
+    def piece(shard, at, length):
+        return out.at[shard, pl.ds(at, length)]
+
+    def run(begin_it):
+        def send(ok, source, target, send_sem, recv_sem, device):
+            copy = pltpu.make_async_remote_copy(
+                src_ref=source, dst_ref=target, send_sem=send_sem, recv_sem=recv_sem,
+                device_id=device, device_id_type=MESH,
+            )
+
+            @pl.when(ok)
+            def _():
+                if begin_it:
+                    copy.start()
+                else:
+                    copy.wait_send()
+
+        def arrived(ok, target, recv_sem):
+            if begin_it:
+                copy = pltpu.make_async_remote_copy(
+                    src_ref=target, dst_ref=target, send_sem=sem_own.at[0], recv_sem=recv_sem,
+                    device_id=(me, seq), device_id_type=MESH,
+                )
+
+                @pl.when(ok)
+                def _():
+                    copy.wait_recv()
+
+        def pass_on(ok, shard, sub):
+            at = base + sub * size
+            mine = piece(shard, at + bulk_at, bulk)
+            send(ok, mine, mine, sc.at[0, shard, sub], rc.at[0, shard, sub], (me, mate))
+            if lone:
+                mine = piece(shard, at + lone_at, lone)
+                send(ok, mine, mine, sy.at[shard, sub], ry.at[shard, sub], (me, over))
+
+        def along_x(ok, zs, dirs, hop, sub, own):
+            for d, step in dirs:
+                shard = zs * wide + x - step * hop
+                go = ok & (x + step >= 0) & (x + step < wide)
+                at = base + sub * size + bulk_at
+                source = src.at[pl.ds(at, bulk)] if own else piece(shard, at, bulk)
+                send(go, source, piece(shard, at, bulk), sx.at[d, hop, zs, sub], rx.at[d, hop + 1, zs, sub], (me + step, seq))
+
+        def columns(s):
+            return [(yes, z)] if s == 0 else [((z - step * s >= 0) & (z - step * s < deep), z - step * s) for _, step in both]
+
+        def x_in(s, hop, sub):
+            for ok, zs in columns(s):
+                for d, step in both:
+                    from_x = x - step * hop
+                    come = ok & (from_x >= 0) & (from_x < wide)
+                    shard = zs * wide + from_x
+                    arrived(come, piece(shard, base + sub * size + bulk_at, bulk), rx.at[d, hop, zs, sub])
+                    along_x(come, zs, ((d, step),), hop, sub, False)
+                    pass_on(come, shard, sub)
+
+        def y_in(ok, shard, sub):
+            if lone:
+                mine = piece(shard, base + sub * size + other_at, lone)
+                arrived(ok, mine, ry.at[shard, sub])
+                send(ok, mine, mine, sc.at[1, shard, sub], rc.at[1, shard, sub], (me, mate))
+
+        def y_all(s, sub):
+            for ok, zs in columns(s):
+                if s > 0:
+                    y_in(ok, zs * wide + x, sub)
+                for hop in range(1, wide):
+                    for _, step in both:
+                        from_x = x - step * hop
+                        y_in(ok & (from_x >= 0) & (from_x < wide), zs * wide + from_x, sub)
+
+        def z_step(s, sub):
+            for d, step in both:
+                zs = z - step * s
+                ok = (zs >= 0) & (zs < deep)
+                shard = zs * wide + x
+                at = base + sub * size + bulk_at
+                mine = piece(shard, at, bulk)
+                if s:
+                    arrived(ok, mine, rz.at[d, s, sub])
+                go = ok & (z + step >= 0) & (z + step < deep)
+                source = mine if s else src.at[pl.ds(at, bulk)]
+                if s + 1 < deep:
+                    send(go, source, mine, sz.at[d, s, sub], rz.at[d, s + 1, sub], (me + step * wide, seq))
+                if s:
+                    along_x(ok, zs, both, 0, sub, False)
+                    pass_on(ok, shard, sub)
+            if s == 0:
+                along_x(yes, z, both, 0, sub, True)
+
+        for s in range(deep):
+            def one(sub, _, s=s):
+                z_step(s, sub)
+                if s:
+                    for hop in range(1, wide):
+                        x_in(s - 1, hop, sub)
+                if s >= 2:
+                    y_all(s - 2, sub)
+                return 0
+
+            lax.fori_loop(0, PIECES, one, 0)
+            if s == 0:
+                local(begin_it, send, arrived)
+
+        def last_x(sub, _):
+            for hop in range(1, wide):
+                x_in(deep - 1, hop, sub)
+            if deep > 1:
+                y_all(deep - 2, sub)
+            return 0
+
+        def last_y(sub, _):
+            y_all(deep - 1, sub)
+            return 0
+
+        lax.fori_loop(0, PIECES, last_x, 0)
+        lax.fori_loop(0, PIECES, last_y, 0)
+
+    def convert(k):
+        part, copy = loads[k]
+        copy.wait()
+        base_at = ((c + k) % CORES) * half
+
+        def one(i, _):
+            src[base_at + i] = wide_own[base_at + i].astype(src.dtype)
+            return 0
+
+        lax.fori_loop(0, half, one, 0, unroll=2)
+
+    keep = pltpu.make_async_copy(src, out.at[me], sem_load.at[0])
     at_home = []
     for t in range(micro):
         m = (seq + t) % micro
         there = m * each + seq // micro
         for k, (source, target) in enumerate(((tokens, rows), (cotangent, given))):
             place_to = target.at[seq % micro]
-            send(there != seq, source.at[m], place_to, s_rows.at[k, t], r_rows.at[k, seq % micro], (me, there))
             take = pltpu.make_async_copy(source.at[m], bounce.at[k], sem_own.at[k])
             put = pltpu.make_async_copy(bounce.at[k], place_to, sem_own.at[k])
             at_home.append((there == seq, take, put))
 
-            @pl.when(there == seq)
-            def _(take=take):
-                take.start()
-
-    labels[seq] = docs[...]
-    for k in range(1, peers):
-        there = (seq + k) % peers
-        send(yes, docs, labels.at[seq], s_docs.at[k], r_docs.at[seq], (me, there))
-
-    def convert(k):
-        part, copy = loads[k]
-        copy.wait()
-        base_at = ((c + k) % CORES) * half
-
-        def one(i, _):
-            src[base_at + i] = wide_own[base_at + i].astype(src.dtype)
-            return 0
-
-        lax.fori_loop(0, half, one, 0, unroll=2)
-
-    convert(0)
-
-    def piece(shard, at, size):
-        return out.at[shard, pl.ds(at, size)]
-
-    def pass_on(ok, shard):
-        send(ok, piece(shard, bulk_at, bulk), piece(shard, bulk_at, bulk), sc.at[0, shard], rc.at[0, shard], (me, mate))
-        if lone:
-            send(ok, piece(shard, lone_at, lone), piece(shard, lone_at, lone), sy.at[shard], ry.at[shard], (me, over))
-
-    def along_x(ok, zs, dirs, hop, own):
-        for d, step in dirs:
-            shard = zs * wide + x - step * hop
-            go = ok & (x + step >= 0) & (x + step < wide)
-            source = src.at[pl.ds(bulk_at, bulk)] if own else piece(shard, bulk_at, bulk)
-            send(go, source, piece(shard, bulk_at, bulk), sx.at[d, hop, zs], rx.at[d, hop + 1, zs], (me + step, seq))
-
-    both = ((0, 1), (1, -1))
-
-    def columns(s):
-        return [(yes, z)] if s == 0 else [((z - step * s >= 0) & (z - step * s < deep), z - step * s) for _, step in both]
-
-    def x_in(s, hop):
-        for ok, zs in columns(s):
-            for d, step in both:
-                from_x = x - step * hop
-                come = ok & (from_x >= 0) & (from_x < wide)
-                shard = zs * wide + from_x
-                arrived(come, piece(shard, bulk_at, bulk), rx.at[d, hop, zs])
-                along_x(come, zs, ((d, step),), hop, False)
-                pass_on(come, shard)
-
-    def y_in(ok, shard):
-        if lone:
-            arrived(ok, piece(shard, other_at, lone), ry.at[shard])
-            send(ok, piece(shard, other_at, lone), piece(shard, other_at, lone), sc.at[1, shard], rc.at[1, shard], (me, mate))
-
-    def y_all(s):
-        for ok, zs in columns(s):
-            if s > 0:
-                y_in(ok, zs * wide + x)
-            for hop in range(1, wide):
-                for _, step in both:
-                    from_x = x - step * hop
-                    y_in(ok & (from_x >= 0) & (from_x < wide), zs * wide + from_x)
-
-    for s in range(deep):
-        for d, step in both:
-            zs = z - step * s
-            ok = (zs >= 0) & (zs < deep)
-            shard = zs * wide + x
-            if s:
-                arrived(ok, piece(shard, bulk_at, bulk), rz.at[d, s])
-            go = ok & (z + step >= 0) & (z + step < deep)
-            source = piece(shard, bulk_at, bulk) if s else src.at[pl.ds(bulk_at, bulk)]
-            if s + 1 < deep:
-                send(go, source, piece(shard, bulk_at, bulk), sz.at[d, s], rz.at[d, s + 1], (me + step * wide, seq))
-            if s:
-                along_x(ok, zs, both, 0, False)
-                pass_on(ok, shard)
-        if s == 0:
-            along_x(yes, z, both, 0, True)
+    def local(begin_it, send, arrived):
+        for t in range(micro):
+            m = (seq + t) % micro
+            there = m * each + seq // micro
+            for k, (source, target) in enumerate(((tokens, rows), (cotangent, given))):
+                send(there != seq, source.at[m], target.at[seq % micro], s_rows.at[k, t], r_rows.at[k, seq % micro], (me, there))
+        if begin_it:
+            labels[seq] = docs[...]
+        for k in range(1, peers):
+            send(yes, docs, labels.at[seq], s_docs.at[k], r_docs.at[seq], (me, (seq + k) % peers))
+        if begin_it:
+            for ok, take, _ in at_home:
+                @pl.when(ok)
+                def _(take=take):
+                    take.start()
             convert(1)
-            keep = pltpu.make_async_copy(src, out.at[me], sem_load.at[0])
             keep.start()
             for ok, take, put in at_home:
                 @pl.when(ok)
                 def _(take=take, put=put):
                     take.wait()
                     put.start()
-        else:
-            for hop in range(1, wide):
-                x_in(s - 1, hop)
-        if s >= 2:
-            y_all(s - 2)
-    for hop in range(1, wide):
-        x_in(deep - 1, hop)
-    for s in range(max(deep - 2, 0), deep):
-        y_all(s)
+
+    convert(0)
+    run(True)
     keep.wait()
     for ok, take, put in at_home:
         @pl.when(ok)
         def _(put=put):
             put.wait()
+
+    def came(ok, target, recv_sem):
+        @pl.when(ok)
+        def _():
+            pltpu.make_async_remote_copy(
+                src_ref=target, dst_ref=target, send_sem=sem_own.at[0], recv_sem=recv_sem,
+                device_id=(me, seq), device_id_type=MESH,
+            ).wait_recv()
+
     for q in range(micro):
         source = seq % each * micro + q
         for k, target in enumerate((rows, given)):
-            arrived(source != seq, target.at[q], r_rows.at[k, q])
+            came(source != seq, target.at[q], r_rows.at[k, q])
     for k in range(1, peers):
         source = (seq + k) % peers
-        arrived(yes, labels.at[source], r_docs.at[source])
-
-    mate_base = (1 - c) * half
-    mate_bulk = mate_base + y * (half - bulk)
-    mate_other = mate_base + (1 - y) * bulk if lone else mate_base
-
-    def last(shard, _):
-        ok = shard != me
-        arrived(ok, piece(shard, mate_bulk, bulk), rc.at[0, shard])
+        came(yes, labels.at[source], r_docs.at[source])
+
+    def last(i, _):
+        shard, sub = i // PIECES, i % PIECES
+        at = (1 - c) * half + sub * size
+        came(shard != me, piece(shard, at + bulk_at, bulk), rc.at[0, shard, sub])
         if lone:
-            arrived(ok, piece(shard, mate_other, lone), rc.at[1, shard])
+            came(shard != me, piece(shard, at + other_at, lone), rc.at[1, shard, sub])
         return 0
 
-    lax.fori_loop(0, wide * deep, last, 0)
-    for ok, copy in sent:
-        @pl.when(ok)
-        def _(copy=copy):
-            copy.wait_send()
+    lax.fori_loop(0, wide * deep * PIECES, last, 0)
+    run(False)
 
 
 def gather_blocks(grid, master, tokens, cotangent, docs):
@@ -357,13 +396,13 @@
         scratch_shapes=[
             pltpu.VMEM(master.shape, master.dtype), pltpu.VMEM(master.shape, low), pltpu.VMEM((2,) + tokens.shape[1:], low),
             sem((2,)), sem((CORES,)),
-            sem((2, deep)), sem((2, deep + 1)),
-            sem((2, wide, deep)), sem((2, wide + 1, deep)),
-            sem((n,)), sem((n,)),
-            sem((2, n)), sem((2, n)),
+            sem((2, deep, PIECES)), sem((2, deep + 1, PIECES)),
+            sem((2, wide, deep, PIECES)), sem((2, wide + 1, deep, PIECES)),
+            sem((n, PIECES)), sem((n, PIECES)),
+            sem((2, n, PIECES)), sem((2, n, PIECES)),
             sem((2, micro)), sem((2, micro)), sem((peers,)), sem((peers,)),
         ],
-        compiler_params=pltpu.CompilerParams(collective_id=0, has_side_effects=True, vmem_limit_bytes=32 << 20),
+        compiler_params=pltpu.CompilerParams(collective_id=0, has_side_effects=True, vmem_limit_bytes=60 << 20),
         name="gather_blocks",
     )(master, tokens, cotangent, docs)
 
@@ -827,31 +866,38 @@
     )(table, blocks)
 
 
-SHAMPOO = 8
+SHAMPOO = 24
 
 
 def shampoo_kernel(norm, total, master, left, right, left_root, right_root, grad, new_left, new_right, new_master, low):
-    for i in range(SHAMPOO):
-        g = total[i]
-        value = g.astype(F32) * norm
-        grad[i] = value
-        new_left[i] = 0.5 * left[i] + dot_nt(g, g) * (0.5 * norm * norm / BS)
-        new_right[i] = 0.5 * right[i] + dot_tn(g, g) * (0.5 * norm * norm / BS)
-        inner = dot(g, right_root[i].astype(BF16))
-        moved = dot(left_root[i].astype(BF16), inner.astype(BF16)) * (LR_MATRIX * norm)
-        fresh = master[i] - moved
-        new_master[i] = fresh
-        low[i] = fresh.astype(BF16)
+    scale = 0.5 * norm * norm / BS
+    for i in range(0, total.shape[0], 2):
+        pair = (i, i + 1)
+        rows = jnp.concatenate([total[k] for k in pair], axis=0)
+        cols = jnp.concatenate([total[k] for k in pair], axis=1)
+        outer = dot_nt(rows, rows) * scale
+        inner = dot_tn(cols, cols) * scale
+        moved = dot(rows, jnp.concatenate([right_root[k] for k in pair], axis=1).astype(BF16))
+        moved = jnp.concatenate([moved[:BS, :BS], moved[BS:, BS:]], axis=1).astype(BF16)
+        moved = dot(jnp.concatenate([left_root[k] for k in pair], axis=0).astype(BF16), moved) * (LR_MATRIX * norm)
+        for k, at in zip(pair, (slice(0, BS), slice(BS, 2 * BS))):
+            grad[k] = total[k].astype(F32) * norm
+            new_left[k] = 0.5 * left[k] + outer[at, at]
+            new_right[k] = 0.5 * right[k] + inner[at, at]
+            fresh = master[k] - moved[at, at]
+            new_master[k] = fresh
+            low[k] = fresh.astype(BF16)
 
 
 def shampoo(norm, total, master, left, right, left_root, right_root):
     slots = total.shape[0]
-    spec = pl.BlockSpec((SHAMPOO, BS, BS), lambda i: (i, 0, 0))
+    each = math.gcd(slots, SHAMPOO)
+    spec = pl.BlockSpec((each, BS, BS), lambda i: (i, 0, 0))
     full = jax.ShapeDtypeStruct(master.shape, F32)
     return pl.pallas_call(
         functools.partial(shampoo_kernel, norm),
         out_shape=(full, full, full, full, jax.ShapeDtypeStruct(master.shape, BF16)),
-        grid=(slots // SHAMPOO,),
+        grid=(slots // each,),
         in_specs=[spec] * 6,
         out_specs=(spec,) * 5,
         compiler_params=kernel_params(),
@@ -911,14 +957,15 @@
         step = 256
         for q in range(0, ref.shape[1], step):
             cols = slice(at + q, at + q + step)
-            own = ref[:, q : q + step].astype(BF16).astype(F32)
+            own = ref[:, q : q + step].astype(F32)
             extended = jnp.concatenate([halo[:, cols].astype(F32), own], axis=0)
             value = conv_tile(extended, taps[:, cols], mark, tokens)
             xbc[:, cols] = (value * sigmoid(value)).astype(BF16)
     delta, decay, sums = chunk_decays(raw[...], params[...])
     decays[0] = delta
     decays[1] = sums
-    decays_t[...] = sums.T
+    for i in range(tokens // BLOCK):
+        decays_t[i] = sums[i * BLOCK : (i + 1) * BLOCK].T
     spread = spread_matrix()
     total = jnp.zeros((NSTATE, INNER), F32)
     product = jnp.ones((1, LANES), F32)
@@ -941,7 +988,7 @@
         out_shape=(
             jax.ShapeDtypeStruct((tokens, CHANNELS), BF16),
             jax.ShapeDtypeStruct((2, tokens, LANES), F32),
-            jax.ShapeDtypeStruct((LANES, tokens), F32),
+            jax.ShapeDtypeStruct((tokens // BLOCK, LANES, BLOCK), F32),
             jax.ShapeDtypeStruct((NSTATE, INNER), BF16),
             jax.ShapeDtypeStruct((8, LANES), F32),
         ),
@@ -1005,13 +1052,13 @@
         sums = wide_sums[at, cols]
         total = jnp.zeros((BLOCK, LANES), F32)
         for a, part in enumerate(halves(scaled)):
-            row = decays_t[pl.ds(2 * j + a, 1), at]
+            row = decays_t[i, pl.ds(2 * j + a, 1), :]
             weight = near[i] * jnp.exp(jnp.minimum(pair_column(sums, a) - row, 0.0))
             total = total + dot(weight.astype(BF16), part)
         carried = dot(c[at], state[...].astype(BF16))
         total = total + carried * jnp.exp(sums) * marks[at, 4:5] + skip[0:1, cols] * tile
         y[at] = total
-        gate = z[at]
+        gate = z[at].astype(F32)
         gate = total * gate * sigmoid(gate)
         gated[at, cols] = gate
         squares[at] += gate * gate
@@ -1062,13 +1109,13 @@
 
 def gate_back_kernel(grad, y, z, gain, c, decays, marks, g_y, g_z, g_gain, g_state):
     step = pl.program_id(0)
-    value, gate = y[...], z[...]
+    value, gate = y[...], z[...].astype(F32)
     opened = sigmoid(gate)
     swish = gate * opened
     gated = value * swish
     scale = lax.rsqrt(jnp.mean(gated * gated, axis=1, keepdims=True) + EPS)
     unit = gated * scale
-    given = grad[...]
+    given = grad[...].astype(F32)
     scaled = given * gain[0:1, :]
     g_gated = scale * (scaled - unit * jnp.mean(scaled * unit, axis=1, keepdims=True))
     fresh = g_gated * swish
@@ -1184,7 +1231,7 @@
         ends[i] += collect(jnp.broadcast_to(jnp.sum(states[i + 1] * state[...], axis=0, keepdims=True), (8, LANES)))
         total = end * dot(b[at], low_state)
         for a, (part, grad) in enumerate(zip(halves(low_scaled), halves(given))):
-            row = decays_t[pl.ds(2 * j + a, 1), at]
+            row = decays_t[i, pl.ds(2 * j + a, 1), :]
             decay = jnp.exp(jnp.minimum(row - pair_column(sums, a), 0.0))
             total = total + dot((near[i] * decay).astype(BF16), grad)
             g_near[i] += decay * dot_nt(part, given)
@@ -1201,7 +1248,7 @@
         state[...] = keep[i, 0:1, cols] * state[...] + dot(c_t[i], reached)
 
     mark = marks[...]
-    own = proj_x[...].astype(BF16).astype(F32)
+    own = proj_x[...].astype(F32)
     extended = jnp.concatenate([halo[:, cols].astype(F32), own], axis=0)
     result, weights = conv_back(jnp.concatenate(g_x[::-1], axis=0), extended, taps[:, cols], mark, tokens)
     g_rim[:HALO, cols] = result[:HALO]
@@ -1220,7 +1267,7 @@
             g_c[at] += dot(grad.T.astype(BF16), b[at])
         for k, ref in enumerate((g_b, g_c)):
             at = slice(INNER + k * NSTATE, INNER + (k + 1) * NSTATE)
-            own = proj_bc[:, k * NSTATE : (k + 1) * NSTATE].astype(BF16).astype(F32)
+            own = proj_bc[:, k * NSTATE : (k + 1) * NSTATE].astype(F32)
             extended = jnp.concatenate([halo[:, at].astype(F32), own], axis=0)
             result, weights = conv_back(ref[...], extended, taps[:, at], mark, tokens)
             g_rim[:HALO, at] = result[:HALO]
@@ -1306,8 +1353,8 @@
     queries, (k, v, cosine, sine, q_out, kv_out) = refs[:QPAIRS], refs[QPAIRS:]
     cos, sin = cosine[...], sine[...]
     for p, q in enumerate(queries):
-        q_out[:, p * LANES : (p + 1) * LANES] = turn(q[...], cos, sin).astype(BF16)
-    kv_out[:, :KDIM] = turn(k[...], cos, sin).astype(BF16)
+        q_out[:, p * LANES : (p + 1) * LANES] = turn(q[...].astype(F32), cos, sin).astype(BF16)
+    kv_out[:, :KDIM] = turn(k[...].astype(F32), cos, sin).astype(BF16)
     kv_out[:, KDIM:] = v[...].astype(BF16)
 
 
@@ -1402,7 +1449,7 @@
     cols = lane_index((window, QBLOCK))
     seen = (rows <= cols + DOC_MOST) & (key_marks[0, :, 0:1] == query_labels[0:1, :])
     at = pl.ds(start, window)
-    query, grad = q[...], given[...].astype(BF16)
+    query, grad = q[...], given[...]
     total = jnp.zeros((QBLOCK, LANES), F32)
     for a, (query_part, grad_part) in enumerate(zip(halves(query), halves(grad))):
         key = keys[group, a, at, :]
@@ -1467,8 +1514,13 @@
     for t in range(micro):
         pairs = [(((j + t) % micro) * each + j // micro, j) for j in range(seq)]
         pieces.append(lax.ppermute(lax.dynamic_index_in_dim(cut, (order - t) % micro, 0, False), "seq", pairs))
-    stacked = jnp.stack(pieces)
-    return jnp.stack([lax.dynamic_index_in_dim(stacked, (m - here) % micro, 0, False) for m in range(micro)])
+    results = []
+    for m in range(micro):
+        chosen = pieces[0]
+        for t in range(1, micro):
+            chosen = jnp.where((m - here) % micro == t, pieces[t], chosen)
+        results.append(chosen)
+    return jnp.stack(results)
 
 
 def along(value, steps, micro):
@@ -1535,9 +1587,9 @@
 
     inputs = rows.astype(F32)
     normed_in = (inputs * rms_scale(inputs) * gain_in).astype(BF16)
-    proj = dot(normed_in, w_in)
+    proj = dot(normed_in, w_in).astype(BF16)
     raw = dot(normed_in, w_dt)
-    halo = along(proj[count - HALO :, INNER : INNER + CHANNELS].astype(BF16), 1, micro)
+    halo = along(proj[count - HALO :, INNER : INNER + CHANNELS], 1, micro)
     q, kv = rope_all(proj, cosine, sine)
     xbc, decays, decays_t, state, factor = mix_first(proj, halo, taps, params, raw, marks)
     past = min(each - 1, -(-DOC_MOST // count))
@@ -1553,8 +1605,8 @@
     context, stats = attend(q, reach, key_labels, marks)
     hidden = inputs + (dot(normed_ssm, w_out[:INNER]) + dot(context, w_out[INNER:]))
     normed_mid = (hidden * rms_scale(hidden) * gain_mid).astype(BF16)
-    both = dot(normed_mid, w_ff)
-    gate, upper = both[:, :FF], both[:, FF:]
+    both = dot(normed_mid, w_ff).astype(BF16)
+    gate, upper = both[:, :FF].astype(F32), both[:, FF:].astype(F32)
     opened = sigmoid(gate)
     mixed = (gate * opened * upper).astype(BF16)
     layer_out = ungroup((hidden + dot(mixed, w_down)).astype(BF16), micro)
@@ -1572,7 +1624,7 @@
     g_values, g_gain_mid = norm_back(dot_nt(g_ff, w_ff), hidden, gain_mid)
     g_hidden = given.astype(F32) + g_values
     hidden_low = g_hidden.astype(BF16)
-    g_out = dot_nt(hidden_low, w_out)
+    g_out = dot_nt(hidden_low, w_out).astype(BF16)
     g_y, g_z, g_gain_mix, g_state = gate_back(g_out, y, proj, wide_gain, xbc, decays, marks)
     low_state = g_state.astype(BF16)
     leaving = along(low_state, 1 - each, micro).astype(F32) if each > 1 else jnp.zeros(state.shape, F32)

time: 552 us -> 521 us (0.944)
  local copies, waits for them, and re-layouts: 34.4 us -> 20 us
  Pallas kernels: 394 us -> 381 us
  matrix products: 63.5 us -> 56.6 us
    unnamed x76 -> x66, local copies, waits for them, and re-layouts: 13.6 us -> 3.32 us
    pallas_call x1, Pallas kernels: 27.5 us -> 20.6 us  [shampoo(): pl.pallas_call(functools.partial(shampoo_kernel, norm), out_shape=(full,...]
  transfers between devices with their start and end apart: 10 -> 10, of which waited for: 0 -> 0; matrix products, arithmetic and copies ran while one was open for 11% -> 9% of each run, Pallas kernels for 44% -> 42%
where the time goes in v3:
time: 521 us; the launch traced here: 511 us
  Pallas kernels  381 us (73%)
  matrix products  56.6 us (11%)
  other arithmetic  29.2 us (6%)
  starting transfers between devices  21.5 us (4%)
  local copies, waits for them, and re-layouts  20 us (4%)
    pallas_call x1, Pallas kernels, reduce_blocks(): pl.pallas_call(functools.partial(reduce_kernel, grid, slots, widths), out...  138 us
    pallas_call x1, Pallas kernels, gather_blocks(): pl.pallas_call(functools.partial(gather_kernel, grid, slots), out_shape=(...  109 us
    pallas_call x1, Pallas kernels, mix_back(): pl.pallas_call(mix_back_kernel, out_shape=(jax.ShapeDtypeStruct((tokens,...  29.8 us
    dot_general x5, matrix products, dot_nt(): lax.dot_general(left, right, (((1,), (1,)), ((), ())), preferred_element_...  28 us
    dot_general x6, matrix products, dot(): return jnp.dot(left, right, preferred_element_type=F32, precision=precision)  27.3 us
    pallas_call x1, Pallas kernels, shampoo(): pl.pallas_call(functools.partial(shampoo_kernel, norm), out_shape=(full,...  20.6 us
    pallas_call x1, Pallas kernels, assemble(): pl.pallas_call(assemble_kernel, out_shape=tuple((jax.ShapeDtypeStruct(sha...  18.3 us
    pallas_call x1, Pallas kernels, attend_back(): pl.pallas_call(attend_back_kernel, out_shape=(jax.ShapeDtypeStruct((token...  17.3 us
  transfers between devices with their start and end apart: 10, of which 0 were waited for; matrix products, arithmetic and copies ran while one was open for 9% of the time, Pallas kernels for 42%

profile of v3, /device:TPU:11, one launch (start us, length us, event | category | flops | bytes accessed | tf_op | source)
XLA Modules:
  0.0 510.6 jit_solution(6229583194998069804)
XLA Ops:
  1.4 109.0 %gather_blocks.1 = (bf16[8,96,128,128]{3,2,1,0:T(8,128)(2,1)}, bf16[2,256,1024]{2,1,0:T(8,128)(2,1)}, bf16[2,256,1024]{2,1,0:T(8,128)(2,1)}, s32[4,2,256]{2,1,0:T(2,128)}) custom-call(f32[96,128,128]{2,1,0:T(8,128)} %master.3, bf16[2,256,1024]{2,1,0:T(8,128)(2,1)} %tokens.1, bf16[2,256,1024]{2,1,0:T(8,128)(2,1)} %cotangent.1, s32[2,256]{1,0:T(2,128)} %docs.1), custom_call_target="tpu_custom_call" | custom-call | tf_op jit(solution)/shard_map/gather_blocks/pallas_call | solution.py:387
  116.7 18.3 %assemble.1 = (bf16[1024,4096]{1,0:T(8,128)(2,1)}, bf16[2048,1024]{1,0:T(8,128)(2,1)}, bf16[1024,4096]{1,0:T(8,128)(2,1)}, bf16[2048,1024]{1,0:T(8,128)(2,1)}) custom-call(s32[768]{0:T(1024)} %get-tuple-element.91.table, bf16[768,128,128]{2,1,0:T(8,128)(2,1)} %bitcast.99), custom_call_target="tpu_custom_call" | custom-call | tf_op jit(solution)/shard_map/assemble/pallas_call | solution.py:853
  135.0 9.4 %convolution_convert_fusion.1.proj_x.proj_bc.z.refs_0_.refs_1_.refs_2_.refs_3_.refs_4_.refs_5_ = bf16[512,4096]{1,0:T(8,128)(2,1)} fusion(bf16[512,1024]{1,0:T(8,128)(2,1)S(1)} %fusion.22.refs_0_, bf16[1024,4096]{1,0:T(8,128)(2,1)} %get-tuple-element.50), kind=kOutput, calls=%fused_computation.4 | convolution fusion | flops 4297064448 | bytes 13631488 | tf_op jit(solution)/shard_map/dot_general | solution.py:82
  146.7 2.7 rope.1
  160.6 7.7 %mix_first.1 = (bf16[512,1792]{1,0:T(8,128)(2,1)}, f32[2,512,128]{2,1,0:T(8,128)}, f32[2,128,256]{2,1,0:T(8,128)}, bf16[128,1536]{1,0:T(8,128)(2,1)}, f32[8,128]{1,0:T(8,128)}) custom-call(bf16[512,4096]{1,0:T(8,128)(2,1)} %convolution_convert_fusion.1.proj_x.proj_bc.z.refs_0_.refs_1_.refs_2_.refs_3_.refs_4_.refs_5_, ...), custom_call_target="tpu_custom_call" | custom-call | tf_op jit(solution)/shard_map/mix_first/pallas_call | solution.py:986
  170.8 10.9 %attend.1 = (bf16[512,512]{1,0:T(8,128)(2,1)}, f32[4,8,512]{2,1,0:T(8,128)}) custom-call(bf16[512,512]{1,0:T(8,128)(2,1)} %get-tuple-element.58.q, bf16[1024,256]{1,0:T(8,128)(2,1)} %copy-done.8, f32[2,8,768]{2,1,0:T(8,128)} %broadcast_in_dim.46.key_labels, f32[512,128]{1,0:T(8,128)} %pad.22.marks), custom_call_target="tpu_custom_call" | custom-call | tf_op jit(solution)/shard_map/attend/pallas_call | solution.py:1420
  181.7 3.4 fusion.35
  186.7 16.8 %mix_second.1 = (f32[512,1536]{1,0:T(8,128)}, bf16[512,1536]{1,0:T(8,128)(2,1)}, f32[3,128,1536]{2,1,0:T(8,128)}) custom-call(bf16[512,1792]{1,0:T(8,128)(2,1)} %get-tuple-element.52.x.b.c, bf16[512,1792]{1,0:T(8,128)(2,1)} %get-tuple-element.52.x.b.c, bf16[512,1792]{1,0:T(8,128)(2,1)} %get-tuple-element.52.x.b.c, ...), custom_call_target="tpu_custom_call" | custom-call | tf_op jit(solution)/shard_map/mix_second/pallas_call | solution.py:1081
  203.5 5.3 %multiply_reduce_fusion.2 = (f32[512]{0:T(512)S(1)}, f32[512,1024]{1,0:T(8,128)S(1)}) fusion(f32[512,1024]{1,0:T(8,128)} %fusion.35, bf16[512,1536]{1,0:T(8,128)(2,1)} %get-tuple-element.56.refs_1_, bf16[2048,1024]{1,0:T(8,128)(2,1)} %get-tuple-element.57, bf16[2,256,1024]{2,1,0:T(8,128)(2,1)} %get-tuple-element.48), kind=kOutput, calls=%fused_computation.51 | convolution fusion | flops 1613233664 | bytes 9963520 | tf_op jit(solution)/shard_map/dot_general | solution.py:82
  209.3 4.7 convolution_convert_fusion
  214.0 4.5 fusion.2
  218.5 3.3 add_convert_fusion
  221.9 7.2 %multiply_reduce_fusion = (f32[1024]{0:T(1024)S(1)}, f32[512]{0:T(512)S(1)}, f32[512,1024]{1,0:T(8,128)S(1)}) fusion(f32[512,1024]{1,0:T(8,128)S(1)} %get-tuple-element.129, f32[512]{0:T(512)S(1)} %add_rsqrt_fusion, f32[1024]{0:T(1024)S(1)} %get-tuple-element.107, bf16[1024,4096]{1,0:T(8,128)(2,1)} %get-tuple-element.61, ...), kind=kOutput, calls=%fused_computation.46 | convolution fusion | flops 4306500096 | bytes 16789504 | tf_op jit(solution)/shard_map/dot_general | solution.py:86
  232.1 3.7 convolution_convert_fusion.2.grad.given
  236.9 17.3 %attend_back.1 = (bf16[512,512]{1,0:T(8,128)(2,1)}, bf16[1024,256]{1,0:T(8,128)(2,1)}) custom-call(bf16[512,512]{1,0:T(8,128)(2,1)} %get-tuple-element.58.q, bf16[1024,256]{1,0:T(8,128)(2,1)} %copy-done.8, bf16[512,2048]{1,0:T(8,128)(2,1)} %convolution_convert_fusion.2.grad.given, f32[2,768,8]{2,1,0:T(8,128)} %broadcast_in_dim.86.key_marks, ...), custom_call_target="tpu_custom_call" | custom-call | tf_op jit(solution)/shard_map/attend_back/pallas_call | solution.py:1479
  255.9 3.8 collective-permute-start.7
  259.7 4.7 pad_maximum_fusion.refs_10_
  264.4 7.4 %gate_back.1 = (bf16[512,1536]{1,0:T(8,128)(2,1)}, bf16[512,1536]{1,0:T(8,128)(2,1)}, f32[8,1536]{1,0:T(8,128)}, f32[128,1536]{1,0:T(8,128)}) custom-call(bf16[512,2048]{1,0:T(8,128)(2,1)} %convolution_convert_fusion.2.grad.given, f32[512,1536]{1,0:T(8,128)} %get-tuple-element.64.y, ...), custom_call_target="tpu_custom_call" | custom-call | tf_op jit(solution)/shard_map/gate_back/pallas_call | solution.py:1149
  286.4 29.8 %mix_back.1 = (bf16[512,1792]{1,0:T(8,128)(2,1)}, f32[16,1792]{1,0:T(8,128)}, f32[8,1792]{1,0:T(8,128)}, bf16[512,128]{1,0:T(8,128)(2,1)}, f32[8,128]{1,0:T(8,128)}) custom-call(bf16[512,1792]{1,0:T(8,128)(2,1)} %get-tuple-element.52.x.b.c, bf16[512,1792]{1,0:T(8,128)(2,1)} %get-tuple-element.52.x.b.c, bf16[512,1792]{1,0:T(8,128)(2,1)} %get-tuple-element.52.x.b.c, ...), custom_call_target="tpu_custom_call" | custom-call | tf_op jit(solution)/shard_map/mix_back/pallas_call | solution.py:1299
  320.3 5.6 %collective-permute-start.6 = (f32[8,1792]{1,0:T(8,128)S(1)}, f32[8,1792]{1,0:T(8,128)S(1)}, u32[]{:S(2)}, u32[]{:S(2)}) collective-permute-start(f32[8,1792]{1,0:T(8,128)S(1)} %slice.139), channel_id=1, source_target_pairs={{1,0},{3,2},{5,4},{7,6},{9,8},{11,10},{13,12},{15,14},{17,16},{19,... | collective-permute-start | bytes 172040 | tf_op jit(solution)/shard_map/ppermute | solution.py:1530
  328.8 9.9 %fusion.28 = (f32[1024]{0:T(1024)S(1)}, f32[512]{0:T(512)S(1)}, f32[512,1024]{1,0:T(8,128)S(1)}) fusion(bf16[2,256,1024]{2,1,0:T(8,128)(2,1)} %get-tuple-element.48, f32[512]{0:T(512)S(1)} %bitcast.109, f32[1024]{0:T(1024)S(1)} %get-tuple-element.108, f32[512,1024]{1,0:T(8,128)} %fusion.37, bf16[1024,4096]{1,0:T(8,128)(2,1)} %get-tuple-element.50, ...), kind=kOutput, calls=%fused_computation.44 | convolution fusion | flops 4315937280 | bytes 17838080 | tf_op jit(solution)/shard_map/dot_general | solution.py:86
  340.9 3.2 collective-permute-start.9
  344.8 138.0 %reduce_blocks.1 = (bf16[96,128,128]{2,1,0:T(8,128)(2,1)}, f32[296,128]{1,0:T(8,128)}) custom-call(s32[768]{0:T(1024)} %get-tuple-element.90.left_at, s32[768]{0:T(1024)} %get-tuple-element.89.right_at, f32[296,128]{1,0:T(8,128)} %bitcast.104, bf16[512,1024]{1,0:T(8,128)(2,1)} %copy-done, bf16[512,1536]{1,0:T(8,128)(2,1)} %get-tuple-element.56.refs_1_, ...), custom_call_target="tpu_custom_call" | custom-call | tf_op jit(solution)/shard_map/reduce_blocks/pallas_call | solution.py:750
  484.6 20.6 %shampoo.1 = (f32[96,128,128]{2,1,0:T(8,128)}, f32[96,128,128]{2,1,0:T(8,128)}, f32[96,128,128]{2,1,0:T(8,128)}, f32[96,128,128]{2,1,0:T(8,128)}, bf16[96,128,128]{2,1,0:T(8,128)(2,1)}) custom-call(bf16[96,128,128]{2,1,0:T(8,128)(2,1)} %get-tuple-element.78.total, f32[96,128,128]{2,1,0:T(8,128)} %master.3, f32[96,128,128]{2,1,0:T(8,128)} %left.1, ...), custom_call_target="tpu_custom_call" | custom-call | tf_op jit(solution)/shard_map/shampoo/pallas_call | solution.py:897
  (168 shorter events, 60.7 us)
Async XLA Ops:
  114.9 204.2 %copy-start = (bf16[512,1024]{1,0:T(8,128)(2,1)}, bf16[512,1024]{1,0:T(8,128)(2,1)S(1)}, u32[]{:S(2)}) copy-start(bf16[512,1024]{1,0:T(8,128)(2,1)S(1)} %fusion.22.refs_0_) | copy-start | bytes 3145732
  146.7 6.5 %copy-start.15 = (f32[37192]{0:T(1024)S(1)}, f32[37192]{0:T(1024)}, u32[]{:S(2)}) copy-start(f32[37192]{0:T(1024)} %param.25) | copy-start | bytes 446308
  149.4 9.1 %slice-start = ((f32[37192]{0:T(1024)}), f32[1536]{0:T(1024)S(1)}, s32[]{:S(2)}) async-start(f32[37192]{0:T(1024)} %param.25), calls=%async_computation | async-start | bytes 16384 | tf_op jit(solution)/shard_map/slice | solution.py:76
  149.4 20.5 %collective-permute-start.2 = (bf16[512,256]{1,0:T(8,128)(2,1)}, bf16[512,256]{1,0:T(8,128)(2,1)S(1)}, u32[]{:S(2)}, u32[]{:S(2)}) collective-permute-start(bf16[512,256]{1,0:T(8,128)(2,1)} %get-tuple-element.59), channel_id=1, source_target_pairs={{0,1},{2,3},{4,5},{6,7},{8,9},{10,11},{12,13},{14,15},{16,17},{18,... | collective-permute-start | bytes 786440 | tf_op jit(solution)/shard_map/ppermute | solution.py:1530
  151.6 8.4 %collective-permute-start = (bf16[8,1792]{1,0:T(8,128)(2,1)S(1)}, bf16[8,1792]{1,0:T(8,128)(2,1)S(1)}, u32[]{:S(2)}, u32[]{:S(2)}) collective-permute-start(bf16[8,1792]{1,0:T(8,128)(2,1)S(1)} %slice.151), channel_id=1, source_target_pairs={{0,1},{2,3},{4,5},{6,7},{8,9},{10,11},{12,13},{14,15},{16,17},{18,... | collective-permute-start | bytes 86024 | tf_op jit(solution)/shard_map/ppermute | solution.py:1530
  159.9 10.0 %copy-start.18 = (bf16[512,256]{1,0:T(8,128)(2,1)S(1)}, bf16[512,256]{1,0:T(8,128)(2,1)}, u32[]{:S(2)}) copy-start(bf16[512,256]{1,0:T(8,128)(2,1)} %get-tuple-element.59) | copy-start | bytes 786436
  168.2 16.9 %collective-permute-start.1 = (bf16[128,1536]{1,0:T(8,128)(2,1)}, bf16[128,1536]{1,0:T(8,128)(2,1)S(1)}, u32[]{:S(2)}, u32[]{:S(2)}) collective-permute-start(bf16[128,1536]{1,0:T(8,128)(2,1)} %get-tuple-element.55), channel_id=1, source_target_pairs={{0,1},{2,3},{4,5},{6,7},{8,9},{10,11},{12,13},{14,15},{16,17},{18,... | collective-permute-start | bytes 1179656 | tf_op jit(solution)/shard_map/ppermute | solution.py:1530
  203.5 5.8 %slice-start.2 = ((s8[8388608]{0:T(1024)(128)(4,1)}), s8[4194304]{0:T(1024)(128)(4,1)S(1)}, s32[]{:S(2)}) async-start(s8[8388608]{0:T(1024)(128)(4,1)} %bitcast.117), calls=%async_computation.2 | async-start | bytes 8388608
  255.9 24.6 %collective-permute-start.7 = (bf16[512,256]{1,0:T(8,128)(2,1)}, bf16[512,256]{1,0:T(8,128)(2,1)}, u32[]{:S(2)}, u32[]{:S(2)}) collective-permute-start(bf16[512,256]{1,0:T(8,128)(2,1)} %slice.141), channel_id=1, source_target_pairs={{1,0},{3,2},{5,4},{7,6},{9,8},{11,10},{13,12},{15,14},{17,16},{19,... | collective-permute-start | bytes 786440 | tf_op jit(solution)/shard_map/ppermute | solution.py:1530
  271.8 8.7 %copy-start.13 = (bf16[1024,256]{1,0:T(8,128)(2,1)S(1)}, bf16[1024,256]{1,0:T(8,128)(2,1)}, u32[]{:S(2)}) copy-start(bf16[1024,256]{1,0:T(8,128)(2,1)} %get-tuple-element.73) | copy-start | bytes 1572868
  273.1 11.4 %collective-permute-start.5 = (bf16[128,1536]{1,0:T(8,128)(2,1)S(1)}, bf16[128,1536]{1,0:T(8,128)(2,1)}, u32[]{:S(2)}, u32[]{:S(2)}) collective-permute-start(bf16[128,1536]{1,0:T(8,128)(2,1)S(1)} %convert_element_type.138), channel_id=1, source_target_pairs={{1,0},{3,2},{5,4},{7,6},{9,8},{11,10},{13,12},{15,14},{17,16},{19,... | collective-permute-start | bytes 1179656 | tf_op jit(solution)/shard_map/ppermute | solution.py:1530
  277.4 227.9 %collective-permute-start.3 = (bf16[256,1024]{1,0:T(8,128)(2,1)}, bf16[256,1024]{1,0:T(8,128)(2,1)}, u32[]{:S(2)}, u32[]{:S(2)}) collective-permute-start(bf16[256,1024]{1,0:T(8,128)(2,1)} %get-tuple-element.106), channel_id=1, source_target_pairs={{2,0},{0,1},{3,2},{1,3},{6,4},{4,5},{7,6},{5,7},{10,8},{8,9},{11,1... | collective-permute-start | bytes 1572872 | tf_op jit(solution)/shard_map/ppermute | solution.py:1516
  277.6 227.7 %collective-permute-start.4 = (bf16[256,1024]{1,0:T(8,128)(2,1)}, bf16[256,1024]{1,0:T(8,128)(2,1)}, u32[]{:S(2)}, u32[]{:S(2)}) collective-permute-start(bf16[256,1024]{1,0:T(8,128)(2,1)} %get-tuple-element.105), channel_id=1, source_target_pairs={{0,0},{2,1},{1,2},{3,3},{4,4},{6,5},{5,6},{7,7},{8,8},{10,9},{9,10... | collective-permute-start | bytes 1572872 | tf_op jit(solution)/shard_map/ppermute | solution.py:1516
  316.3 10.4 %copy-start.23 = (f32[8,1792]{1,0:T(8,128)S(1)}, f32[8,1792]{1,0:T(8,128)}, u32[]{:S(2)}) copy-start(f32[8,1792]{1,0:T(8,128)} %get-tuple-element.76) | copy-start | bytes 172036
  319.0 9.7 %copy-start.12 = (bf16[512,256]{1,0:T(8,128)(2,1)S(1)}, bf16[512,256]{1,0:T(8,128)(2,1)}, u32[]{:S(2)}) copy-start(bf16[512,256]{1,0:T(8,128)(2,1)} %turn_back.1.refs_8_) | copy-start | bytes 786436
  320.3 7.8 %collective-permute-start.6 = (f32[8,1792]{1,0:T(8,128)S(1)}, f32[8,1792]{1,0:T(8,128)S(1)}, u32[]{:S(2)}, u32[]{:S(2)}) collective-permute-start(f32[8,1792]{1,0:T(8,128)S(1)} %slice.139), channel_id=1, source_target_pairs={{1,0},{3,2},{5,4},{7,6},{9,8},{11,10},{13,12},{15,14},{17,16},{19,... | collective-permute-start | bytes 172040 | tf_op jit(solution)/shard_map/ppermute | solution.py:1530
  328.8 9.9 %copy-start.2 = (bf16[2,256,1024]{2,1,0:T(8,128)(2,1)S(1)}, bf16[2,256,1024]{2,1,0:T(8,128)(2,1)}, u32[]{:S(2)}) copy-start(bf16[2,256,1024]{2,1,0:T(8,128)(2,1)} %get-tuple-element.63) | copy-start | bytes 3145732
  328.8 9.9 %copy-start.3 = (bf16[2,256,1024]{2,1,0:T(8,128)(2,1)S(1)}, bf16[2,256,1024]{2,1,0:T(8,128)(2,1)}, u32[]{:S(2)}) copy-start(bf16[2,256,1024]{2,1,0:T(8,128)(2,1)} %get-tuple-element.48) | copy-start | bytes 3145732
  328.8 9.9 %copy-start.5 = (f32[512,1024]{1,0:T(8,128)S(1)}, f32[512,1024]{1,0:T(8,128)}, u32[]{:S(2)}) copy-start(f32[512,1024]{1,0:T(8,128)} %copy-done.4) | copy-start | bytes 6291460
  340.9 166.8 %collective-permute-start.8 = (bf16[256,1024]{1,0:T(8,128)(2,1)}, bf16[256,1024]{1,0:T(8,128)(2,1)S(1)}, u32[]{:S(2)}, u32[]{:S(2)}) collective-permute-start(bf16[256,1024]{1,0:T(8,128)(2,1)} %get-tuple-element.102), channel_id=1, source_target_pairs={{2,0},{0,1},{3,2},{1,3},{6,4},{4,5},{7,6},{5,7},{10,8},{8,9},{11,1... | collective-permute-start | bytes 1572872 | tf_op jit(solution)/shard_map/ppermute | solution.py:1516
  340.9 166.8 %collective-permute-start.9 = (bf16[256,1024]{1,0:T(8,128)(2,1)}, bf16[256,1024]{1,0:T(8,128)(2,1)}, u32[]{:S(2)}, u32[]{:S(2)}) collective-permute-start(bf16[256,1024]{1,0:T(8,128)(2,1)} %get-tuple-element.101), channel_id=1, source_target_pairs={{0,0},{2,1},{1,2},{3,3},{4,4},{6,5},{5,6},{7,7},{8,8},{10,9},{9,10... | collective-permute-start | bytes 1572872 | tf_op jit(solution)/shard_map/ppermute | solution.py:1516
  344.8 138.0 %copy-start.16 = (f32[37192]{0:T(1024)S(1)}, f32[37192]{0:T(1024)}, u32[]{:S(2)}) copy-start(f32[37192]{0:T(1024)} %param.25) | copy-start | bytes 446308
  344.8 138.0 %copy-start.19 = (f32[37192]{0:T(1024)S(1)}, f32[37192]{0:T(1024)}, u32[]{:S(2)}) copy-start(f32[37192]{0:T(1024)} %param.26) | copy-start | bytes 446308
  344.8 138.0 %copy-start.20 = (f32[37192]{0:T(1024)S(1)}, f32[37192]{0:T(1024)}, u32[]{:S(2)}) copy-start(f32[37192]{0:T(1024)} %param.27) | copy-start | bytes 446308
  (18 other events, 63.7 us)

commit v4 on v3

--- a/solution.py
+++ b/solution.py
@@ -765,144 +765,6 @@
         compiler_params=pltpu.CompilerParams(collective_id=1, has_side_effects=True, vmem_limit_bytes=63 << 20),
         name="reduce_blocks",
     )(left_at, right_at, vec, *lefts, *rights)
-
-
-STEP_BLOCKS = 32
-DEPTH = 4
-
-
-def assemble_kernel(table, blocks, w_in, w_out, w_ff, w_down, wide, tall, s_in, s_out):
-    outs = []
-    for ref in (w_in, w_out, w_ff, w_down):
-        rows, cols = ref.shape
-        per_row = cols // BS
-        deep = STEP_BLOCKS // per_row
-        for r in range(rows // (BS * deep)):
-            outs.append((ref, r * BS * deep, deep, per_row))
-
-    def target(step):
-        ref, at, deep, per_row = outs[step]
-        slot = step % DEPTH
-        return (wide.at[slot] if deep == 1 else tall.at[slot]), ref.at[pl.ds(at, BS * deep)], deep, per_row
-
-    def fetch(step):
-        buffer, _, deep, per_row = target(step)
-
-        def one(i, _):
-            rows = pl.ds(pl.multiple_of(i // per_row * BS, BS), BS)
-            cols = pl.ds(pl.multiple_of(i % per_row * BS, BS), BS)
-            pltpu.make_async_copy(blocks.at[table[step * STEP_BLOCKS + i]], buffer.at[rows, cols], s_in.at[step % DEPTH]).start()
-            return 0
-
-        lax.fori_loop(0, STEP_BLOCKS, one, 0)
-
-    def put(step):
-        buffer, place_to, _, _ = target(step)
-        return pltpu.make_async_copy(buffer, place_to, s_out.at[step % DEPTH])
-
-    steps = len(outs)
-    for step in range(min(DEPTH - 1, steps)):
-        fetch(step)
-    for step in range(steps):
-        buffer, place_to, _, _ = target(step)
-        pltpu.make_async_copy(place_to, buffer, s_in.at[step % DEPTH]).wait()
-        put(step).start()
-        ahead = step + DEPTH - 1
-        if ahead < steps:
-            if step >= 1:
-                put(step - 1).wait()
-            fetch(ahead)
-    for step in range(max(steps - DEPTH, 0), steps):
-        put(step).wait()
-
-
-def slots_in_order(block_of_slot, order):
-    match = jnp.array(order, jnp.int32)[:, None] == block_of_slot[None, :]
-    return jnp.sum(jnp.where(match, jnp.arange(block_of_slot.shape[0], dtype=jnp.int32)[None, :], 0), axis=1)
-
-
-def values_of(block_of_slot, values):
-    match = block_of_slot[:, None] == jnp.arange(len(values), dtype=jnp.int32)[None, :]
-    return jnp.sum(jnp.where(match, jnp.array(values, jnp.int32)[None, :], 0), axis=1)
-
-
-def grad_tables():
-    lefts, rights = [], []
-    left_base = right_base = 0
-    for members, beside in ((WIDE_IN, True), (TALL_OUT, False), (WIDE_FF, True), (TALL_FF, False)):
-        for m in members:
-            rows, cols = SHAPES[m]
-            for r in range(0, rows, BS):
-                for q in range(0, cols, BS):
-                    lefts.append((left_base + r) // BS)
-                    rights.append((right_base + q) // BS)
-            if beside:
-                right_base += cols
-            else:
-                left_base += rows
-        if beside:
-            left_base += rows
-        else:
-            right_base += cols
-    return lefts, rights
-
-
-def assemble(blocks, table):
-    shapes = [(D, sum(SHAPES[m][1] for m in WIDE_IN)), (sum(SHAPES[m][0] for m in TALL_OUT), D), (D, 2 * FF), (FF, D)]
-    hbm = pl.BlockSpec(memory_space=pl.ANY)
-    return pl.pallas_call(
-        assemble_kernel,
-        out_shape=tuple(jax.ShapeDtypeStruct(shape, BF16) for shape in shapes),
-        grid_spec=pltpu.PrefetchScalarGridSpec(
-            num_scalar_prefetch=1, grid=(1,), in_specs=[hbm], out_specs=(hbm,) * 4,
-            scratch_shapes=[
-                pltpu.VMEM((DEPTH, BS, STEP_BLOCKS * BS), BF16),
-                pltpu.VMEM((DEPTH, STEP_BLOCKS // (D // BS) * BS, D), BF16),
-                pltpu.SemaphoreType.DMA((DEPTH,)), pltpu.SemaphoreType.DMA((DEPTH,)),
-            ],
-        ),
-        compiler_params=kernel_params(),
-        name="assemble",
-    )(table, blocks)
-
-
-SHAMPOO = 24
-
-
-def shampoo_kernel(norm, total, master, left, right, left_root, right_root, grad, new_left, new_right, new_master, low):
-    scale = 0.5 * norm * norm / BS
-    for i in range(0, total.shape[0], 2):
-        pair = (i, i + 1)
-        rows = jnp.concatenate([total[k] for k in pair], axis=0)
-        cols = jnp.concatenate([total[k] for k in pair], axis=1)
-        outer = dot_nt(rows, rows) * scale
-        inner = dot_tn(cols, cols) * scale
-        moved = dot(rows, jnp.concatenate([right_root[k] for k in pair], axis=1).astype(BF16))
-        moved = jnp.concatenate([moved[:BS, :BS], moved[BS:, BS:]], axis=1).astype(BF16)
-        moved = dot(jnp.concatenate([left_root[k] for k in pair], axis=0).astype(BF16), moved) * (LR_MATRIX * norm)
-        for k, at in zip(pair, (slice(0, BS), slice(BS, 2 * BS))):
-            grad[k] = total[k].astype(F32) * norm
-            new_left[k] = 0.5 * left[k] + outer[at, at]
-            new_right[k] = 0.5 * right[k] + inner[at, at]
-            fresh = master[k] - moved[at, at]
-            new_master[k] = fresh
-            low[k] = fresh.astype(BF16)
-
-
-def shampoo(norm, total, master, left, right, left_root, right_root):
-    slots = total.shape[0]
-    each = math.gcd(slots, SHAMPOO)
-    spec = pl.BlockSpec((each, BS, BS), lambda i: (i, 0, 0))
-    full = jax.ShapeDtypeStruct(master.shape, F32)
-    return pl.pallas_call(
-        functools.partial(shampoo_kernel, norm),
-        out_shape=(full, full, full, full, jax.ShapeDtypeStruct(master.shape, BF16)),
-        grid=(slots // each,),
-        in_specs=[spec] * 6,
-        out_specs=(spec,) * 5,
-        compiler_params=kernel_params(),
-        name="shampoo",
-    )(total, master, left, right, left_root, right_root)
 
 
 BLOCK = 256
@@ -1349,31 +1211,6 @@
     return values * cosine + swap_halves(values) * sine
 
 
-def rope_kernel(*refs):
-    queries, (k, v, cosine, sine, q_out, kv_out) = refs[:QPAIRS], refs[QPAIRS:]
-    cos, sin = cosine[...], sine[...]
-    for p, q in enumerate(queries):
-        q_out[:, p * LANES : (p + 1) * LANES] = turn(q[...].astype(F32), cos, sin).astype(BF16)
-    kv_out[:, :KDIM] = turn(k[...].astype(F32), cos, sin).astype(BF16)
-    kv_out[:, KDIM:] = v[...].astype(BF16)
-
-
-def rope_all(proj, cosine, sine):
-    tokens = proj.shape[0]
-    start = 2 * INNER + 2 * NSTATE
-    return pl.pallas_call(
-        rope_kernel,
-        out_shape=(jax.ShapeDtypeStruct((tokens, QDIM), BF16), jax.ShapeDtypeStruct((tokens, 2 * KDIM), BF16)),
-        grid=(1,),
-        in_specs=[
-            pl.BlockSpec((tokens, LANES), lambda i, p=p: (0, start // LANES + p)) for p in range(QPAIRS + 2)
-        ] + [whole(cosine.shape), whole(sine.shape)],
-        out_specs=(whole((tokens, QDIM)), whole((tokens, 2 * KDIM))),
-        compiler_params=kernel_params(),
-        name="rope",
-    )(*[proj] * (QPAIRS + 2), cosine, sine)
-
-
 def both_sides(tile, both):
     low = lane_index(tile.shape) < HEAD
     zero = jnp.zeros_like(tile)
@@ -1504,23 +1341,294 @@
     )(g_kv, cosine, sine)
 
 
-def ungroup(rows, micro):
+FF_TILE = 512
+
+
+def feed_kernel(hidden, given, gain, w_gate, w_up, w_down, normed, mixed, g_gate, g_up, result, g_hidden, low, g_gain, total, g_mid):
+    j = pl.program_id(0)
+
+    @pl.when(j == 0)
+    def _():
+        values = hidden[...]
+        normed[...] = (values * rms_scale(values) * gain[0:1, :]).astype(BF16)
+
+    gate = dot(normed[...], w_gate[...])
+    upper = dot(normed[...], w_up[...])
+    grad = dot_nt(given[...], w_down[...])
+    opened = sigmoid(gate)
+    swish = gate * opened
+    product = (swish * upper).astype(BF16)
+    left = (grad * upper * (opened + swish * (1.0 - opened))).astype(BF16)
+    right = (grad * swish).astype(BF16)
+    mixed[...] = product
+    g_gate[...] = left
+    g_up[...] = right
+    forward = dot(product, w_down[...])
+    backward = dot_nt(left, w_gate[...]) + dot_nt(right, w_up[...])
+
+    @pl.when(j == 0)
+    def _():
+        total[...] = forward
+        g_mid[...] = backward
+
+    @pl.when(j > 0)
+    def _():
+        total[...] += forward
+        g_mid[...] += backward
+
+    @pl.when(j == pl.num_programs(0) - 1)
+    def _():
+        values = hidden[...]
+        result[...] = (values + total[...]).astype(BF16)
+        scale = rms_scale(values)
+        unit = values * scale
+        back = g_mid[...]
+        scaled = back * gain[0:1, :]
+        fresh = given[...].astype(F32) + scale * (scaled - unit * jnp.mean(scaled * unit, axis=1, keepdims=True))
+        g_hidden[...] = fresh
+        low[...] = fresh.astype(BF16)
+        g_gain[...] = jnp.broadcast_to(jnp.sum(back * unit, axis=0, keepdims=True), g_gain.shape)
+
+
+def feed(hidden, given, gain, w_ff, w_down):
+    tokens = hidden.shape[0]
+    tiles = FF // FF_TILE
+    rows = whole((tokens, D))
+    tile = pl.BlockSpec((tokens, FF_TILE), lambda j: (0, j))
+    return pl.pallas_call(
+        feed_kernel,
+        out_shape=(
+            jax.ShapeDtypeStruct((tokens, D), BF16),
+            jax.ShapeDtypeStruct((tokens, FF), BF16), jax.ShapeDtypeStruct((tokens, FF), BF16), jax.ShapeDtypeStruct((tokens, FF), BF16),
+            jax.ShapeDtypeStruct((tokens, D), BF16), jax.ShapeDtypeStruct((tokens, D), F32), jax.ShapeDtypeStruct((tokens, D), BF16),
+            jax.ShapeDtypeStruct((8, D), F32),
+        ),
+        grid=(tiles,),
+        in_specs=[
+            rows, rows, whole((8, D)),
+            pl.BlockSpec((D, FF_TILE), lambda j: (0, j)), pl.BlockSpec((D, FF_TILE), lambda j: (0, tiles + j)),
+            pl.BlockSpec((FF_TILE, D), lambda j: (j, 0)),
+        ],
+        out_specs=(rows, tile, tile, tile, rows, rows, rows, whole((8, D))),
+        scratch_shapes=[pltpu.VMEM((tokens, D), F32), pltpu.VMEM((tokens, D), F32)],
+        compiler_params=kernel_params(),
+        name="feed",
+    )(hidden, given, gain, w_ff, w_ff, w_down)
+
+
+STEP_BLOCKS = 32
+DEPTH = 4
+
+
+def project_kernel(table, blocks, rows, gain, w_dt, cosine, sine, w_in, w_out, w_ff, w_down, proj, q_out, kv_out, normed, raw, halo,
+                   held, wide, tall, s_first, s_put, s_in, s_out):
+    across = held.shape[1] // BS
+    down = held.shape[0] // BS
+
+    def first(r):
+        def one(i, _):
+            cols = pl.ds(pl.multiple_of(i * BS, BS), BS)
+            pltpu.make_async_copy(blocks.at[table[r * across + i]], held.at[pl.ds(r * BS, BS), cols], s_first.at[r]).start()
+            return 0
+
+        lax.fori_loop(0, across, one, 0)
+
+    outs = []
+    for ref in (w_out, w_ff, w_down):
+        count, cols = ref.shape
+        per_row = cols // BS
+        deep = STEP_BLOCKS // per_row
+        for r in range(count // (BS * deep)):
+            outs.append((ref, r * BS * deep, deep, per_row))
+
+    def target(step):
+        ref, at, deep, per_row = outs[step]
+        slot = step % DEPTH
+        return (wide.at[slot] if deep == 1 else tall.at[slot]), ref.at[pl.ds(at, BS * deep)], per_row
+
+    def fetch(step):
+        buffer, _, per_row = target(step)
+
+        def one(i, _):
+            block_rows = pl.ds(pl.multiple_of(i // per_row * BS, BS), BS)
+            cols = pl.ds(pl.multiple_of(i % per_row * BS, BS), BS)
+            source = blocks.at[table[down * across + step * STEP_BLOCKS + i]]
+            pltpu.make_async_copy(source, buffer.at[block_rows, cols], s_in.at[step % DEPTH]).start()
+            return 0
+
+        lax.fori_loop(0, STEP_BLOCKS, one, 0)
+
+    def put(step):
+        buffer, place_to, _ = target(step)
+        return pltpu.make_async_copy(buffer, place_to, s_out.at[step % DEPTH])
+
+    steps = len(outs)
+
+    def advance(step):
+        buffer, place_to, _ = target(step)
+        pltpu.make_async_copy(place_to, buffer, s_in.at[step % DEPTH]).wait()
+        put(step).start()
+        ahead = step + DEPTH - 1
+        if ahead < steps:
+            if step >= 1:
+                put(step - 1).wait()
+            fetch(ahead)
+
+    for r in range(down):
+        first(r)
+    for step in range(min(DEPTH - 1, steps)):
+        fetch(step)
+    values = rows[...].astype(F32)
+    low = (values * rms_scale(values) * gain[0:1, :]).astype(BF16)
+    normed[...] = low
+    raw[...] = dot(low, w_dt[...])
+    for r in range(down):
+        part = held.at[pl.ds(r * BS, BS)]
+        pltpu.make_async_copy(part, part, s_first.at[r]).wait()
+    whole_put = pltpu.make_async_copy(held, w_in, s_put.at[0])
+    whole_put.start()
+    cos, sin = cosine[...], sine[...]
+    tokens = rows.shape[0]
+    plain = proj.shape[1]
+    cuts = [(at, min(512, plain - at)) for at in range(0, plain, 512)] + [(plain, QDIM), (plain + QDIM, 2 * KDIM)]
+    done = 0
+    for k, (at, width) in enumerate(cuts):
+        value = dot(normed[...], held[:, at : at + width])
+        if at < plain:
+            proj[:, at : at + width] = value.astype(BF16)
+        elif at == plain:
+            for p in range(QPAIRS):
+                lanes = slice(p * LANES, (p + 1) * LANES)
+                q_out[:, lanes] = turn(value[:, lanes], cos, sin).astype(BF16)
+        else:
+            kv_out[:, :KDIM] = turn(value[:, :KDIM], cos, sin).astype(BF16)
+            kv_out[:, KDIM:] = value[:, KDIM:].astype(BF16)
+        goal = steps * (k + 1) // len(cuts)
+        for step in range(done, goal):
+            advance(step)
+        done = goal
+    halo[...] = proj[tokens - halo.shape[0] :, INNER:]
+    for step in range(max(steps - DEPTH, 0), steps):
+        put(step).wait()
+    whole_put.wait()
+
+
+def slots_in_order(block_of_slot, order):
+    match = jnp.array(order, jnp.int32)[:, None] == block_of_slot[None, :]
+    return jnp.sum(jnp.where(match, jnp.arange(block_of_slot.shape[0], dtype=jnp.int32)[None, :], 0), axis=1)
+
+
+def values_of(block_of_slot, values):
+    match = block_of_slot[:, None] == jnp.arange(len(values), dtype=jnp.int32)[None, :]
+    return jnp.sum(jnp.where(match, jnp.array(values, jnp.int32)[None, :], 0), axis=1)
+
+
+def grad_tables():
+    lefts, rights = [], []
+    left_base = right_base = 0
+    for members, beside in ((WIDE_IN, True), (TALL_OUT, False), (WIDE_FF, True), (TALL_FF, False)):
+        for m in members:
+            rows, cols = SHAPES[m]
+            for r in range(0, rows, BS):
+                for q in range(0, cols, BS):
+                    lefts.append((left_base + r) // BS)
+                    rights.append((right_base + q) // BS)
+            if beside:
+                right_base += cols
+            else:
+                left_base += rows
+        if beside:
+            left_base += rows
+        else:
+            right_base += cols
+    return lefts, rights
+
+
+def project(blocks, table, rows, gain, w_dt, cosine, sine):
+    tokens = rows.shape[0]
+    total = sum(SHAPES[m][1] for m in WIDE_IN)
+    plain = total - QDIM - 2 * KDIM
+    shapes = [(D, total), (sum(SHAPES[m][0] for m in TALL_OUT), D), (D, 2 * FF), (FF, D)]
+    results = [(tokens, plain), (tokens, QDIM), (tokens, 2 * KDIM), (tokens, D), (tokens, LANES), (HALO, CHANNELS)]
+    kinds = [BF16, BF16, BF16, BF16, F32, BF16]
+    hbm = pl.BlockSpec(memory_space=pl.ANY)
+    vmem = pl.BlockSpec(memory_space=pltpu.VMEM)
+    return pl.pallas_call(
+        project_kernel,
+        out_shape=tuple(jax.ShapeDtypeStruct(shape, BF16) for shape in shapes)
+        + tuple(jax.ShapeDtypeStruct(shape, kind) for shape, kind in zip(results, kinds)),
+        grid_spec=pltpu.PrefetchScalarGridSpec(
+            num_scalar_prefetch=1, grid=(1,), in_specs=[hbm] + [vmem] * 5, out_specs=(hbm,) * 4 + (vmem,) * 6,
+            scratch_shapes=[
+                pltpu.VMEM((D, total), BF16),
+                pltpu.VMEM((DEPTH, BS, STEP_BLOCKS * BS), BF16),
+                pltpu.VMEM((DEPTH, STEP_BLOCKS // (D // BS) * BS, D), BF16),
+                pltpu.SemaphoreType.DMA((D // BS,)), pltpu.SemaphoreType.DMA((1,)),
+                pltpu.SemaphoreType.DMA((DEPTH,)), pltpu.SemaphoreType.DMA((DEPTH,)),
+            ],
+        ),
+        compiler_params=kernel_params(),
+        name="project",
+    )(table, blocks, rows, gain, w_dt, cosine, sine)
+
+
+SHAMPOO = 24
+
+
+def shampoo_kernel(norm, total, master, left, right, left_root, right_root, grad, new_left, new_right, new_master, low):
+    scale = 0.5 * norm * norm / BS
+    for i in range(0, total.shape[0], 2):
+        pair = (i, i + 1)
+        rows = jnp.concatenate([total[k] for k in pair], axis=0)
+        cols = jnp.concatenate([total[k] for k in pair], axis=1)
+        outer = dot_nt(rows, rows) * scale
+        inner = dot_tn(cols, cols) * scale
+        moved = dot(rows, jnp.concatenate([right_root[k] for k in pair], axis=1).astype(BF16))
+        moved = jnp.concatenate([moved[:BS, :BS], moved[BS:, BS:]], axis=1).astype(BF16)
+        moved = dot(jnp.concatenate([left_root[k] for k in pair], axis=0).astype(BF16), moved) * (LR_MATRIX * norm)
+        for k, at in zip(pair, (slice(0, BS), slice(BS, 2 * BS))):
+            grad[k] = total[k].astype(F32) * norm
+            new_left[k] = 0.5 * left[k] + outer[at, at]
+            new_right[k] = 0.5 * right[k] + inner[at, at]
+            fresh = master[k] - moved[at, at]
+            new_master[k] = fresh
+            low[k] = fresh.astype(BF16)
+
+
+def shampoo(norm, total, master, left, right, left_root, right_root):
+    slots = total.shape[0]
+    each = math.gcd(slots, SHAMPOO)
+    spec = pl.BlockSpec((each, BS, BS), lambda i: (i, 0, 0))
+    full = jax.ShapeDtypeStruct(master.shape, F32)
+    return pl.pallas_call(
+        functools.partial(shampoo_kernel, norm),
+        out_shape=(full, full, full, full, jax.ShapeDtypeStruct(master.shape, BF16)),
+        grid=(slots // each,),
+        in_specs=[spec] * 6,
+        out_specs=(spec,) * 5,
+        compiler_params=kernel_params(),
+        name="shampoo",
+    )(total, master, left, right, left_root, right_root)
+
+
+def ungroup(values, micro):
     seq = lax.axis_size("seq")
     each = seq // micro
     here = lax.axis_index("seq")
     order = here // each
-    cut = rows.reshape((micro, rows.shape[0] // micro) + rows.shape[1:])
+    stacked = jnp.stack(values)
+    cut = stacked.reshape((len(values), micro, -1) + stacked.shape[2:])
     pieces = []
     for t in range(micro):
         pairs = [(((j + t) % micro) * each + j // micro, j) for j in range(seq)]
-        pieces.append(lax.ppermute(lax.dynamic_index_in_dim(cut, (order - t) % micro, 0, False), "seq", pairs))
+        pieces.append(lax.ppermute(lax.dynamic_index_in_dim(cut, (order - t) % micro, 1, False), "seq", pairs))
     results = []
     for m in range(micro):
         chosen = pieces[0]
         for t in range(1, micro):
             chosen = jnp.where((m - here) % micro == t, pieces[t], chosen)
         results.append(chosen)
-    return jnp.stack(results)
+    return [jnp.stack([chosen[k] for chosen in results]) for k in range(len(values))]
 
 
 def along(value, steps, micro):
@@ -1550,7 +1658,6 @@
     table = slots_in_order(block_of_slot, sum(orders, []))
     left_at, right_at = (values_of(block_of_slot, values) for values in grad_tables())
     gathered, rows, given, labels_all = gather_blocks(grid, master_blocks, tokens, cotangent, doc_ids)
-    w_in, w_out, w_ff, w_down = assemble(gathered.reshape(-1, BS, BS), table)
     rows, given = rows.reshape(count, D), given.reshape(count, D)
     gain_in, gain_mid, gain_mix, conv_weight, conv_bias, dt_bias, a_log, skip, w_dt = unpack_vectors(vector_params)
     w_dt = jnp.pad(w_dt.reshape(D, HEADS_SSM), ((0, 0), (0, LANES - HEADS_SSM))).astype(BF16)
@@ -1586,11 +1693,10 @@
     sine = jnp.concatenate([-sin, sin] * 2, axis=1)
 
     inputs = rows.astype(F32)
-    normed_in = (inputs * rms_scale(inputs) * gain_in).astype(BF16)
-    proj = dot(normed_in, w_in).astype(BF16)
-    raw = dot(normed_in, w_dt)
-    halo = along(proj[count - HALO :, INNER : INNER + CHANNELS], 1, micro)
-    q, kv = rope_all(proj, cosine, sine)
+    w_in, w_out, w_ff, w_down, proj, q, kv, normed_in, raw, halo = project(
+        gathered.reshape(-1, BS, BS), table, rows, pad_rows(gain_in), w_dt, cosine, sine
+    )
+    halo = along(halo, 1, micro)
     xbc, decays, decays_t, state, factor = mix_first(proj, halo, taps, params, raw, marks)
     past = min(each - 1, -(-DOC_MOST // count))
     earlier = [along(kv, back, micro) for back in range(past, 0, -1)]
@@ -1604,26 +1710,14 @@
     y, normed_ssm, states = mix_second(xbc, proj, decays, decays_t, marks, label_rows, incoming, wide_skip, wide_gain)
     context, stats = attend(q, reach, key_labels, marks)
     hidden = inputs + (dot(normed_ssm, w_out[:INNER]) + dot(context, w_out[INNER:]))
-    normed_mid = (hidden * rms_scale(hidden) * gain_mid).astype(BF16)
-    both = dot(normed_mid, w_ff).astype(BF16)
-    gate, upper = both[:, :FF].astype(F32), both[:, FF:].astype(F32)
-    opened = sigmoid(gate)
-    mixed = (gate * opened * upper).astype(BF16)
-    layer_out = ungroup((hidden + dot(mixed, w_down)).astype(BF16), micro)
-
-    g_mixed = dot_nt(given, w_down)
-    g_gate = g_mixed * upper * (opened + gate * opened * (1.0 - opened))
-    g_ff = jnp.concatenate([g_gate.astype(BF16), (g_mixed * gate * opened).astype(BF16)], axis=1)
-
     def norm_back(grad, values, gain):
         scale = rms_scale(values)
         unit = values * scale
         scaled = grad * gain
         return scale * (scaled - unit * jnp.mean(scaled * unit, axis=1, keepdims=True)), jnp.sum(grad * unit, axis=0)
 
-    g_values, g_gain_mid = norm_back(dot_nt(g_ff, w_ff), hidden, gain_mid)
-    g_hidden = given.astype(F32) + g_values
-    hidden_low = g_hidden.astype(BF16)
+    normed_mid, mixed, g_gate, g_up, result, g_hidden, hidden_low, g_gain_mid = feed(hidden, given, pad_rows(gain_mid), w_ff, w_down)
+    (layer_out,) = ungroup([result], micro)
     g_out = dot_nt(hidden_low, w_out).astype(BF16)
     g_y, g_z, g_gain_mix, g_state = gate_back(g_out, y, proj, wide_gain, xbc, decays, marks)
     low_state = g_state.astype(BF16)
@@ -1645,16 +1739,17 @@
     g_conv = lax.dynamic_update_slice(g_conv, (g_rim[HALO:] + rim).astype(BF16), (count - HALO, 0))
     g_in = jnp.concatenate([g_z, g_conv, g_q, g_kv], axis=1)
     g_values, g_gain_in = norm_back(dot_nt(g_in, w_in) + dot_nt(g_raw, w_dt), inputs, gain_in)
-    grad_tokens = ungroup((g_values + g_hidden).astype(BF16), micro).astype(F32)
+    (grad_tokens,) = ungroup([(g_values + g_hidden).astype(BF16)], micro)
+    grad_tokens = grad_tokens.astype(F32)
     g_w_dt = dot_tn(normed_in, g_raw)
 
-    parts = [g_gain_in, g_gain_mid, g_gain_mix[0], g_taps[:KERNEL].reshape(-1), g_taps[KERNEL]]
+    parts = [g_gain_in, g_gain_mid[0], g_gain_mix[0], g_taps[:KERNEL].reshape(-1), g_taps[KERNEL]]
     parts += [g_params[i, :HEADS_SSM] for i in range(3)] + [g_w_dt[:, :HEADS_SSM].reshape(-1)]
     width = vector_params.shape[0]
     height = -(-width // (8 * LANES)) * 8
     vector = jnp.concatenate(parts + [jnp.zeros((height * LANES - width,), F32)]).reshape(height, LANES)
     total, vector = reduce_blocks(grid, slots, left_at, right_at, [normed_in, normed_ssm, context, normed_mid, mixed],
-                                  [g_z, g_conv, g_q, g_kv, hidden_low, g_ff, given], vector)
+                                  [g_z, g_conv, g_q, g_kv, hidden_low, g_gate, g_up, given], vector)
     norm = 1.0 / math.sqrt(count * seq * lax.axis_size("dp"))
     updates = shampoo(norm, total, master_blocks, left_stats, right_stats, left_roots, right_roots)
     g_vector = vector.reshape(-1)[:width] * norm

time: 521 us -> 510 us (0.979)
  Pallas kernels: 381 us -> 411 us
  matrix products: 56.6 us -> 26.7 us
  other arithmetic: 29.2 us -> 20.1 us
    pallas_call x2, Pallas kernels: 21 us -> 49.9 us  [the longest x1 26 us: project(): pl.pallas_call(project_kernel, out_shape=tuple((jax.ShapeDtypeStruct(shap...]
    dot_general x6 -> x2, matrix products: 27.3 us -> 7.58 us  [dot(): return jnp.dot(left, right, preferred_element_type=F32, precision=precision)]
    dot_general x5 -> x3, matrix products: 28 us -> 17.9 us  [dot_nt(): lax.dot_general(left, right, (((1,), (1,)), ((), ())), preferred_element_...]
  transfers between devices with their start and end apart: 10 -> 10, of which waited for: 0 -> 0; matrix products, arithmetic and copies ran while one was open for 9% -> 8% of each run, Pallas kernels for 42% -> 43%
where the time goes in v4:
time: 510 us; the launch traced here: 501 us
  Pallas kernels  411 us (81%)
  matrix products  26.7 us (5%)
  local copies, waits for them, and re-layouts  21 us (4%)
  other arithmetic  20.1 us (4%)
  starting transfers between devices  20.1 us (4%)
    pallas_call x1, Pallas kernels, reduce_blocks(): pl.pallas_call(functools.partial(reduce_kernel, grid, slots, widths), out...  139 us
    pallas_call x1, Pallas kernels, gather_blocks(): pl.pallas_call(functools.partial(gather_kernel, grid, slots), out_shape=(...  109 us
    pallas_call x1, Pallas kernels, mix_back(): pl.pallas_call(mix_back_kernel, out_shape=(jax.ShapeDtypeStruct((tokens,...  29.8 us
    pallas_call x1, Pallas kernels, project(): pl.pallas_call(project_kernel, out_shape=tuple((jax.ShapeDtypeStruct(shap...  26 us
    pallas_call x1, Pallas kernels, feed(): pl.pallas_call(feed_kernel, out_shape=(jax.ShapeDtypeStruct((tokens, D),...  23.9 us
    pallas_call x1, Pallas kernels, shampoo(): pl.pallas_call(functools.partial(shampoo_kernel, norm), out_shape=(full,...  20.6 us
    dot_general x3, matrix products, dot_nt(): lax.dot_general(left, right, (((1,), (1,)), ((), ())), preferred_element_...  17.9 us
    pallas_call x1, Pallas kernels, attend_back(): pl.pallas_call(attend_back_kernel, out_shape=(jax.ShapeDtypeStruct((token...  17.3 us
  transfers between devices with their start and end apart: 10, of which 0 were waited for; matrix products, arithmetic and copies ran while one was open for 8% of the time, Pallas kernels for 43%

profile of v4, /device:TPU:11, one launch (start us, length us, event | category | flops | bytes accessed | tf_op | source)
XLA Modules:
  0.0 501.2 jit_solution(2935260582373090060)
XLA Ops:
  2.8 109.1 %gather_blocks.1 = (bf16[8,96,128,128]{3,2,1,0:T(8,128)(2,1)}, bf16[2,256,1024]{2,1,0:T(8,128)(2,1)}, bf16[2,256,1024]{2,1,0:T(8,128)(2,1)}, s32[4,2,256]{2,1,0:T(2,128)}) custom-call(f32[96,128,128]{2,1,0:T(8,128)} %master.3, bf16[2,256,1024]{2,1,0:T(8,128)(2,1)} %tokens.1, bf16[2,256,1024]{2,1,0:T(8,128)(2,1)} %cotangent.1, s32[2,256]{1,0:T(2,128)} %docs.1), custom_call_target="tpu_custom_call" | custom-call | tf_op jit(solution)/shard_map/gather_blocks/pallas_call | solution.py:387
  116.8 1.9 select_reduce_fusion
  118.7 26.0 %project.1 = (bf16[1024,4096]{1,0:T(8,128)(2,1)}, bf16[2048,1024]{1,0:T(8,128)(2,1)}, bf16[1024,4096]{1,0:T(8,128)(2,1)}, bf16[2048,1024]{1,0:T(8,128)(2,1)}, bf...) custom-call(s32[768]{0:T(1024)} %get-tuple-element.113.table, ...), custom_call_target="tpu_custom_call" | custom-call | tf_op jit(solution)/shard_map/project/pallas_call | solution.py:1556
  146.0 1.8 collective-permute-start
  153.7 7.7 %mix_first.1 = (bf16[512,1792]{1,0:T(8,128)(2,1)}, f32[2,512,128]{2,1,0:T(8,128)}, f32[2,128,256]{2,1,0:T(8,128)}, bf16[128,1536]{1,0:T(8,128)(2,1)}, f32[8,128]{1,0:T(8,128)}) custom-call(bf16[512,3328]{1,0:T(8,128)(2,1)} %get-tuple-element.63.proj_x.proj_bc.z, bf16[512,3328]{1,0:T(8,128)(2,1)} %get-tuple-element.63.proj_x.proj_bc.z, ...), custom_call_target="tpu_custom_call" | custom-call | tf_op jit(solution)/shard_map/mix_first/pallas_call | solution.py:848
  163.6 10.9 %attend.1 = (bf16[512,512]{1,0:T(8,128)(2,1)}, f32[4,8,512]{2,1,0:T(8,128)}) custom-call(bf16[512,512]{1,0:T(8,128)(2,1)} %get-tuple-element.72.q, bf16[1024,256]{1,0:T(8,128)(2,1)} %copy-done.2, f32[2,8,768]{2,1,0:T(8,128)} %broadcast_in_dim.78.key_labels, f32[512,128]{1,0:T(8,128)} %pad.24.marks), custom_call_target="tpu_custom_call" | custom-call | tf_op jit(solution)/shard_map/attend/pallas_call | solution.py:1257
  174.5 2.1 fusion.24
  176.6 2.0 convert_element_type.82.incoming
  179.2 16.8 %mix_second.1 = (f32[512,1536]{1,0:T(8,128)}, bf16[512,1536]{1,0:T(8,128)(2,1)}, f32[3,128,1536]{2,1,0:T(8,128)}) custom-call(bf16[512,1792]{1,0:T(8,128)(2,1)} %get-tuple-element.66.x.b.c, bf16[512,1792]{1,0:T(8,128)(2,1)} %get-tuple-element.66.x.b.c, bf16[512,1792]{1,0:T(8,128)(2,1)} %get-tuple-element.66.x.b.c, ...), custom_call_target="tpu_custom_call" | custom-call | tf_op jit(solution)/shard_map/mix_second/pallas_call | solution.py:943
  196.0 5.5 %convert_add_fusion.hidden = f32[512,1024]{1,0:T(8,128)} fusion(bf16[512,1024]{1,0:T(8,128)(2,1)S(1)} %bitcast.60, f32[512,1024]{1,0:T(8,128)S(1)} %fusion.24, bf16[512,1536]{1,0:T(8,128)(2,1)} %get-tuple-element.70.refs_1_, bf16[2048,1024]{1,0:T(8,128)(2,1)} %get-tuple-element.71), kind=kOutput, calls=%fused_computation.12 | convolution fusion | flops 1612185600 | bytes 9961472 | tf_op jit(solution)/shard_map/dot_general | solution.py:82
  201.5 23.9 %feed.1 = (bf16[512,1024]{1,0:T(8,128)(2,1)}, bf16[512,2048]{1,0:T(8,128)(2,1)}, bf16[512,2048]{1,0:T(8,128)(2,1)}, bf16[512,2048]{1,0:T(8,128)(2,1)}, bf16[512,...) custom-call(f32[512,1024]{1,0:T(8,128)} %convert_add_fusion.hidden, ...), custom_call_target="tpu_custom_call" | custom-call | tf_op jit(solution)/shard_map/feed/pallas_call | solution.py:1398
  225.4 6.2 %convolution_convert_fusion.grad.given = bf16[512,2048]{1,0:T(8,128)(2,1)} fusion(bf16[512,1024]{1,0:T(8,128)(2,1)} %get-tuple-element.79.refs_9_, bf16[2048,1024]{1,0:T(8,128)(2,1)} %get-tuple-element.71), kind=kOutput, calls=%fused_computation.10 | convolution fusion | flops 2148532224 | bytes 7340032 | tf_op jit(solution)/shard_map/dot_general | solution.py:86
  232.7 17.3 %attend_back.1 = (bf16[512,512]{1,0:T(8,128)(2,1)}, bf16[1024,256]{1,0:T(8,128)(2,1)}) custom-call(bf16[512,512]{1,0:T(8,128)(2,1)} %get-tuple-element.72.q, bf16[1024,256]{1,0:T(8,128)(2,1)} %copy-done.2, bf16[512,2048]{1,0:T(8,128)(2,1)} %convolution_convert_fusion.grad.given, f32[2,768,8]{2,1,0:T(8,128)} %broadcast_in_dim.79.key_marks, ...), custom_call_target="tpu_custom_call" | custom-call | tf_op jit(solution)/shard_map/attend_back/pallas_call | solution.py:1316
  251.0 3.8 collective-permute-start.7
  256.3 7.7 %gate_back.1 = (bf16[512,1536]{1,0:T(8,128)(2,1)}, bf16[512,1536]{1,0:T(8,128)(2,1)}, f32[8,1536]{1,0:T(8,128)}, f32[128,1536]{1,0:T(8,128)}) custom-call(bf16[512,2048]{1,0:T(8,128)(2,1)} %convolution_convert_fusion.grad.given, f32[512,1536]{1,0:T(8,128)} %get-tuple-element.80.y, bf16[512,3328]{1,0:T(8,128)(2,1)} %get-tuple-element.63.proj_x.proj_bc.z, ...), custom_call_target="tpu_custom_call" | custom-call | tf_op jit(solution)/shard_map/gate_back/pallas_call | solution.py:1011
  267.9 2.7 collective-permute-start.4
  273.6 2.1 turn_back.1.refs_8_
  276.7 29.8 %mix_back.1 = (bf16[512,1792]{1,0:T(8,128)(2,1)}, f32[16,1792]{1,0:T(8,128)}, f32[8,1792]{1,0:T(8,128)}, bf16[512,128]{1,0:T(8,128)(2,1)}, f32[8,128]{1,0:T(8,128)}) custom-call(bf16[512,1792]{1,0:T(8,128)(2,1)} %get-tuple-element.66.x.b.c, bf16[512,1792]{1,0:T(8,128)(2,1)} %get-tuple-element.66.x.b.c, bf16[512,1792]{1,0:T(8,128)(2,1)} %get-tuple-element.66.x.b.c, ...), custom_call_target="tpu_custom_call" | custom-call | tf_op jit(solution)/shard_map/mix_back/pallas_call | solution.py:1161
  308.6 5.5 %collective-permute-start.6 = (f32[8,1792]{1,0:T(8,128)}, f32[8,1792]{1,0:T(8,128)}, u32[]{:S(2)}, u32[]{:S(2)}) collective-permute-start(f32[8,1792]{1,0:T(8,128)} %slice.130), channel_id=1, source_target_pairs={{1,0},{3,2},{5,4},{7,6},{9,8},{11,10},{13,12},{15,14},{17,16},{19,... | collective-permute-start | bytes 172040 | tf_op jit(solution)/shard_map/ppermute | solution.py:1638
  319.6 10.2 %fusion.18 = (f32[1024]{0:T(1024)}, f32[512]{0:T(512)S(1)}, f32[512,1024]{1,0:T(8,128)S(1)}) fusion(f32[512]{0:T(512)} %bitcast.73, bf16[2,256,1024]{2,1,0:T(8,128)(2,1)S(1)} %copy-done, f32[1024]{0:T(1024)S(1)} %get-tuple-element.127, f32[512,1024]{1,0:T(8,128)S(1)} %fusion.35, bf16[1024,4096]{1,0:T(8,128)(2,1)} %get-tuple-element.90, ...), kind=kOutput, calls=%fused_computation.25 | convolution fusion | flops 4315937280 | bytes 17838080 | tf_op jit(solution)/shard_map/dot_general | solution.py:86
  331.6 2.3 collective-permute-start.9
  334.8 138.6 %reduce_blocks.1 = (bf16[96,128,128]{2,1,0:T(8,128)(2,1)}, f32[296,128]{1,0:T(8,128)}) custom-call(s32[768]{0:T(1024)} %get-tuple-element.112.left_at, s32[768]{0:T(1024)} %get-tuple-element.111.right_at, f32[296,128]{1,0:T(8,128)} %bitcast.65, bf16[512,1024]{1,0:T(8,128)(2,1)} %get-tuple-element.97.refs_0_, bf16[512,1536]{1,0:T(8,128)(2,1)} %get-tuple-element.70.refs_1_, ...), custom_call_target="tpu_custom_call" | custom-call | tf_op jit(solution)/shard_map/reduce_blocks/pallas_call | solution.py:750
  473.4 1.8 divide_subtract_fusion
  475.2 20.6 %shampoo.1 = (f32[96,128,128]{2,1,0:T(8,128)}, f32[96,128,128]{2,1,0:T(8,128)}, f32[96,128,128]{2,1,0:T(8,128)}, f32[96,128,128]{2,1,0:T(8,128)}, bf16[96,128,128]{2,1,0:T(8,128)(2,1)}) custom-call(bf16[96,128,128]{2,1,0:T(8,128)(2,1)} %get-tuple-element.102.total, f32[96,128,128]{2,1,0:T(8,128)} %master.3, f32[96,128,128]{2,1,0:T(8,128)} %left.1, ...), custom_call_target="tpu_custom_call" | custom-call | tf_op jit(solution)/shard_map/shampoo/pallas_call | solution.py:1603
  (148 shorter events, 42.4 us)
Async XLA Ops:
  118.7 29.2 %copy-start.8 = (f32[37192]{0:T(1024)S(1)}, f32[37192]{0:T(1024)}, u32[]{:S(2)}) copy-start(f32[37192]{0:T(1024)} %param.25) | copy-start | bytes 446308
  118.7 31.1 %copy-start = (bf16[2,256,1024]{2,1,0:T(8,128)(2,1)S(1)}, bf16[2,256,1024]{2,1,0:T(8,128)(2,1)}, u32[]{:S(2)}) copy-start(bf16[2,256,1024]{2,1,0:T(8,128)(2,1)} %get-tuple-element.60) | copy-start | bytes 3145732
  144.7 18.0 %collective-permute-start.2 = (bf16[512,256]{1,0:T(8,128)(2,1)}, bf16[512,256]{1,0:T(8,128)(2,1)S(1)}, u32[]{:S(2)}, u32[]{:S(2)}) collective-permute-start(bf16[512,256]{1,0:T(8,128)(2,1)} %get-tuple-element.73), channel_id=1, source_target_pairs={{0,1},{2,3},{4,5},{6,7},{8,9},{10,11},{12,13},{14,15},{16,17},{18,... | collective-permute-start | bytes 786440 | tf_op jit(solution)/shard_map/ppermute | solution.py:1638
  146.0 7.1 %collective-permute-start = (bf16[8,1792]{1,0:T(8,128)(2,1)}, bf16[8,1792]{1,0:T(8,128)(2,1)S(1)}, u32[]{:S(2)}, u32[]{:S(2)}) collective-permute-start(bf16[8,1792]{1,0:T(8,128)(2,1)} %get-tuple-element.64), channel_id=1, source_target_pairs={{0,1},{2,3},{4,5},{6,7},{8,9},{10,11},{12,13},{14,15},{16,17},{18,... | collective-permute-start | bytes 86024 | tf_op jit(solution)/shard_map/ppermute | solution.py:1638
  153.7 9.0 %copy-start.10 = (bf16[512,256]{1,0:T(8,128)(2,1)S(1)}, bf16[512,256]{1,0:T(8,128)(2,1)}, u32[]{:S(2)}) copy-start(bf16[512,256]{1,0:T(8,128)(2,1)} %get-tuple-element.73) | copy-start | bytes 786436
  161.4 15.2 %collective-permute-start.1 = (bf16[128,1536]{1,0:T(8,128)(2,1)}, bf16[128,1536]{1,0:T(8,128)(2,1)}, u32[]{:S(2)}, u32[]{:S(2)}) collective-permute-start(bf16[128,1536]{1,0:T(8,128)(2,1)} %get-tuple-element.69), channel_id=1, source_target_pairs={{0,1},{2,3},{4,5},{6,7},{8,9},{10,11},{12,13},{14,15},{16,17},{18,... | collective-permute-start | bytes 1179656 | tf_op jit(solution)/shard_map/ppermute | solution.py:1638
  251.0 21.7 %collective-permute-start.7 = (bf16[512,256]{1,0:T(8,128)(2,1)S(1)}, bf16[512,256]{1,0:T(8,128)(2,1)S(1)}, u32[]{:S(2)}, u32[]{:S(2)}) collective-permute-start(bf16[512,256]{1,0:T(8,128)(2,1)S(1)} %slice.132), channel_id=1, source_target_pairs={{1,0},{3,2},{5,4},{7,6},{9,8},{11,10},{13,12},{15,14},{17,16},{19,... | collective-permute-start | bytes 786440 | tf_op jit(solution)/shard_map/ppermute | solution.py:1638
  256.3 10.3 %copy-start.5 = (bf16[512,1024]{1,0:T(8,128)(2,1)S(1)}, bf16[512,1024]{1,0:T(8,128)(2,1)}, u32[]{:S(2)}) copy-start(bf16[512,1024]{1,0:T(8,128)(2,1)} %get-tuple-element.78) | copy-start | bytes 3145732
  264.0 8.7 %copy-start.6 = (bf16[1024,256]{1,0:T(8,128)(2,1)S(1)}, bf16[1024,256]{1,0:T(8,128)(2,1)}, u32[]{:S(2)}) copy-start(bf16[1024,256]{1,0:T(8,128)(2,1)} %get-tuple-element.89) | copy-start | bytes 1572868
  265.3 10.5 %collective-permute-start.5 = (bf16[128,1536]{1,0:T(8,128)(2,1)S(1)}, bf16[128,1536]{1,0:T(8,128)(2,1)S(1)}, u32[]{:S(2)}, u32[]{:S(2)}) collective-permute-start(bf16[128,1536]{1,0:T(8,128)(2,1)S(1)} %convert_element_type.86), channel_id=1, source_target_pairs={{1,0},{3,2},{5,4},{7,6},{9,8},{11,10},{13,12},{15,14},{17,16},{19,... | collective-permute-start | bytes 1179656 | tf_op jit(solution)/shard_map/ppermute | solution.py:1638
  267.7 228.1 %collective-permute-start.3 = (bf16[1,256,1024]{2,1,0:T(8,128)(2,1)}, bf16[1,256,1024]{2,1,0:T(8,128)(2,1)}, u32[]{:S(2)}, u32[]{:S(2)}) collective-permute-start(bf16[1,256,1024]{2,1,0:T(8,128)(2,1)} %get-tuple-element.125), channel_id=1, source_target_pairs={{2,0},{0,1},{3,2},{1,3},{6,4},{4,5},{7,6},{5,7},{10,8},{8,9},{11,1... | collective-permute-start | bytes 1572872 | tf_op jit(solution)/shard_map/ppermute | solution.py:1624
  267.9 227.9 %collective-permute-start.4 = (bf16[1,256,1024]{2,1,0:T(8,128)(2,1)}, bf16[1,256,1024]{2,1,0:T(8,128)(2,1)}, u32[]{:S(2)}, u32[]{:S(2)}) collective-permute-start(bf16[1,256,1024]{2,1,0:T(8,128)(2,1)} %get-tuple-element.124), channel_id=1, source_target_pairs={{0,0},{2,1},{1,2},{3,3},{4,4},{6,5},{5,6},{7,7},{8,8},{10,9},{9,10... | collective-permute-start | bytes 1572872 | tf_op jit(solution)/shard_map/ppermute | solution.py:1624
  306.5 8.9 %copy-start.1 = (bf16[512,1024]{1,0:T(8,128)(2,1)S(1)}, bf16[512,1024]{1,0:T(8,128)(2,1)}, u32[]{:S(2)}) copy-start(bf16[512,1024]{1,0:T(8,128)(2,1)} %get-tuple-element.97.refs_0_) | copy-start | bytes 3145732
  306.5 8.9 %copy-start.7 = (bf16[512,128]{1,0:T(8,128)(2,1)S(1)}, bf16[512,128]{1,0:T(8,128)(2,1)}, u32[]{:S(2)}) copy-start(bf16[512,128]{1,0:T(8,128)(2,1)} %get-tuple-element.91) | copy-start | bytes 393220
  306.5 10.2 %copy-start.15 = (f32[8,1792]{1,0:T(8,128)S(1)}, f32[8,1792]{1,0:T(8,128)}, u32[]{:S(2)}) copy-start(f32[8,1792]{1,0:T(8,128)} %get-tuple-element.95) | copy-start | bytes 172036
  308.0 11.6 %copy-start.4 = (bf16[512,256]{1,0:T(8,128)(2,1)S(1)}, bf16[512,256]{1,0:T(8,128)(2,1)}, u32[]{:S(2)}) copy-start(bf16[512,256]{1,0:T(8,128)(2,1)} %turn_back.1.refs_8_) | copy-start | bytes 786436
  308.6 9.5 %collective-permute-start.6 = (f32[8,1792]{1,0:T(8,128)}, f32[8,1792]{1,0:T(8,128)}, u32[]{:S(2)}, u32[]{:S(2)}) collective-permute-start(f32[8,1792]{1,0:T(8,128)} %slice.130), channel_id=1, source_target_pairs={{1,0},{3,2},{5,4},{7,6},{9,8},{11,10},{13,12},{15,14},{17,16},{19,... | collective-permute-start | bytes 172040 | tf_op jit(solution)/shard_map/ppermute | solution.py:1638
  319.6 10.3 %copy-start.3 = (f32[512,1024]{1,0:T(8,128)S(1)}, f32[512,1024]{1,0:T(8,128)}, u32[]{:S(2)}) copy-start(f32[512,1024]{1,0:T(8,128)} %get-tuple-element.92) | copy-start | bytes 6291460
  319.6 10.3 %copy-start.18 = (f32[1,2,2,128]{3,1,2,0:T(2,128)S(1)}, f32[1,2,2,128]{3,1,2,0:T(2,128)}, u32[]{:S(2)}) copy-start(f32[1,2,2,128]{3,1,2,0:T(2,128)} %copy.52) | copy-start | bytes 6148
  331.6 166.5 %collective-permute-start.8 = (bf16[1,256,1024]{2,1,0:T(8,128)(2,1)}, bf16[1,256,1024]{2,1,0:T(8,128)(2,1)S(1)}, u32[]{:S(2)}, u32[]{:S(2)}) collective-permute-start(bf16[1,256,1024]{2,1,0:T(8,128)(2,1)} %get-tuple-element.121), channel_id=1, source_target_pairs={{2,0},{0,1},{3,2},{1,3},{6,4},{4,5},{7,6},{5,7},{10,8},{8,9},{11,1... | collective-permute-start | bytes 1572872 | tf_op jit(solution)/shard_map/ppermute | solution.py:1624
  331.6 166.5 %collective-permute-start.9 = (bf16[1,256,1024]{2,1,0:T(8,128)(2,1)}, bf16[1,256,1024]{2,1,0:T(8,128)(2,1)}, u32[]{:S(2)}, u32[]{:S(2)}) collective-permute-start(bf16[1,256,1024]{2,1,0:T(8,128)(2,1)} %get-tuple-element.120), channel_id=1, source_target_pairs={{0,0},{2,1},{1,2},{3,3},{4,4},{6,5},{5,6},{7,7},{8,8},{10,9},{9,10... | collective-permute-start | bytes 1572872 | tf_op jit(solution)/shard_map/ppermute | solution.py:1624
  334.7 138.6 %copy-start.9 = (f32[37192]{0:T(1024)S(1)}, f32[37192]{0:T(1024)}, u32[]{:S(2)}) copy-start(f32[37192]{0:T(1024)} %param.25) | copy-start | bytes 446308
  334.7 138.6 %copy-start.11 = (f32[37192]{0:T(1024)S(1)}, f32[37192]{0:T(1024)}, u32[]{:S(2)}) copy-start(f32[37192]{0:T(1024)} %param.26) | copy-start | bytes 446308
  334.7 138.6 %copy-start.12 = (f32[37192]{0:T(1024)S(1)}, f32[37192]{0:T(1024)}, u32[]{:S(2)}) copy-start(f32[37192]{0:T(1024)} %param.27) | copy-start | bytes 446308
  (13 other events, 47.0 us)

commit v5 on v4

--- a/solution.py
+++ b/solution.py
@@ -991,7 +991,7 @@
     keep = dot(jnp.broadcast_to(own, (8, LANES)), spread, HIGHEST)[0:1]
     weighted = (fresh * dot(entry_weight.astype(BF16), spread.astype(BF16))).astype(BF16)
     local = dot_tn(c[...], weighted)
-    gains = jnp.broadcast_to(jnp.sum(given * unit, axis=0, keepdims=True), g_gain.shape)
+    gains = jnp.sum(given * unit, axis=0, keepdims=True)
 
     @pl.when(step == 0)
     def _():
@@ -1013,7 +1013,7 @@
         out_shape=(
             jax.ShapeDtypeStruct((tokens, INNER), BF16),
             jax.ShapeDtypeStruct((tokens, INNER), BF16),
-            jax.ShapeDtypeStruct((8, INNER), F32),
+            jax.ShapeDtypeStruct((1, INNER), F32),
             jax.ShapeDtypeStruct((NSTATE, INNER), F32),
         ),
         grid=(blocks,),
@@ -1021,7 +1021,7 @@
             rows(INNER, 0), rows(INNER, 0), rows(INNER, 0), whole(gain.shape), rows(NSTATE, INNER // NSTATE + 1),
             pl.BlockSpec((2, BLOCK, LANES), lambda i: (0, blocks - 1 - i, 0)), rows(LANES, 0),
         ],
-        out_specs=(rows(INNER, 0), rows(INNER, 0), whole((8, INNER)), whole((NSTATE, INNER))),
+        out_specs=(rows(INNER, 0), rows(INNER, 0), whole((1, INNER)), whole((NSTATE, INNER))),
         compiler_params=kernel_params(),
         name="gate_back",
     )(grad, y, proj, gain, xbc, decays, marks)
@@ -1344,12 +1344,14 @@
 FF_TILE = 512
 
 
-def feed_kernel(hidden, given, gain, w_gate, w_up, w_down, normed, mixed, g_gate, g_up, result, g_hidden, low, g_gain, total, g_mid):
+def feed_kernel(rows, scanned, context, given, gain, w_out, w_gate, w_up, w_down,
+                normed, mixed, g_gate, g_up, result, g_hidden, low, g_gain, g_out, hidden, total, g_mid):
     j = pl.program_id(0)
 
     @pl.when(j == 0)
     def _():
-        values = hidden[...]
+        values = rows[...].astype(F32) + (dot(scanned[...], w_out[:INNER, :]) + dot(context[...], w_out[INNER:, :]))
+        hidden[...] = values
         normed[...] = (values * rms_scale(values) * gain[0:1, :]).astype(BF16)
 
     gate = dot(normed[...], w_gate[...])
@@ -1387,13 +1389,16 @@
         fresh = given[...].astype(F32) + scale * (scaled - unit * jnp.mean(scaled * unit, axis=1, keepdims=True))
         g_hidden[...] = fresh
         low[...] = fresh.astype(BF16)
-        g_gain[...] = jnp.broadcast_to(jnp.sum(back * unit, axis=0, keepdims=True), g_gain.shape)
-
-
-def feed(hidden, given, gain, w_ff, w_down):
-    tokens = hidden.shape[0]
+        g_gain[...] = jnp.sum(back * unit, axis=0, keepdims=True)
+        for at in range(0, g_out.shape[1], FF_TILE):
+            g_out[:, at : at + FF_TILE] = dot_nt(low[...], w_out[at : at + FF_TILE, :]).astype(BF16)
+
+
+def feed(inputs, scanned, context, given, gain, w_out, w_ff, w_down):
+    tokens = inputs.shape[0]
     tiles = FF // FF_TILE
     rows = whole((tokens, D))
+    once = lambda a: pl.BlockSpec(a.shape, lambda j: (0, 0), pipeline_mode=pl.Buffered(1))
     tile = pl.BlockSpec((tokens, FF_TILE), lambda j: (0, j))
     return pl.pallas_call(
         feed_kernel,
@@ -1401,19 +1406,19 @@
             jax.ShapeDtypeStruct((tokens, D), BF16),
             jax.ShapeDtypeStruct((tokens, FF), BF16), jax.ShapeDtypeStruct((tokens, FF), BF16), jax.ShapeDtypeStruct((tokens, FF), BF16),
             jax.ShapeDtypeStruct((tokens, D), BF16), jax.ShapeDtypeStruct((tokens, D), F32), jax.ShapeDtypeStruct((tokens, D), BF16),
-            jax.ShapeDtypeStruct((8, D), F32),
+            jax.ShapeDtypeStruct((1, D), F32), jax.ShapeDtypeStruct((tokens, INNER + QDIM), BF16),
         ),
         grid=(tiles,),
         in_specs=[
-            rows, rows, whole((8, D)),
+            once(inputs), once(scanned), once(context), once(given), once(gain), once(w_out),
             pl.BlockSpec((D, FF_TILE), lambda j: (0, j)), pl.BlockSpec((D, FF_TILE), lambda j: (0, tiles + j)),
             pl.BlockSpec((FF_TILE, D), lambda j: (j, 0)),
         ],
-        out_specs=(rows, tile, tile, tile, rows, rows, rows, whole((8, D))),
-        scratch_shapes=[pltpu.VMEM((tokens, D), F32), pltpu.VMEM((tokens, D), F32)],
+        out_specs=(rows, tile, tile, tile, rows, rows, rows, whole((1, D)), whole((tokens, INNER + QDIM))),
+        scratch_shapes=[pltpu.VMEM((tokens, D), F32)] * 3,
         compiler_params=kernel_params(),
         name="feed",
-    )(hidden, given, gain, w_ff, w_ff, w_down)
+    )(inputs, scanned, context, given, gain, w_out, w_ff, w_ff, w_down)
 
 
 STEP_BLOCKS = 32
@@ -1664,8 +1669,8 @@
     taps = pad_rows(conv_weight.reshape(KERNEL, CHANNELS), conv_bias)
     lane_pad = lambda v: jnp.pad(v, (0, LANES - HEADS_SSM))
     params = pad_rows(lane_pad(dt_bias), lane_pad(a_log))
-    wide_skip = pad_rows(jnp.repeat(skip, HEAD))
-    wide_gain = pad_rows(gain_mix)
+    wide_skip = jnp.repeat(skip, HEAD)[None]
+    wide_gain = gain_mix[None]
 
     row = lax.dynamic_index_in_dim(labels_all, here // each, 1, False).reshape(-1)
     before = jnp.concatenate([jnp.full((DOC_MOST,), -1, jnp.int32), row])
@@ -1687,14 +1692,13 @@
     positions = (start + jnp.arange(count) - first).astype(F32)
     half = HEAD // 2
     frequency = jnp.exp(jnp.arange(half, dtype=F32) * (-2.0 * math.log(THETA) / HEAD))
-    angles = positions[:, None] * frequency[None, :]
-    cos, sin = jnp.cos(angles), jnp.sin(angles)
-    cosine = jnp.concatenate([cos] * 4, axis=1)
-    sine = jnp.concatenate([-sin, sin] * 2, axis=1)
+    angles = positions[:, None] * jnp.tile(frequency, LANES // half)[None, :]
+    cosine = jnp.cos(angles)
+    sine = jnp.sin(angles) * jnp.where(jnp.arange(LANES) % HEAD < half, -1.0, 1.0).astype(F32)[None, :]
 
     inputs = rows.astype(F32)
     w_in, w_out, w_ff, w_down, proj, q, kv, normed_in, raw, halo = project(
-        gathered.reshape(-1, BS, BS), table, rows, pad_rows(gain_in), w_dt, cosine, sine
+        gathered.reshape(-1, BS, BS), table, rows, gain_in[None], w_dt, cosine, sine
     )
     halo = along(halo, 1, micro)
     xbc, decays, decays_t, state, factor = mix_first(proj, halo, taps, params, raw, marks)
@@ -1709,16 +1713,16 @@
         incoming = along(state, back, micro).astype(F32) + wide(along(factor, back, micro)) * incoming
     y, normed_ssm, states = mix_second(xbc, proj, decays, decays_t, marks, label_rows, incoming, wide_skip, wide_gain)
     context, stats = attend(q, reach, key_labels, marks)
-    hidden = inputs + (dot(normed_ssm, w_out[:INNER]) + dot(context, w_out[INNER:]))
     def norm_back(grad, values, gain):
         scale = rms_scale(values)
         unit = values * scale
         scaled = grad * gain
         return scale * (scaled - unit * jnp.mean(scaled * unit, axis=1, keepdims=True)), jnp.sum(grad * unit, axis=0)
 
-    normed_mid, mixed, g_gate, g_up, result, g_hidden, hidden_low, g_gain_mid = feed(hidden, given, pad_rows(gain_mid), w_ff, w_down)
+    normed_mid, mixed, g_gate, g_up, result, g_hidden, hidden_low, g_gain_mid, g_out = feed(
+        rows, normed_ssm, context, given, gain_mid[None], w_out, w_ff, w_down
+    )
     (layer_out,) = ungroup([result], micro)
-    g_out = dot_nt(hidden_low, w_out).astype(BF16)
     g_y, g_z, g_gain_mix, g_state = gate_back(g_out, y, proj, wide_gain, xbc, decays, marks)
     low_state = g_state.astype(BF16)
     leaving = along(low_state, 1 - each, micro).astype(F32) if each > 1 else jnp.zeros(state.shape, F32)

time: 510 us -> 499 us (0.978)
  matrix products: 26.7 us -> 13 us
  Pallas kernels: 411 us -> 417 us
    dot_general x2 -> x0, matrix products: 7.58 us -> none  [dot(): return jnp.dot(left, right, preferred_element_type=F32, precision=precision)]
    pallas_call x1, Pallas kernels: 23.9 us -> 30.5 us  [feed(): pl.pallas_call(feed_kernel, out_shape=(jax.ShapeDtypeStruct((tokens, D),...]
    dot_general x3 -> x2, matrix products: 17.9 us -> 11.7 us  [dot_nt(): lax.dot_general(left, right, (((1,), (1,)), ((), ())), preferred_element_...]
  transfers between devices with their start and end apart: 10 -> 10, of which waited for: 0 -> 0; matrix products, arithmetic and copies ran while one was open for 8% -> 7% of each run, Pallas kernels for 43% -> 46%
where the time goes in v5:
time: 499 us; the launch traced here: 491 us
  Pallas kernels  417 us (84%)
  local copies, waits for them, and re-layouts  19.7 us (4%)
  starting transfers between devices  19.4 us (4%)
  other arithmetic  18.7 us (4%)
  matrix products  13 us (3%)
    pallas_call x1, Pallas kernels, reduce_blocks(): pl.pallas_call(functools.partial(reduce_kernel, grid, slots, widths), out...  139 us
    pallas_call x1, Pallas kernels, gather_blocks(): pl.pallas_call(functools.partial(gather_kernel, grid, slots), out_shape=(...  109 us
    pallas_call x1, Pallas kernels, feed(): pl.pallas_call(feed_kernel, out_shape=(jax.ShapeDtypeStruct((tokens, D),...  30.5 us
    pallas_call x1, Pallas kernels, mix_back(): pl.pallas_call(mix_back_kernel, out_shape=(jax.ShapeDtypeStruct((tokens,...  30 us
    pallas_call x1, Pallas kernels, project(): pl.pallas_call(project_kernel, out_shape=tuple((jax.ShapeDtypeStruct(shap...  26 us
    pallas_call x1, Pallas kernels, shampoo(): pl.pallas_call(functools.partial(shampoo_kernel, norm), out_shape=(full,...  20.6 us
    pallas_call x1, Pallas kernels, attend_back(): pl.pallas_call(attend_back_kernel, out_shape=(jax.ShapeDtypeStruct((token...  17.7 us
    pallas_call x1, Pallas kernels, mix_second(): pl.pallas_call(mix_second_kernel, out_shape=(jax.ShapeDtypeStruct((tokens...  16.8 us
  transfers between devices with their start and end apart: 10, of which 0 were waited for; matrix products, arithmetic and copies ran while one was open for 7% of the time, Pallas kernels for 46%

profile of v5, /device:TPU:11, one launch (start us, length us, event | category | flops | bytes accessed | tf_op | source)
XLA Modules:
  0.0 490.8 jit_solution(310350504143744438)
XLA Ops:
  3.0 109.1 %gather_blocks.1 = (bf16[8,96,128,128]{3,2,1,0:T(8,128)(2,1)}, bf16[2,256,1024]{2,1,0:T(8,128)(2,1)}, bf16[2,256,1024]{2,1,0:T(8,128)(2,1)}, s32[4,2,256]{2,1,0:T(2,128)}) custom-call(f32[96,128,128]{2,1,0:T(8,128)} %master.3, bf16[2,256,1024]{2,1,0:T(8,128)(2,1)} %tokens.1, bf16[2,256,1024]{2,1,0:T(8,128)(2,1)} %cotangent.1, s32[2,256]{1,0:T(2,128)} %docs.1), custom_call_target="tpu_custom_call" | custom-call | tf_op jit(solution)/shard_map/gather_blocks/pallas_call | solution.py:387
  114.6 1.8 fusion.11
  116.4 1.9 select_reduce_fusion
  118.3 26.0 %project.1 = (bf16[1024,4096]{1,0:T(8,128)(2,1)}, bf16[2048,1024]{1,0:T(8,128)(2,1)}, bf16[1024,4096]{1,0:T(8,128)(2,1)}, bf16[2048,1024]{1,0:T(8,128)(2,1)}, bf...) custom-call(s32[768]{0:T(1024)} %get-tuple-element.115.table, ...), custom_call_target="tpu_custom_call" | custom-call | tf_op jit(solution)/shard_map/project/pallas_call | solution.py:1561
  145.5 1.8 collective-permute-start
  152.3 7.8 %mix_first.1 = (bf16[512,1792]{1,0:T(8,128)(2,1)}, f32[2,512,128]{2,1,0:T(8,128)}, f32[2,128,256]{2,1,0:T(8,128)}, bf16[128,1536]{1,0:T(8,128)(2,1)}, f32[8,128]{1,0:T(8,128)}) custom-call(bf16[512,3328]{1,0:T(8,128)(2,1)} %get-tuple-element.64.proj_x.proj_bc.z, bf16[512,3328]{1,0:T(8,128)(2,1)} %get-tuple-element.64.proj_x.proj_bc.z, ...), custom_call_target="tpu_custom_call" | custom-call | tf_op jit(solution)/shard_map/mix_first/pallas_call | solution.py:848
  162.5 10.9 %attend.1 = (bf16[512,512]{1,0:T(8,128)(2,1)}, f32[4,8,512]{2,1,0:T(8,128)}) custom-call(bf16[512,512]{1,0:T(8,128)(2,1)} %get-tuple-element.72.q, bf16[1024,256]{1,0:T(8,128)(2,1)} %copy-done.3, f32[2,8,768]{2,1,0:T(8,128)} %broadcast_in_dim.99.key_labels, f32[512,128]{1,0:T(8,128)} %pad.20.marks), custom_call_target="tpu_custom_call" | custom-call | tf_op jit(solution)/shard_map/attend/pallas_call | solution.py:1257
  175.0 16.8 %mix_second.1 = (f32[512,1536]{1,0:T(8,128)}, bf16[512,1536]{1,0:T(8,128)(2,1)}, f32[3,128,1536]{2,1,0:T(8,128)}) custom-call(bf16[512,1792]{1,0:T(8,128)(2,1)} %get-tuple-element.67.x.b.c, bf16[512,1792]{1,0:T(8,128)(2,1)} %get-tuple-element.67.x.b.c, bf16[512,1792]{1,0:T(8,128)(2,1)} %get-tuple-element.67.x.b.c, ...), custom_call_target="tpu_custom_call" | custom-call | tf_op jit(solution)/shard_map/mix_second/pallas_call | solution.py:943
  191.8 30.5 %feed.1 = (bf16[512,1024]{1,0:T(8,128)(2,1)}, bf16[512,2048]{1,0:T(8,128)(2,1)}, bf16[512,2048]{1,0:T(8,128)(2,1)}, bf16[512,2048]{1,0:T(8,128)(2,1)}, bf16[512,...) custom-call(bf16[512,1024]{1,0:T(8,128)(2,1)} %bitcast.56, ...), custom_call_target="tpu_custom_call" | custom-call | tf_op jit(solution)/shard_map/feed/pallas_call | solution.py:1403
  222.4 7.4 %gate_back.1 = (bf16[512,1536]{1,0:T(8,128)(2,1)}, bf16[512,1536]{1,0:T(8,128)(2,1)}, f32[1,1536]{1,0:T(1,128)}, f32[128,1536]{1,0:T(8,128)}) custom-call(bf16[512,2048]{1,0:T(8,128)(2,1)} %get-tuple-element.80.grad.given, f32[512,1536]{1,0:T(8,128)} %get-tuple-element.81.y, bf16[512,3328]{1,0:T(8,128)(2,1)} %get-tuple-element.64.proj_x.proj_bc.z, ...), custom_call_target="tpu_custom_call" | custom-call | tf_op jit(solution)/shard_map/gate_back/pallas_call | solution.py:1011
  231.0 3.1 collective-permute-start.5
  235.2 17.7 %attend_back.1 = (bf16[512,512]{1,0:T(8,128)(2,1)}, bf16[1024,256]{1,0:T(8,128)(2,1)}) custom-call(bf16[512,512]{1,0:T(8,128)(2,1)} %get-tuple-element.72.q, bf16[1024,256]{1,0:T(8,128)(2,1)} %copy-done.3, bf16[512,2048]{1,0:T(8,128)(2,1)} %get-tuple-element.80.grad.given, f32[2,768,8]{2,1,0:T(8,128)} %broadcast_in_dim.101.key_marks, ...), custom_call_target="tpu_custom_call" | custom-call | tf_op jit(solution)/shard_map/attend_back/pallas_call | solution.py:1316
  258.1 2.7 collective-permute-start.4
  261.7 2.1 turn_back.1.refs_8_
  264.7 30.0 %mix_back.1 = (bf16[512,1792]{1,0:T(8,128)(2,1)}, f32[16,1792]{1,0:T(8,128)}, f32[8,1792]{1,0:T(8,128)}, bf16[512,128]{1,0:T(8,128)(2,1)}, f32[8,128]{1,0:T(8,128)}) custom-call(bf16[512,1792]{1,0:T(8,128)(2,1)} %get-tuple-element.67.x.b.c, bf16[512,1792]{1,0:T(8,128)(2,1)} %get-tuple-element.67.x.b.c, bf16[512,1792]{1,0:T(8,128)(2,1)} %get-tuple-element.67.x.b.c, ...), custom_call_target="tpu_custom_call" | custom-call | tf_op jit(solution)/shard_map/mix_back/pallas_call | solution.py:1161
  294.8 1.5 fusion.20
  298.2 5.5 %collective-permute-start.6 = (f32[8,1792]{1,0:T(8,128)}, f32[8,1792]{1,0:T(8,128)}, u32[]{:S(2)}, u32[]{:S(2)}) collective-permute-start(f32[8,1792]{1,0:T(8,128)} %slice.116), channel_id=1, source_target_pairs={{1,0},{3,2},{5,4},{7,6},{9,8},{11,10},{13,12},{15,14},{17,16},{19,... | collective-permute-start | bytes 172040 | tf_op jit(solution)/shard_map/ppermute | solution.py:1643
  307.7 1.5 fusion.14.refs_6_
  309.2 10.2 %multiply_reduce_fusion = (f32[1024]{0:T(1024)}, f32[512]{0:T(512)S(1)}, f32[512,1024]{1,0:T(8,128)S(1)}) fusion(f32[512]{0:T(512)} %bitcast.68, bf16[2,256,1024]{2,1,0:T(8,128)(2,1)S(1)} %copy-done.1, f32[1024]{0:T(1024)S(1)} %copy-done.15, f32[512,1024]{1,0:T(8,128)S(1)} %fusion.20, bf16[1024,4096]{1,0:T(8,128)(2,1)} %get-tuple-element.91, ...), kind=kOutput, calls=%fused_computation.12 | convolution fusion | flops 4315937280 | bytes 17838080 | tf_op jit(solution)/shard_map/dot_general | solution.py:86
  321.2 2.3 collective-permute-start.9
  324.4 138.6 %reduce_blocks.1 = (bf16[96,128,128]{2,1,0:T(8,128)(2,1)}, f32[296,128]{1,0:T(8,128)}) custom-call(s32[768]{0:T(1024)} %get-tuple-element.114.left_at, s32[768]{0:T(1024)} %get-tuple-element.113.right_at, f32[296,128]{1,0:T(8,128)} %bitcast.61, bf16[512,1024]{1,0:T(8,128)(2,1)} %get-tuple-element.98.refs_0_, ...), custom_call_target="tpu_custom_call" | custom-call | tf_op jit(solution)/shard_map/reduce_blocks/pallas_call | solution.py:750
  463.0 1.9 divide_subtract_fusion
  464.8 20.6 %shampoo.1 = (f32[96,128,128]{2,1,0:T(8,128)}, f32[96,128,128]{2,1,0:T(8,128)}, f32[96,128,128]{2,1,0:T(8,128)}, f32[96,128,128]{2,1,0:T(8,128)}, bf16[96,128,128]{2,1,0:T(8,128)(2,1)}) custom-call(bf16[96,128,128]{2,1,0:T(8,128)(2,1)} %get-tuple-element.104.total, f32[96,128,128]{2,1,0:T(8,128)} %master.3, f32[96,128,128]{2,1,0:T(8,128)} %left.1, ...), custom_call_target="tpu_custom_call" | custom-call | tf_op jit(solution)/shard_map/shampoo/pallas_call | solution.py:1608
  488.9 1.5 maximum_convert_fusion
  (146 shorter events, 35.3 us)
Async XLA Ops:
  3.0 113.4 %copy-start.17 = (s32[768]{0:T(1024)S(1)}, s32[768]{0:T(1024)}, u32[]{:S(2)}) copy-start(s32[768]{0:T(1024)} %param.20) | copy-start | bytes 9220
  3.0 113.4 %copy-start.22 = (s32[768]{0:T(1024)S(1)}, s32[768]{0:T(1024)}, u32[]{:S(2)}) copy-start(s32[768]{0:T(1024)} %constant.150.clone) | copy-start | bytes 9220
  3.0 113.4 %copy-start.23 = (s32[768]{0:T(1024)S(1)}, s32[768]{0:T(1024)}, u32[]{:S(2)}) copy-start(s32[768]{0:T(1024)} %constant.151.clone) | copy-start | bytes 9220
  3.0 113.4 %copy-start.24 = (s32[768]{0:T(1024)S(1)}, s32[768]{0:T(1024)}, u32[]{:S(2)}) copy-start(s32[768]{0:T(1024)} %constant.152.clone) | copy-start | bytes 9220
  118.3 29.1 %copy-start.9 = (f32[37192]{0:T(1024)S(1)}, f32[37192]{0:T(1024)}, u32[]{:S(2)}) copy-start(f32[37192]{0:T(1024)} %param.25) | copy-start | bytes 446308
  118.3 32.8 %slice-start = ((f32[37192]{0:T(1024)}), f32[1536]{0:T(1024)S(1)}, s32[]{:S(2)}) async-start(f32[37192]{0:T(1024)} %param.25), calls=%async_computation | async-start | bytes 16384 | tf_op jit(solution)/shard_map/slice | solution.py:76
  144.2 17.4 %collective-permute-start.2 = (bf16[512,256]{1,0:T(8,128)(2,1)}, bf16[512,256]{1,0:T(8,128)(2,1)S(1)}, u32[]{:S(2)}, u32[]{:S(2)}) collective-permute-start(bf16[512,256]{1,0:T(8,128)(2,1)} %get-tuple-element.73), channel_id=1, source_target_pairs={{0,1},{2,3},{4,5},{6,7},{8,9},{10,11},{12,13},{14,15},{16,17},{18,... | collective-permute-start | bytes 786440 | tf_op jit(solution)/shard_map/ppermute | solution.py:1643
  145.5 6.1 %collective-permute-start = (bf16[8,1792]{1,0:T(8,128)(2,1)}, bf16[8,1792]{1,0:T(8,128)(2,1)S(1)}, u32[]{:S(2)}, u32[]{:S(2)}) collective-permute-start(bf16[8,1792]{1,0:T(8,128)(2,1)} %get-tuple-element.65), channel_id=1, source_target_pairs={{0,1},{2,3},{4,5},{6,7},{8,9},{10,11},{12,13},{14,15},{16,17},{18,... | collective-permute-start | bytes 86024 | tf_op jit(solution)/shard_map/ppermute | solution.py:1643
  160.1 13.4 %collective-permute-start.1 = (bf16[128,1536]{1,0:T(8,128)(2,1)}, bf16[128,1536]{1,0:T(8,128)(2,1)S(1)}, u32[]{:S(2)}, u32[]{:S(2)}) collective-permute-start(bf16[128,1536]{1,0:T(8,128)(2,1)} %get-tuple-element.70), channel_id=1, source_target_pairs={{0,1},{2,3},{4,5},{6,7},{8,9},{10,11},{12,13},{14,15},{16,17},{18,... | collective-permute-start | bytes 1179656 | tf_op jit(solution)/shard_map/ppermute | solution.py:1643
  231.0 32.8 %collective-permute-start.5 = (bf16[128,1536]{1,0:T(8,128)(2,1)S(1)}, bf16[128,1536]{1,0:T(8,128)(2,1)S(1)}, u32[]{:S(2)}, u32[]{:S(2)}) collective-permute-start(bf16[128,1536]{1,0:T(8,128)(2,1)S(1)} %convert_element_type.81), channel_id=1, source_target_pairs={{1,0},{3,2},{5,4},{7,6},{9,8},{11,10},{13,12},{15,14},{17,16},{19,... | collective-permute-start | bytes 1179656 | tf_op jit(solution)/shard_map/ppermute | solution.py:1643
  235.2 21.5 %copy-start.6 = (bf16[512,1024]{1,0:T(8,128)(2,1)S(1)}, bf16[512,1024]{1,0:T(8,128)(2,1)}, u32[]{:S(2)}) copy-start(bf16[512,1024]{1,0:T(8,128)(2,1)} %get-tuple-element.79) | copy-start | bytes 3145732
  254.0 6.8 %collective-permute-start.7 = (bf16[512,256]{1,0:T(8,128)(2,1)S(1)}, bf16[512,256]{1,0:T(8,128)(2,1)S(1)}, u32[]{:S(2)}, u32[]{:S(2)}) collective-permute-start(bf16[512,256]{1,0:T(8,128)(2,1)S(1)} %slice.118), channel_id=1, source_target_pairs={{1,0},{3,2},{5,4},{7,6},{9,8},{11,10},{13,12},{15,14},{17,16},{19,... | collective-permute-start | bytes 786440 | tf_op jit(solution)/shard_map/ppermute | solution.py:1643
  257.9 227.6 %collective-permute-start.3 = (bf16[1,256,1024]{2,1,0:T(8,128)(2,1)}, bf16[1,256,1024]{2,1,0:T(8,128)(2,1)}, u32[]{:S(2)}, u32[]{:S(2)}) collective-permute-start(bf16[1,256,1024]{2,1,0:T(8,128)(2,1)} %get-tuple-element.127), channel_id=1, source_target_pairs={{2,0},{0,1},{3,2},{1,3},{6,4},{4,5},{7,6},{5,7},{10,8},{8,9},{11,1... | collective-permute-start | bytes 1572872 | tf_op jit(solution)/shard_map/ppermute | solution.py:1629
  258.1 227.4 %collective-permute-start.4 = (bf16[1,256,1024]{2,1,0:T(8,128)(2,1)}, bf16[1,256,1024]{2,1,0:T(8,128)(2,1)}, u32[]{:S(2)}, u32[]{:S(2)}) collective-permute-start(bf16[1,256,1024]{2,1,0:T(8,128)(2,1)} %get-tuple-element.126), channel_id=1, source_target_pairs={{0,0},{2,1},{1,2},{3,3},{4,4},{6,5},{5,6},{7,7},{8,8},{10,9},{9,10... | collective-permute-start | bytes 1572872 | tf_op jit(solution)/shard_map/ppermute | solution.py:1629
  294.8 14.4 %copy-start.1 = (bf16[2,256,1024]{2,1,0:T(8,128)(2,1)S(1)}, bf16[2,256,1024]{2,1,0:T(8,128)(2,1)}, u32[]{:S(2)}) copy-start(bf16[2,256,1024]{2,1,0:T(8,128)(2,1)} %get-tuple-element.61) | copy-start | bytes 3145732
  294.8 14.4 %copy-start.15 = (f32[1024]{0:T(1024)S(1)}, f32[1024]{0:T(1024)}, u32[]{:S(2)}) copy-start(f32[1024]{0:T(1024)} %get-tuple-element.129) | copy-start | bytes 12292
  296.3 12.9 %copy-start.5 = (bf16[512,256]{1,0:T(8,128)(2,1)S(1)}, bf16[512,256]{1,0:T(8,128)(2,1)}, u32[]{:S(2)}) copy-start(bf16[512,256]{1,0:T(8,128)(2,1)} %turn_back.1.refs_8_) | copy-start | bytes 786436
  298.2 9.5 %collective-permute-start.6 = (f32[8,1792]{1,0:T(8,128)}, f32[8,1792]{1,0:T(8,128)}, u32[]{:S(2)}, u32[]{:S(2)}) collective-permute-start(f32[8,1792]{1,0:T(8,128)} %slice.116), channel_id=1, source_target_pairs={{1,0},{3,2},{5,4},{7,6},{9,8},{11,10},{13,12},{15,14},{17,16},{19,... | collective-permute-start | bytes 172040 | tf_op jit(solution)/shard_map/ppermute | solution.py:1643
  309.2 10.3 %copy-start.4 = (f32[512,1024]{1,0:T(8,128)S(1)}, f32[512,1024]{1,0:T(8,128)}, u32[]{:S(2)}) copy-start(f32[512,1024]{1,0:T(8,128)} %get-tuple-element.93) | copy-start | bytes 6291460
  309.2 10.3 %copy-start.18 = (f32[1,2,2,128]{3,1,2,0:T(2,128)S(1)}, f32[1,2,2,128]{3,1,2,0:T(2,128)}, u32[]{:S(2)}) copy-start(f32[1,2,2,128]{3,1,2,0:T(2,128)} %copy.49) | copy-start | bytes 6148
  321.2 166.6 %collective-permute-start.8 = (bf16[1,256,1024]{2,1,0:T(8,128)(2,1)}, bf16[1,256,1024]{2,1,0:T(8,128)(2,1)S(1)}, u32[]{:S(2)}, u32[]{:S(2)}) collective-permute-start(bf16[1,256,1024]{2,1,0:T(8,128)(2,1)} %get-tuple-element.123), channel_id=1, source_target_pairs={{2,0},{0,1},{3,2},{1,3},{6,4},{4,5},{7,6},{5,7},{10,8},{8,9},{11,1... | collective-permute-start | bytes 1572872 | tf_op jit(solution)/shard_map/ppermute | solution.py:1629
  321.2 166.6 %collective-permute-start.9 = (bf16[1,256,1024]{2,1,0:T(8,128)(2,1)}, bf16[1,256,1024]{2,1,0:T(8,128)(2,1)}, u32[]{:S(2)}, u32[]{:S(2)}) collective-permute-start(bf16[1,256,1024]{2,1,0:T(8,128)(2,1)} %get-tuple-element.122), channel_id=1, source_target_pairs={{0,0},{2,1},{1,2},{3,3},{4,4},{6,5},{5,6},{7,7},{8,8},{10,9},{9,10... | collective-permute-start | bytes 1572872 | tf_op jit(solution)/shard_map/ppermute | solution.py:1629
  324.4 138.6 %copy-start.10 = (f32[37192]{0:T(1024)S(1)}, f32[37192]{0:T(1024)}, u32[]{:S(2)}) copy-start(f32[37192]{0:T(1024)} %param.25) | copy-start | bytes 446308
  324.4 138.6 %copy-start.12 = (f32[37192]{0:T(1024)S(1)}, f32[37192]{0:T(1024)}, u32[]{:S(2)}) copy-start(f32[37192]{0:T(1024)} %param.26) | copy-start | bytes 446308
  (15 other events, 69.1 us)

commit v6 on v5

--- a/solution.py
+++ b/solution.py
@@ -1341,7 +1341,7 @@
     )(g_kv, cosine, sine)
 
 
-FF_TILE = 512
+FF_TILE = 1024
 
 
 def feed_kernel(rows, scanned, context, given, gain, w_out, w_gate, w_up, w_down,

time: 499 us -> 511 us (1.024)
  Pallas kernels: 417 us -> 428 us
    pallas_call x1, Pallas kernels: 30.5 us -> 42.2 us  [feed(): pl.pallas_call(feed_kernel, out_shape=(jax.ShapeDtypeStruct((tokens, D),...]
  transfers between devices with their start and end apart: 10 -> 10, of which waited for: 0 -> 0; matrix products, arithmetic and copies ran while one was open for 7% -> 7% of each run, Pallas kernels for 46% -> 45%
where the time goes in v6:
time: 511 us; the launch traced here: 501 us
  Pallas kernels  428 us (84%)
  local copies, waits for them, and re-layouts  19.7 us (4%)
  starting transfers between devices  19.2 us (4%)
  other arithmetic  18.7 us (4%)
  matrix products  12.7 us (2%)
    pallas_call x1, Pallas kernels, reduce_blocks(): pl.pallas_call(functools.partial(reduce_kernel, grid, slots, widths), out...  138 us
    pallas_call x1, Pallas kernels, gather_blocks(): pl.pallas_call(functools.partial(gather_kernel, grid, slots), out_shape=(...  109 us
    pallas_call x1, Pallas kernels, feed(): pl.pallas_call(feed_kernel, out_shape=(jax.ShapeDtypeStruct((tokens, D),...  42.2 us
    pallas_call x1, Pallas kernels, mix_back(): pl.pallas_call(mix_back_kernel, out_shape=(jax.ShapeDtypeStruct((tokens,...  30.2 us
    pallas_call x1, Pallas kernels, project(): pl.pallas_call(project_kernel, out_shape=tuple((jax.ShapeDtypeStruct(shap...  26 us
    pallas_call x1, Pallas kernels, shampoo(): pl.pallas_call(functools.partial(shampoo_kernel, norm), out_shape=(full,...  20.6 us
    pallas_call x1, Pallas kernels, attend_back(): pl.pallas_call(attend_back_kernel, out_shape=(jax.ShapeDtypeStruct((token...  17.5 us
    pallas_call x1, Pallas kernels, mix_second(): pl.pallas_call(mix_second_kernel, out_shape=(jax.ShapeDtypeStruct((tokens...  16.8 us
  transfers between devices with their start and end apart: 10, of which 0 were waited for; matrix products, arithmetic and copies ran while one was open for 7% of the time, Pallas kernels for 45%

profile of v6, /device:TPU:11, one launch (start us, length us, event | category | flops | bytes accessed | tf_op | source)
XLA Modules:
  0.0 501.3 jit_solution(11124741016837620920)
XLA Ops:
  3.0 109.1 %gather_blocks.1 = (bf16[8,96,128,128]{3,2,1,0:T(8,128)(2,1)}, bf16[2,256,1024]{2,1,0:T(8,128)(2,1)}, bf16[2,256,1024]{2,1,0:T(8,128)(2,1)}, s32[4,2,256]{2,1,0:T(2,128)}) custom-call(f32[96,128,128]{2,1,0:T(8,128)} %master.3, bf16[2,256,1024]{2,1,0:T(8,128)(2,1)} %tokens.1, bf16[2,256,1024]{2,1,0:T(8,128)(2,1)} %cotangent.1, s32[2,256]{1,0:T(2,128)} %docs.1), custom_call_target="tpu_custom_call" | custom-call | tf_op jit(solution)/shard_map/gather_blocks/pallas_call | solution.py:387
  114.6 1.8 fusion.11
  116.4 1.9 select_reduce_fusion
  118.3 26.0 %project.1 = (bf16[1024,4096]{1,0:T(8,128)(2,1)}, bf16[2048,1024]{1,0:T(8,128)(2,1)}, bf16[1024,4096]{1,0:T(8,128)(2,1)}, bf16[2048,1024]{1,0:T(8,128)(2,1)}, bf...) custom-call(s32[768]{0:T(1024)} %get-tuple-element.115.table, ...), custom_call_target="tpu_custom_call" | custom-call | tf_op jit(solution)/shard_map/project/pallas_call | solution.py:1561
  145.5 1.5 collective-permute-start
  152.1 7.8 %mix_first.1 = (bf16[512,1792]{1,0:T(8,128)(2,1)}, f32[2,512,128]{2,1,0:T(8,128)}, f32[2,128,256]{2,1,0:T(8,128)}, bf16[128,1536]{1,0:T(8,128)(2,1)}, f32[8,128]{1,0:T(8,128)}) custom-call(bf16[512,3328]{1,0:T(8,128)(2,1)} %get-tuple-element.64.proj_x.proj_bc.z, bf16[512,3328]{1,0:T(8,128)(2,1)} %get-tuple-element.64.proj_x.proj_bc.z, ...), custom_call_target="tpu_custom_call" | custom-call | tf_op jit(solution)/shard_map/mix_first/pallas_call | solution.py:848
  162.3 10.9 %attend.1 = (bf16[512,512]{1,0:T(8,128)(2,1)}, f32[4,8,512]{2,1,0:T(8,128)}) custom-call(bf16[512,512]{1,0:T(8,128)(2,1)} %get-tuple-element.72.q, bf16[1024,256]{1,0:T(8,128)(2,1)} %copy-done.3, f32[2,8,768]{2,1,0:T(8,128)} %broadcast_in_dim.99.key_labels, f32[512,128]{1,0:T(8,128)} %pad.20.marks), custom_call_target="tpu_custom_call" | custom-call | tf_op jit(solution)/shard_map/attend/pallas_call | solution.py:1257
  174.8 16.8 %mix_second.1 = (f32[512,1536]{1,0:T(8,128)}, bf16[512,1536]{1,0:T(8,128)(2,1)}, f32[3,128,1536]{2,1,0:T(8,128)}) custom-call(bf16[512,1792]{1,0:T(8,128)(2,1)} %get-tuple-element.67.x.b.c, bf16[512,1792]{1,0:T(8,128)(2,1)} %get-tuple-element.67.x.b.c, bf16[512,1792]{1,0:T(8,128)(2,1)} %get-tuple-element.67.x.b.c, ...), custom_call_target="tpu_custom_call" | custom-call | tf_op jit(solution)/shard_map/mix_second/pallas_call | solution.py:943
  191.6 42.2 %feed.1 = (bf16[512,1024]{1,0:T(8,128)(2,1)}, bf16[512,2048]{1,0:T(8,128)(2,1)}, bf16[512,2048]{1,0:T(8,128)(2,1)}, bf16[512,2048]{1,0:T(8,128)(2,1)}, bf16[512,...) custom-call(bf16[512,1024]{1,0:T(8,128)(2,1)} %bitcast.56, ...), custom_call_target="tpu_custom_call" | custom-call | tf_op jit(solution)/shard_map/feed/pallas_call | solution.py:1403
  233.9 7.4 %gate_back.1 = (bf16[512,1536]{1,0:T(8,128)(2,1)}, bf16[512,1536]{1,0:T(8,128)(2,1)}, f32[1,1536]{1,0:T(1,128)}, f32[128,1536]{1,0:T(8,128)}) custom-call(bf16[512,2048]{1,0:T(8,128)(2,1)} %get-tuple-element.80.grad.given, f32[512,1536]{1,0:T(8,128)} %get-tuple-element.81.y, bf16[512,3328]{1,0:T(8,128)(2,1)} %get-tuple-element.64.proj_x.proj_bc.z, ...), custom_call_target="tpu_custom_call" | custom-call | tf_op jit(solution)/shard_map/gate_back/pallas_call | solution.py:1011
  242.5 3.1 collective-permute-start.5
  246.7 17.5 %attend_back.1 = (bf16[512,512]{1,0:T(8,128)(2,1)}, bf16[1024,256]{1,0:T(8,128)(2,1)}) custom-call(bf16[512,512]{1,0:T(8,128)(2,1)} %get-tuple-element.72.q, bf16[1024,256]{1,0:T(8,128)(2,1)} %copy-done.3, bf16[512,2048]{1,0:T(8,128)(2,1)} %get-tuple-element.80.grad.given, f32[2,768,8]{2,1,0:T(8,128)} %broadcast_in_dim.101.key_marks, ...), custom_call_target="tpu_custom_call" | custom-call | tf_op jit(solution)/shard_map/attend_back/pallas_call | solution.py:1316
  269.4 2.7 collective-permute-start.4
  272.9 2.1 turn_back.1.refs_8_
  276.0 30.2 %mix_back.1 = (bf16[512,1792]{1,0:T(8,128)(2,1)}, f32[16,1792]{1,0:T(8,128)}, f32[8,1792]{1,0:T(8,128)}, bf16[512,128]{1,0:T(8,128)(2,1)}, f32[8,128]{1,0:T(8,128)}) custom-call(bf16[512,1792]{1,0:T(8,128)(2,1)} %get-tuple-element.67.x.b.c, bf16[512,1792]{1,0:T(8,128)(2,1)} %get-tuple-element.67.x.b.c, bf16[512,1792]{1,0:T(8,128)(2,1)} %get-tuple-element.67.x.b.c, ...), custom_call_target="tpu_custom_call" | custom-call | tf_op jit(solution)/shard_map/mix_back/pallas_call | solution.py:1161
  306.3 1.5 fusion.20
  309.7 5.5 %collective-permute-start.6 = (f32[8,1792]{1,0:T(8,128)}, f32[8,1792]{1,0:T(8,128)}, u32[]{:S(2)}, u32[]{:S(2)}) collective-permute-start(f32[8,1792]{1,0:T(8,128)} %slice.116), channel_id=1, source_target_pairs={{1,0},{3,2},{5,4},{7,6},{9,8},{11,10},{13,12},{15,14},{17,16},{19,... | collective-permute-start | bytes 172040 | tf_op jit(solution)/shard_map/ppermute | solution.py:1643
  319.2 1.5 fusion.14.refs_6_
  320.7 10.0 %multiply_reduce_fusion = (f32[1024]{0:T(1024)}, f32[512]{0:T(512)S(1)}, f32[512,1024]{1,0:T(8,128)S(1)}) fusion(f32[512]{0:T(512)} %bitcast.68, bf16[2,256,1024]{2,1,0:T(8,128)(2,1)S(1)} %copy-done.1, f32[1024]{0:T(1024)S(1)} %copy-done.15, f32[512,1024]{1,0:T(8,128)S(1)} %fusion.20, bf16[1024,4096]{1,0:T(8,128)(2,1)} %get-tuple-element.91, ...), kind=kOutput, calls=%fused_computation.12 | convolution fusion | flops 4315937280 | bytes 17838080 | tf_op jit(solution)/shard_map/dot_general | solution.py:86
  332.5 2.3 collective-permute-start.9
  335.6 137.8 %reduce_blocks.1 = (bf16[96,128,128]{2,1,0:T(8,128)(2,1)}, f32[296,128]{1,0:T(8,128)}) custom-call(s32[768]{0:T(1024)} %get-tuple-element.114.left_at, s32[768]{0:T(1024)} %get-tuple-element.113.right_at, f32[296,128]{1,0:T(8,128)} %bitcast.61, bf16[512,1024]{1,0:T(8,128)(2,1)} %get-tuple-element.98.refs_0_, ...), custom_call_target="tpu_custom_call" | custom-call | tf_op jit(solution)/shard_map/reduce_blocks/pallas_call | solution.py:750
  473.4 1.9 divide_subtract_fusion
  475.3 20.6 %shampoo.1 = (f32[96,128,128]{2,1,0:T(8,128)}, f32[96,128,128]{2,1,0:T(8,128)}, f32[96,128,128]{2,1,0:T(8,128)}, f32[96,128,128]{2,1,0:T(8,128)}, bf16[96,128,128]{2,1,0:T(8,128)(2,1)}) custom-call(bf16[96,128,128]{2,1,0:T(8,128)(2,1)} %get-tuple-element.104.total, f32[96,128,128]{2,1,0:T(8,128)} %master.3, f32[96,128,128]{2,1,0:T(8,128)} %left.1, ...), custom_call_target="tpu_custom_call" | custom-call | tf_op jit(solution)/shard_map/shampoo/pallas_call | solution.py:1608
  499.4 1.5 maximum_convert_fusion
  (146 shorter events, 35.3 us)
Async XLA Ops:
  3.0 113.4 %copy-start.17 = (s32[768]{0:T(1024)S(1)}, s32[768]{0:T(1024)}, u32[]{:S(2)}) copy-start(s32[768]{0:T(1024)} %param.20) | copy-start | bytes 9220
  3.0 113.4 %copy-start.22 = (s32[768]{0:T(1024)S(1)}, s32[768]{0:T(1024)}, u32[]{:S(2)}) copy-start(s32[768]{0:T(1024)} %constant.150.clone) | copy-start | bytes 9220
  3.0 113.4 %copy-start.23 = (s32[768]{0:T(1024)S(1)}, s32[768]{0:T(1024)}, u32[]{:S(2)}) copy-start(s32[768]{0:T(1024)} %constant.151.clone) | copy-start | bytes 9220
  3.0 113.4 %copy-start.24 = (s32[768]{0:T(1024)S(1)}, s32[768]{0:T(1024)}, u32[]{:S(2)}) copy-start(s32[768]{0:T(1024)} %constant.152.clone) | copy-start | bytes 9220
  118.3 28.9 %copy-start.9 = (f32[37192]{0:T(1024)S(1)}, f32[37192]{0:T(1024)}, u32[]{:S(2)}) copy-start(f32[37192]{0:T(1024)} %param.25) | copy-start | bytes 446308
  118.3 32.6 %slice-start = ((f32[37192]{0:T(1024)}), f32[1536]{0:T(1024)S(1)}, s32[]{:S(2)}) async-start(f32[37192]{0:T(1024)} %param.25), calls=%async_computation | async-start | bytes 16384 | tf_op jit(solution)/shard_map/slice | solution.py:76
  144.2 17.2 %collective-permute-start.2 = (bf16[512,256]{1,0:T(8,128)(2,1)}, bf16[512,256]{1,0:T(8,128)(2,1)S(1)}, u32[]{:S(2)}, u32[]{:S(2)}) collective-permute-start(bf16[512,256]{1,0:T(8,128)(2,1)} %get-tuple-element.73), channel_id=1, source_target_pairs={{0,1},{2,3},{4,5},{6,7},{8,9},{10,11},{12,13},{14,15},{16,17},{18,... | collective-permute-start | bytes 786440 | tf_op jit(solution)/shard_map/ppermute | solution.py:1643
  145.5 5.9 %collective-permute-start = (bf16[8,1792]{1,0:T(8,128)(2,1)}, bf16[8,1792]{1,0:T(8,128)(2,1)S(1)}, u32[]{:S(2)}, u32[]{:S(2)}) collective-permute-start(bf16[8,1792]{1,0:T(8,128)(2,1)} %get-tuple-element.65), channel_id=1, source_target_pairs={{0,1},{2,3},{4,5},{6,7},{8,9},{10,11},{12,13},{14,15},{16,17},{18,... | collective-permute-start | bytes 86024 | tf_op jit(solution)/shard_map/ppermute | solution.py:1643
  159.8 13.4 %collective-permute-start.1 = (bf16[128,1536]{1,0:T(8,128)(2,1)}, bf16[128,1536]{1,0:T(8,128)(2,1)S(1)}, u32[]{:S(2)}, u32[]{:S(2)}) collective-permute-start(bf16[128,1536]{1,0:T(8,128)(2,1)} %get-tuple-element.70), channel_id=1, source_target_pairs={{0,1},{2,3},{4,5},{6,7},{8,9},{10,11},{12,13},{14,15},{16,17},{18,... | collective-permute-start | bytes 1179656 | tf_op jit(solution)/shard_map/ppermute | solution.py:1643
  242.5 32.6 %collective-permute-start.5 = (bf16[128,1536]{1,0:T(8,128)(2,1)S(1)}, bf16[128,1536]{1,0:T(8,128)(2,1)S(1)}, u32[]{:S(2)}, u32[]{:S(2)}) collective-permute-start(bf16[128,1536]{1,0:T(8,128)(2,1)S(1)} %convert_element_type.81), channel_id=1, source_target_pairs={{1,0},{3,2},{5,4},{7,6},{9,8},{11,10},{13,12},{15,14},{17,16},{19,... | collective-permute-start | bytes 1179656 | tf_op jit(solution)/shard_map/ppermute | solution.py:1643
  246.7 21.3 %copy-start.6 = (bf16[512,1024]{1,0:T(8,128)(2,1)S(1)}, bf16[512,1024]{1,0:T(8,128)(2,1)}, u32[]{:S(2)}) copy-start(bf16[512,1024]{1,0:T(8,128)(2,1)} %get-tuple-element.79) | copy-start | bytes 3145732
  265.2 6.8 %collective-permute-start.7 = (bf16[512,256]{1,0:T(8,128)(2,1)S(1)}, bf16[512,256]{1,0:T(8,128)(2,1)S(1)}, u32[]{:S(2)}, u32[]{:S(2)}) collective-permute-start(bf16[512,256]{1,0:T(8,128)(2,1)S(1)} %slice.118), channel_id=1, source_target_pairs={{1,0},{3,2},{5,4},{7,6},{9,8},{11,10},{13,12},{15,14},{17,16},{19,... | collective-permute-start | bytes 786440 | tf_op jit(solution)/shard_map/ppermute | solution.py:1643
  269.1 226.8 %collective-permute-start.3 = (bf16[1,256,1024]{2,1,0:T(8,128)(2,1)}, bf16[1,256,1024]{2,1,0:T(8,128)(2,1)}, u32[]{:S(2)}, u32[]{:S(2)}) collective-permute-start(bf16[1,256,1024]{2,1,0:T(8,128)(2,1)} %get-tuple-element.127), channel_id=1, source_target_pairs={{2,0},{0,1},{3,2},{1,3},{6,4},{4,5},{7,6},{5,7},{10,8},{8,9},{11,1... | collective-permute-start | bytes 1572872 | tf_op jit(solution)/shard_map/ppermute | solution.py:1629
  269.4 226.5 %collective-permute-start.4 = (bf16[1,256,1024]{2,1,0:T(8,128)(2,1)}, bf16[1,256,1024]{2,1,0:T(8,128)(2,1)}, u32[]{:S(2)}, u32[]{:S(2)}) collective-permute-start(bf16[1,256,1024]{2,1,0:T(8,128)(2,1)} %get-tuple-element.126), channel_id=1, source_target_pairs={{0,0},{2,1},{1,2},{3,3},{4,4},{6,5},{5,6},{7,7},{8,8},{10,9},{9,10... | collective-permute-start | bytes 1572872 | tf_op jit(solution)/shard_map/ppermute | solution.py:1629
  306.2 10.2 %copy-start.16 = (f32[8,1792]{1,0:T(8,128)S(1)}, f32[8,1792]{1,0:T(8,128)}, u32[]{:S(2)}) copy-start(f32[8,1792]{1,0:T(8,128)} %get-tuple-element.96) | copy-start | bytes 172036
  306.2 14.4 %copy-start.1 = (bf16[2,256,1024]{2,1,0:T(8,128)(2,1)S(1)}, bf16[2,256,1024]{2,1,0:T(8,128)(2,1)}, u32[]{:S(2)}) copy-start(bf16[2,256,1024]{2,1,0:T(8,128)(2,1)} %get-tuple-element.61) | copy-start | bytes 3145732
  306.2 14.4 %copy-start.15 = (f32[1024]{0:T(1024)S(1)}, f32[1024]{0:T(1024)}, u32[]{:S(2)}) copy-start(f32[1024]{0:T(1024)} %get-tuple-element.129) | copy-start | bytes 12292
  307.7 12.9 %copy-start.5 = (bf16[512,256]{1,0:T(8,128)(2,1)S(1)}, bf16[512,256]{1,0:T(8,128)(2,1)}, u32[]{:S(2)}) copy-start(bf16[512,256]{1,0:T(8,128)(2,1)} %turn_back.1.refs_8_) | copy-start | bytes 786436
  309.7 9.5 %collective-permute-start.6 = (f32[8,1792]{1,0:T(8,128)}, f32[8,1792]{1,0:T(8,128)}, u32[]{:S(2)}, u32[]{:S(2)}) collective-permute-start(f32[8,1792]{1,0:T(8,128)} %slice.116), channel_id=1, source_target_pairs={{1,0},{3,2},{5,4},{7,6},{9,8},{11,10},{13,12},{15,14},{17,16},{19,... | collective-permute-start | bytes 172040 | tf_op jit(solution)/shard_map/ppermute | solution.py:1643
  320.7 10.0 %copy-start.4 = (f32[512,1024]{1,0:T(8,128)S(1)}, f32[512,1024]{1,0:T(8,128)}, u32[]{:S(2)}) copy-start(f32[512,1024]{1,0:T(8,128)} %get-tuple-element.93) | copy-start | bytes 6291460
  332.5 165.8 %collective-permute-start.8 = (bf16[1,256,1024]{2,1,0:T(8,128)(2,1)}, bf16[1,256,1024]{2,1,0:T(8,128)(2,1)S(1)}, u32[]{:S(2)}, u32[]{:S(2)}) collective-permute-start(bf16[1,256,1024]{2,1,0:T(8,128)(2,1)} %get-tuple-element.123), channel_id=1, source_target_pairs={{2,0},{0,1},{3,2},{1,3},{6,4},{4,5},{7,6},{5,7},{10,8},{8,9},{11,1... | collective-permute-start | bytes 1572872 | tf_op jit(solution)/shard_map/ppermute | solution.py:1629
  332.5 165.8 %collective-permute-start.9 = (bf16[1,256,1024]{2,1,0:T(8,128)(2,1)}, bf16[1,256,1024]{2,1,0:T(8,128)(2,1)}, u32[]{:S(2)}, u32[]{:S(2)}) collective-permute-start(bf16[1,256,1024]{2,1,0:T(8,128)(2,1)} %get-tuple-element.122), channel_id=1, source_target_pairs={{0,0},{2,1},{1,2},{3,3},{4,4},{6,5},{5,6},{7,7},{8,8},{10,9},{9,10... | collective-permute-start | bytes 1572872 | tf_op jit(solution)/shard_map/ppermute | solution.py:1629
  335.6 137.8 %copy-start.10 = (f32[37192]{0:T(1024)S(1)}, f32[37192]{0:T(1024)}, u32[]{:S(2)}) copy-start(f32[37192]{0:T(1024)} %param.25) | copy-start | bytes 446308
  335.6 137.8 %copy-start.12 = (f32[37192]{0:T(1024)S(1)}, f32[37192]{0:T(1024)}, u32[]{:S(2)}) copy-start(f32[37192]{0:T(1024)} %param.26) | copy-start | bytes 446308
  (15 other events, 68.9 us)
